TPU v7x, 1024 devices: a whole 4x4x32 slice. The times are simulated.
1024 devices in a mesh: dp: 8 (over z_hi, core), ctx: 128 (over x, y, z_lo).
Axes of the slice: x: 4, y: 4, z: 32 (z_hi: 4, z_lo: 8; z = z_hi * 8 + z_lo), core: 2. Of those that a mesh axis runs over, the one named last changes fastest.
Arguments:
- activations: bfloat16 [10240, 4096], P('ctx', 'dp'), may hold values from -6 to 6
- queries: bfloat16 [10240, 32, 128], P('ctx', 'dp'), may hold values from -300 to 300
- w_kv: bfloat16 [4096, 8, 2, 128], P(('dp', 'ctx')), may hold values from -0.09375 to 0.09375
- span_of: int32 [256], P('ctx'), may hold values from 0 to 255, as said below
Outputs:
- attended: bfloat16 [10240, 4096], P('ctx', 'dp')
Inputs may be any that keep to these rules, and one draw needn't show every extreme that they name: `span_of`: each span number appears once. The two slots of one ctx index hold spans c and 2 * 128 - 1 - c for some c, in either order.
All inputs are finite; a program needn't handle non-finite values.
Results may differ from a plain program's by a relative error of at most 0.0066.
Values may be sent and summed in bfloat16 or wider, within the bound.
No kernel may reach another device: no remote copies, remote signals or barrier semaphores. Data moves between devices by JAX's collectives and lax.ppermute only.
A program may use at most 32 MiB of HBM per device.

v0:
```python
import math

import jax
import jax.numpy as jnp
from jax import lax
from jax.sharding import Mesh
from jax.sharding import PartitionSpec as P

CTX = ("ctx_0", "ctx_1", "ctx_2")
DP_CTX = ("dp", "ctx_0", "ctx_1", "ctx_2")


def cut_along(shard, dim, peers):
    before, after = (shard.shape[:dim], shard.shape[dim + 1 :])
    return jnp.moveaxis(shard.reshape(*before, peers, -1, *after), dim, 0)


def sum_at_owner(shard, axis, dim):
    peers = lax.axis_size(axis)
    blocks = lax.all_to_all(cut_along(shard, dim, peers), axis, 0, 0, tiled=True)
    return jnp.sum(blocks, axis=0)


def joined_along(blocks, dim):
    blocks = jnp.moveaxis(blocks, 0, dim)
    lengths = blocks.shape
    return blocks.reshape(*lengths[:dim], lengths[dim] * lengths[dim + 1], *lengths[dim + 2 :])


def all_blocks(shard, axes, turns):
    blocks = shard[None]
    for k in turns:
        blocks = lax.all_gather(blocks, axes[k], axis=0, tiled=True)
    current = [lax.axis_size(axes[k]) for k in reversed(turns)]
    blocks = blocks.reshape(*current, *shard.shape)
    turned = sorted(range(len(turns)), key=lambda place: turns[len(turns) - 1 - place])
    return blocks.transpose(*turned, *range(len(turns), blocks.ndim)).reshape(-1, *shard.shape)


def whole_of(shard, axes, turns, dim):
    return joined_along(all_blocks(shard, axes, turns), dim)


def attend(carry, keys, values, key_pos, query, query_pos, scale):
    top, total, accum = carry
    score = jnp.einsum("tgd,nd->tgn", query, keys, preferred_element_type=jnp.float32) * scale
    visible = (key_pos[None, :] <= query_pos[:, None])[:, None, :]
    new_top = jnp.maximum(top, jnp.max(jnp.where(visible, score, -1e30), axis=2))
    weight = jnp.where(visible, jnp.exp(score - new_top[..., None]), 0.0)
    factor = jnp.exp(top - new_top)
    total = total * factor + jnp.sum(weight, axis=2)
    accum = accum * factor[..., None] + jnp.einsum(
        "tgn,nd->tgd", weight.astype(jnp.bfloat16), values, preferred_element_type=jnp.float32
    )
    return (new_top, total, accum)


def body(activations, queries, w_kv, span_of):
    tokens = activations.shape[0]
    head_dim = queries.shape[2]
    half = tokens // 2
    scale = 1.0 / math.sqrt(head_dim)
    piece = lax.all_gather(w_kv, CTX, axis=0, tiled=True)
    count = piece.shape[0]
    partial_kv = jnp.dot(activations, piece.reshape(count, -1), preferred_element_type=jnp.float32)
    projected = sum_at_owner(partial_kv, "dp", 1)
    key_value = projected.astype(jnp.bfloat16).reshape(tokens, 2, head_dim)
    all_spans = lax.all_gather(span_of, CTX, axis=0, tiled=True)
    offsets = jnp.arange(tokens, dtype=jnp.int32)
    own_pos = jnp.where(offsets < half, span_of[0], span_of[1]) * half + offsets % half

    def update(state, part, part_pos):
        return attend(state, part[:, 0], part[:, 1], part_pos, queries, own_pos, scale)

    group = queries.shape[1]
    start_state = (
        jnp.full((tokens, group), -1e30, jnp.float32),
        jnp.zeros((tokens, group), jnp.float32),
        jnp.zeros((tokens, group, head_dim), jnp.float32),
    )
    state = start_state
    piece = whole_of(key_value, CTX, (2, 0, 1), 0)
    count = piece.shape[0]
    index = jnp.arange(count, dtype=jnp.int32)
    key_pos = jnp.take(all_spans, index // half) * half + index % half
    block = 1024

    def step(held, item):
        return (update(held, item[0], item[1]), None)

    blocks = (
        piece.reshape(count // block, block, 2, head_dim),
        key_pos.reshape(count // block, block),
    )
    state, _ = lax.scan(step, state, blocks)
    top, total, accum = state
    return (accum / total[..., None]).astype(jnp.bfloat16).reshape(tokens, group * head_dim)


def solution(mesh):
    finer = Mesh(mesh.devices.reshape(mesh.shape["dp"], 4, 4, 8), ("dp", "ctx_0", "ctx_1", "ctx_2"))
    in_specs = (P(CTX, "dp"), P(CTX, "dp", None), P(DP_CTX, None, None, None), P(CTX))
    out_specs = P(CTX, "dp")
    return jax.shard_map(body, mesh=finer, in_specs=in_specs, out_specs=out_specs, check_vma=False)
```

profile of v0, /device:TPU:32, one launch (start us, length us, event | category | flops | bytes accessed | tf_op | source)
XLA Modules:
  0.0 1286.4 jit_solution(15322165021275656815)
XLA Ops:
  6.5 1.4 copy.29
  8.0 978.5 %all-gather.4.cloned.1.call-done = bf16[512,8,2,128]{3,1,2,0:T(8,128)(2,1)} async-done(((bf16[4,8,2,128]{3,1,2,0:T(8,128)(2,1)}), bf16[512,8,2,128]{3,1,2,0:T(8,128)(2,1)}) %all-gather.4.cloned.1.call-update) | async-done | bytes 2097168 | tf_op jit(solution)/shard_map/all_gather | solution.py:63
  986.5 3.0 copy.30
  989.5 0.7 convolution_bitcast_fusion
  990.2 74.5 %all_to_all.5 = f32[8,80,256]{2,1,0:T(8,128)S(1)} all-to-all(f32[8,80,256]{2,1,0:T(8,128)S(1)} %convolution_bitcast_fusion), channel_id=1, replica_groups=mesh['dp'=8,'ctx_0'=4,'ctx_1'=4,'ctx_2'=8] {'dp'}, dimensions={0} | all-to-all | bytes 1310720 | tf_op jit(solution)/shard_map/all_to_all | solution.py:20
  1064.8 43.3 %all_gather.17 = bf16[8,80,2,128]{3,1,2,0:T(8,128)(2,1)} all-gather(bf16[1,80,2,128]{3,1,2,0:T(8,128)(2,1)S(1)} %copy.31), channel_id=1, replica_groups=mesh['dp'=8,'ctx_0'=4,'ctx_1'=4,'ctx_2'=8] {'ctx_2'}, dimensions={0}, use_global_device_ids=true | all-gather | bytes 368640 | tf_op jit(solution)/shard_map/all_gather | solution.py:33
  1108.2 30.3 %all-gather.6.cloned.1.call-done = bf16[32,80,2,128]{3,1,2,0:T(8,128)(2,1)} async-done(((bf16[8,80,2,128]{3,1,2,0:T(8,128)(2,1)}), bf16[32,80,2,128]{3,1,2,0:T(8,128)(2,1)}) %all-gather.6.cloned.1.call-update) | async-done | bytes 1310736 | tf_op jit(solution)/shard_map/all_gather | solution.py:33
  1138.5 1.3 dynamic-slice
  1140.7 29.8 %all-reduce = s32[256]{0:T(256)S(1)} all-reduce(s32[256]{0:T(256)S(1)} %dynamic-update-slice), channel_id=1, replica_groups=mesh['dp'=8,'ctx_0'=4,'ctx_1'=4,'ctx_2'=8] {'ctx_0','ctx_1','ctx_2'}, use_global_device_ids=true, to_apply=%add | all-reduce | flops 256 | bytes 2048
  1170.6 63.6 %gather_fusion = s32[10240]{0:T(1024)S(1)} fusion(s32[256]{0:T(256)S(1)} %all-reduce, s32[10240]{0:T(1024)S(1)} %broadcast_clamp_fusion), kind=kCustom, calls=%fused_computation | custom fusion | bytes 122880 | tf_op jit(solution)/shard_map/jit(_take)/gather | solution.py:85
  1234.3 0.6 fusion.21
  1235.0 6.3 copy.32
  1241.2 37.9 %while.15 = (s32[]{:T(128)}, f32[80,4]{0,1:T(4,128)S(1)}, f32[80,4]{0,1:T(4,128)S(1)}, f32[80,4,128]{2,0,1:T(8,128)S(1)}, s32[10,1024]{1,0:T(8,128)S(1)}, /*inde...) while((s32[]{:T(128)}, f32[80,4]{0,1:T(4,128)S(1)}, ...), condition=%wide.region_4.5_spmd.clone, body=%wide.region_1.4_spmd.clone.sunk | while | flops 170928480 | bytes 6277385 | solution.py:95
  1241.3 1.2 fusion.32
  1242.6 1.1 dynamic-slice_bitcast_fusion.2
  1243.7 0.5 select_reduce_fusion.2
  1244.1 0.4 fusion.33
  1244.6 0.4 convolution_add_fusion.2
  1245.0 1.2 fusion.32
  1246.4 1.1 dynamic-slice_bitcast_fusion.2
  1247.4 0.5 select_reduce_fusion.2
  1247.9 0.4 fusion.33
  1248.4 0.4 convolution_add_fusion.2
  1248.8 1.2 fusion.32
  1250.1 1.1 dynamic-slice_bitcast_fusion.2
  1251.2 0.5 select_reduce_fusion.2
  1251.7 0.4 fusion.33
  1252.2 0.4 convolution_add_fusion.2
  1252.6 1.2 fusion.32
  1253.9 1.1 dynamic-slice_bitcast_fusion.2
  1255.0 0.5 select_reduce_fusion.2
  1255.5 0.4 fusion.33
  1255.9 0.4 convolution_add_fusion.2
  1256.4 1.2 fusion.32
  1257.7 1.1 dynamic-slice_bitcast_fusion.2
  1258.8 0.5 select_reduce_fusion.2
  1259.3 0.4 fusion.33
  1259.7 0.4 convolution_add_fusion.2
  1260.2 1.2 fusion.32
  1261.5 1.1 dynamic-slice_bitcast_fusion.2
  1262.6 0.5 select_reduce_fusion.2
  1263.1 0.4 fusion.33
  1263.5 0.4 convolution_add_fusion.2
  1264.0 1.2 fusion.32
  1265.3 1.1 dynamic-slice_bitcast_fusion.2
  1266.4 0.5 select_reduce_fusion.2
  1266.9 0.4 fusion.33
  1267.3 0.4 convolution_add_fusion.2
  1267.8 1.2 fusion.32
  1269.1 1.1 dynamic-slice_bitcast_fusion.2
  1270.2 0.5 select_reduce_fusion.2
  1270.7 0.4 fusion.33
  1271.1 0.4 convolution_add_fusion.2
  1271.6 1.2 fusion.32
  1272.9 1.1 dynamic-slice_bitcast_fusion.2
  1274.0 0.5 select_reduce_fusion.2
  1274.4 0.4 fusion.33
  1274.9 0.4 convolution_add_fusion.2
  1275.4 1.2 fusion.32
  1276.7 1.1 dynamic-slice_bitcast_fusion.2
  1277.8 0.5 select_reduce_fusion.2
  1278.2 0.4 fusion.33
  1278.7 0.4 convolution_add_fusion.2
  1279.1 0.8 copy_bitcast_fusion
  (76 shorter events, 2.2 us)
Async XLA Ops:
  6.5 983.0 %copy-start = (bf16[80,512]{1,0:T(8,128)(2,1)S(1)}, bf16[80,512]{1,0:T(8,128)(2,1)}, u32[]{:S(2)}) copy-start(bf16[80,512]{1,0:T(8,128)(2,1)} %param.6) | copy-start | bytes 245764
  6.5 979.9 %all-gather.4.cloned.1.call-start = ((), (), s32[]{:S(2)}) async-start(), calls=%async_computation.1 | async-start | bytes 2113536 | tf_op jit(solution)/shard_map/all_gather | solution.py:63
  7.9 1130.5 %all-gather.6.cloned.1.call-start = ((), (), s32[]{:S(2)}) async-start(), calls=%async_computation.2 | async-start | bytes 1638400 | tf_op jit(solution)/shard_map/all_gather | solution.py:33
  1064.7 75.8 %copy-start.2 = (s32[2]{0:T(128)S(1)}, s32[2]{0:T(128)}, u32[]{:S(2)}) copy-start(s32[2]{0:T(128)} %param.9) | copy-start | bytes 28
  1108.1 126.8 %all-gather.8.cloned.1.call-start = ((), (), s32[]{:S(2)}) async-start(), calls=%async_computation.3 | async-start | bytes 6553600 | tf_op jit(solution)/shard_map/all_gather | solution.py:33
  1170.6 63.6 %copy-start.1 = (bf16[80,4,128]{2,1,0:T(4,128)(2,1)S(1)}, bf16[80,4,128]{2,1,0:T(4,128)(2,1)}, u32[]{:S(2)}) copy-start(bf16[80,4,128]{2,1,0:T(4,128)(2,1)} %param.7) | copy-start | bytes 245764
Sparse Core Ops, SparseCore 0:
  10.0 976.4 all-gather.3
  1108.2 30.1 all-gather.5
  1141.1 75.6 all-gather.7
where the time goes:
time: 1290 us
  waiting for transfers between devices  1010 us (78%)
  blocking collectives  148 us (11%)
  local copies, waits for them, and re-layouts  87.4 us (7%)
  other arithmetic  18.5 us (1%)
  between operations  13.9 us (1%)
    all_gather x1, waiting for transfers between devices, body(): piece = lax.all_gather(w_kv, CTX, axis=0, tiled=True)  979 us
    all_to_all x1, blocking collectives, sum_at_owner(): lax.all_to_all(cut_along(shard, dim, peers), axis, 0, 0, tiled=True)  74.5 us
    gather x2, local copies, waits for them, and re-layouts, body(): key_pos = jnp.take(all_spans, index // half) * half + index % half  63.6 us
    all_gather x1, blocking collectives, all_blocks(): blocks = lax.all_gather(blocks, axes[k], axis=0, tiled=True)  43.3 us
    all_gather x2, waiting for transfers between devices, all_blocks(): blocks = lax.all_gather(blocks, axes[k], axis=0, tiled=True)  30.3 us
    unnamed x1, blocking collectives  29.8 us
  transfers between devices with their start and end apart: 3, of which 2 were waited for; matrix products, arithmetic and copies ran while one was open for 5% of the time, Pallas kernels for 0%

commit v1 on v0

v1 whole, which is shorter than its diff:
```python
import math

import jax
import jax.numpy as jnp
from jax import lax
from jax.experimental import pallas as pl
from jax.experimental.pallas import tpu as pltpu
from jax.sharding import Mesh
from jax.sharding import PartitionSpec as P


ROWS = ("x", "y", "zl")
HEADS = ("zh", "core")
PLANE = ("x", "y")
HIDDEN = -1e30
FLOOR = -1e29
STAT_ROWS = 16
SPAN_ROWS = 8


def shifted(value, axis, by):
    size = lax.axis_size(axis)
    return lax.ppermute(value, axis, [(i, (i + by) % size) for i in range(size)])


def exchanged(blocks, axes):
    return lax.all_to_all(blocks, axes, 0, 0, tiled=True)


def copies(value, count):
    return jnp.broadcast_to(value[None], (count, *value.shape))


def span_rows(first, second, shape):
    lane = lax.broadcasted_iota(jnp.int32, shape, 1)
    row = jnp.where(lane == 0, first, jnp.where(lane == 1, second, 0))
    return row.astype(jnp.float32).astype(jnp.bfloat16)


def project_kernel(zh_ref, span_ref, act_ref, w_ref, out_ref):
    zh = zh_ref[0]
    places, tokens = act_ref.shape[1:3]
    total = None
    for place in range(places):
        source = lax.rem(zh + place, places)
        for core in range(2):
            act = act_ref[core, place]
            w = w_ref[:, source * 2 + core]
            part = jnp.dot(act, w.reshape(-1, w.shape[-1]), preferred_element_type=jnp.float32)
            total = part if total is None else total + part
    rounded = total.astype(out_ref.dtype)
    spans = span_rows(span_ref[0], span_ref[1], (SPAN_ROWS, total.shape[1]))
    for peer in range(out_ref.shape[0]):
        out_ref[peer, :tokens, :] = rounded
        out_ref[peer, tokens:, :] = spans


def attend_kernel(q_ref, kv_ref, out_ref, stat_ref, pos_ref, *, scale):
    blocks, _, width = q_ref.shape
    chunks, peers = kv_ref.shape[:2]
    tokens = kv_ref.shape[2] - SPAN_ROWS
    rows = q_ref.shape[1] - SPAN_ROWS
    half = tokens // 2
    count = peers * tokens
    factor = scale * math.log2(math.e)

    lane = lax.broadcasted_iota(jnp.int32, (peers, count), 1)
    start = lax.broadcasted_iota(jnp.int32, (peers, count), 0) * tokens
    inside = lane - start
    early = (inside >= 0) & (inside < half)
    late = (inside >= half) & (inside < tokens)
    for chunk in range(chunks):
        held = kv_ref[chunk, :, tokens:, :128].astype(jnp.float32)
        spans = jnp.max(held, axis=1) * half
        place = jnp.where(early, spans[:, 0:1], jnp.where(late, spans[:, 1:2] - half, 0.0))
        place = place + jnp.where(early | late, inside.astype(jnp.float32), 0.0)
        pos_ref[chunk : chunk + 1, :] = jnp.sum(place, axis=0, keepdims=True)

    row = lax.broadcasted_iota(jnp.int32, (tokens, 1), 0).astype(jnp.float32)
    column = lax.broadcasted_iota(jnp.int32, (rows, 128), 1)
    stat_ref[...] = jnp.zeros(stat_ref.shape, jnp.float32)

    def step(block, carry):
        spans = q_ref[block, rows : rows + SPAN_ROWS, :].astype(jnp.float32) * half
        query_pos = jnp.where(row < half, spans[0:1, 0:1], spans[0:1, 1:2] - half) + row
        query_pos = jnp.concatenate([query_pos] * (rows // tokens), axis=0)
        query = q_ref[block, :rows, :]
        scores = []
        top = jnp.full((rows, 1), FLOOR, jnp.float32)
        for chunk in range(chunks):
            keys = kv_ref[chunk, :, :tokens, :width].reshape(count, width)
            score = lax.dot_general(
                query, keys, (((1,), (1,)), ((), ())), preferred_element_type=jnp.float32
            )
            score = jnp.where(pos_ref[chunk : chunk + 1, :] <= query_pos, score, HIDDEN)
            top = jnp.maximum(top, jnp.max(score, axis=1, keepdims=True))
            scores.append(score)
        total = jnp.zeros((rows, 1), jnp.float32)
        mixed = jnp.zeros((rows, width), jnp.float32)
        for chunk in range(chunks):
            values = kv_ref[chunk, :, :tokens, width:].reshape(count, width)
            weight = jnp.exp2((scores[chunk] - top) * factor)
            total = total + jnp.sum(weight, axis=1, keepdims=True)
            mixed = mixed + jnp.dot(
                weight.astype(jnp.bfloat16), values, preferred_element_type=jnp.float32
            )
        seen = total > 0.0
        safe = jnp.where(seen, total, 1.0)
        out_ref[block, :rows, :] = (mixed / safe).astype(jnp.bfloat16)
        size = jnp.where(seen, top * factor + jnp.log2(safe), HIDDEN)
        stat_ref[:rows, :] = jnp.where(column == block, size, stat_ref[:rows, :])
        return carry

    lax.fori_loop(0, blocks, step, 0)
    parts = []
    for chunk in range(stat_ref.shape[0] // 128):
        rest = stat_ref[chunk * 128 : (chunk + 1) * 128, :].T[:8]
        for third in range(3):
            high = rest.astype(jnp.bfloat16).astype(jnp.float32)
            parts.append((third * 4 + chunk, high))
            rest = rest - high
    place = lax.broadcasted_iota(jnp.int32, (STAT_ROWS, 128), 0)
    for block in range(blocks):
        tile = jnp.zeros((STAT_ROWS, 128), jnp.float32)
        for where, part in parts:
            tile = jnp.where(place == where, part[block : block + 1], tile)
        out_ref[block, rows:, :] = tile.astype(jnp.bfloat16)


def combine_kernel(in_ref, out_ref, total_ref, *, rows):
    blocks, _, width = in_ref.shape
    tokens = out_ref.shape[0]
    sizes = []
    for block in range(blocks):
        tile = in_ref[block, rows:, :].astype(jnp.float32)
        first = tile[:8]
        sizes.append(first + pltpu.roll(first, 4, 0) + tile[8:])
    top = sizes[0]
    for size in sizes[1:]:
        top = jnp.maximum(top, size)
    shares = [jnp.exp2(size - top) for size in sizes]
    whole = shares[0]
    for share in shares[1:]:
        whole = whole + share
    turned = jnp.concatenate([share / whole for share in shares], axis=0).T
    for start in range(0, rows, 128):
        count = min(128, rows - start)
        held = jnp.zeros((count, width), jnp.float32)
        for block in range(blocks):
            place = block * 8 + start // 128
            mixed = in_ref[block, start : start + count, :].astype(jnp.float32)
            held = held + turned[:count, place : place + 1] * mixed
        total_ref[start : start + count, :] = held
    for head in range(rows // tokens):
        kept = total_ref[head * tokens : (head + 1) * tokens, :]
        out_ref[:, head * width : (head + 1) * width] = kept.astype(out_ref.dtype)


VMEM = pl.BlockSpec(memory_space=pltpu.VMEM)
SMEM = pl.BlockSpec(memory_space=pltpu.SMEM)


def body(activations, queries, w_kv, span_of):
    tokens, features = activations.shape
    group, width = queries.shape[1:]
    rows = tokens * group
    ranks = lax.axis_size(HEADS)
    line = lax.axis_size("zl")
    plane = lax.axis_size(PLANE)
    side = lax.axis_size("y")
    zh = lax.axis_index("zh").astype(jnp.int32).reshape(1)

    left = shifted(activations, "zh", 1)
    right = shifted(activations, "zh", -1)
    cut = features // 2
    far_a = shifted(left[:, :cut], "zh", 1)
    far_b = shifted(right[:, cut:], "zh", -1)
    far = jnp.concatenate([far_a, far_b], axis=1)
    near = jnp.stack([activations, right, far, left])
    acts = lax.all_gather(near, "core")

    piece = w_kv.shape[0]
    w = w_kv.reshape(piece, ranks, 2 * width).transpose(1, 0, 2)
    w = exchanged(w, HEADS)
    w = exchanged(copies(w, line), "zl")
    w = w.transpose(1, 0, 2, 3).reshape(ranks, line * piece, 2 * width)
    w = exchanged(copies(w, plane), PLANE)

    spans = jnp.pad(span_of.astype(jnp.bfloat16)[None], ((0, SPAN_ROWS - 1), (0, width - 2)))
    q = queries.transpose(1, 0, 2).reshape(rows, width)
    q = exchanged(copies(jnp.concatenate([q, spans]), side), "y")

    kv = pl.pallas_call(
        project_kernel,
        out_shape=jax.ShapeDtypeStruct((line, tokens + SPAN_ROWS, 2 * width), jnp.bfloat16),
        in_specs=[SMEM, SMEM, VMEM, VMEM],
        out_specs=VMEM,
        name="project",
    )(zh, span_of, acts, w)
    kv = exchanged(kv, "zl")
    kv = exchanged(copies(kv, side), "x")

    padded = (rows + 127) // 128 * 128
    mixed = pl.pallas_call(
        lambda *refs: attend_kernel(*refs, scale=1.0 / math.sqrt(width)),
        out_shape=jax.ShapeDtypeStruct((side, rows + STAT_ROWS, width), jnp.bfloat16),
        in_specs=[VMEM, VMEM],
        out_specs=VMEM,
        scratch_shapes=[
            pltpu.VMEM((padded, 128), jnp.float32),
            pltpu.VMEM((8, line * tokens), jnp.float32),
        ],
        name="attend",
    )(q, kv)
    mixed = exchanged(mixed, "y")
    return pl.pallas_call(
        lambda *refs: combine_kernel(*refs, rows=rows),
        out_shape=jax.ShapeDtypeStruct((tokens, group * width), jnp.bfloat16),
        in_specs=[VMEM],
        out_specs=VMEM,
        scratch_shapes=[pltpu.VMEM((rows, width), jnp.float32)],
        name="combine",
    )(mixed)


def solution(mesh):
    finer = Mesh(mesh.devices.reshape(4, 2, 4, 4, 8), ("zh", "core", "x", "y", "zl"))
    in_specs = (P(ROWS, HEADS), P(ROWS, HEADS, None), P(HEADS + ROWS, None, None, None), P(ROWS))
    return jax.shard_map(body, mesh=finer, in_specs=in_specs, out_specs=P(ROWS, HEADS), check_vma=False)
```

time: 1290 us -> 202 us (0.16)
  waiting for transfers between devices: 1010 us -> 7.88 us
  local copies, waits for them, and re-layouts: 87.4 us -> 3.38 us
  starting transfers between devices: 0.09 us -> 44 us
  other arithmetic: 18.5 us -> 0.06 us
  blocking collectives: 148 us -> 131 us
  Pallas kernels: 0 us -> 13.8 us
  between operations: 13.9 us -> 0.15 us
    all_gather x3 -> x0, waiting for transfers between devices: 1010 us -> none  [the longest x1 979 us: body(): piece = lax.all_gather(w_kv, CTX, axis=0, tiled=True)]
    gather x2 -> x0, local copies, waits for them, and re-layouts: 63.6 us -> none  [body(): key_pos = jnp.take(all_spans, index // half) * half + index % half]
    all_to_all x1 -> x5, blocking collectives: 74.5 us -> 129 us  [exchanged(): return lax.all_to_all(blocks, axes, 0, 0, tiled=True)]
    all_gather x1, blocking collectives: 43.3 us -> 2.41 us  [body(): acts = lax.all_gather(near, 'core')]
    ppermute x0 -> x4, starting transfers between devices: none -> 32.5 us  [shifted(): lax.ppermute(value, axis, [(i, (i + by) % size) for i in range(size)])]
    unnamed x1 -> x0, blocking collectives: 29.8 us -> none
    pallas_call x0 -> x3, Pallas kernels: none -> 13.8 us  [the longest x1 8.7 us: body(): pl.pallas_call(lambda *refs: attend_kernel(*refs, scale=1.0 / math.sqrt(w...]
  transfers between devices with their start and end apart: 3 -> 6, of which waited for: 2 -> 4; matrix products, arithmetic and copies ran while one was open for 5% -> 0% of each run, Pallas kernels for 0% -> 2%
where the time goes in v1:
time: 202 us; the launch traced here: 201 us
  blocking collectives  131 us (65%)
  starting transfers between devices  44 us (22%)
  Pallas kernels  13.8 us (7%)
  waiting for transfers between devices  7.88 us (4%)
  local copies, waits for them, and re-layouts  3.38 us (2%)
    all_to_all x5, blocking collectives, exchanged(): return lax.all_to_all(blocks, axes, 0, 0, tiled=True)  129 us
    ppermute x4, starting transfers between devices, shifted(): lax.ppermute(value, axis, [(i, (i + by) % size) for i in range(size)])  32.5 us
    all_to_all x2, starting transfers between devices, exchanged(): return lax.all_to_all(blocks, axes, 0, 0, tiled=True)  11.5 us
    pallas_call x1, Pallas kernels, body(): pl.pallas_call(lambda *refs: attend_kernel(*refs, scale=1.0 / math.sqrt(w...  8.7 us
    ppermute x4, waiting for transfers between devices, shifted(): lax.ppermute(value, axis, [(i, (i + by) % size) for i in range(size)])  6.31 us
  transfers between devices with their start and end apart: 6, of which 4 were waited for; matrix products, arithmetic and copies ran while one was open for 0% of the time, Pallas kernels for 2%

profile of v1, /device:TPU:32, one launch (start us, length us, event | category | flops | bytes accessed | tf_op | source)
XLA Modules:
  0.0 200.7 jit_solution(13010322574380312260)
XLA Ops:
  0.0 0.7 reshape.17
  0.8 49.5 %all_to_all.35 = bf16[8,4,256]{2,1,0:T(4,128)(2,1)S(1)} all-to-all(bf16[8,4,256]{2,1,0:T(4,128)(2,1)S(1)} %bitcast.24), channel_id=1, replica_groups=mesh['zh'=4,'core'=2,'x'=4,'y'=4,'zl'=8] {'zh','core'}, dimensions={0} | all-to-all | bytes 32768 | tf_op jit(solution)/shard_map/all_to_all | solution.py:27
  50.3 17.0 %all_to_all.36 = bf16[8,8,4,256]{3,2,1,0:T(4,128)(2,1)S(1)} all-to-all(bf16[8,8,4,256]{3,2,1,0:T(4,128)(2,1)S(1)} %broadcast_in_dim.14), channel_id=1, replica_groups=mesh['zh'=4,'core'=2,'x'=4,'y'=4,'zl'=8] {'zl'}, dimensions={0} | all-to-all | bytes 262144 | tf_op jit(solution)/shard_map/all_to_all | solution.py:27
  67.3 1.6 broadcast_in_dim.32
  68.9 0.0 copy-start.2
  68.9 0.0 copy-start.4
  68.9 0.0 copy-start.3
  68.9 7.2 %all-to-all-start.3 = ((bf16[16,8,32,256]{3,2,1,0:T(8,128)(2,1)}), bf16[16,8,32,256]{3,2,1,0:T(8,128)(2,1)S(1)}, u32[]{:S(2)}, u32[]{:S(2)}) async-start(bf16[16,8,32,256]{3,2,1,0:T(8,128)(2,1)} %broadcast_in_dim.32), calls=%async_computation.3 | async-start | bytes 4194304 | tf_op jit(solution)/shard_map/all_to_all | solution.py:27
  76.0 0.0 copy-done.2
  76.0 2.7 %collective-permute-start.1 = (bf16[80,512]{1,0:T(8,128)(2,1)S(1)}, bf16[80,512]{1,0:T(8,128)(2,1)S(1)}, u32[]{:S(2)}, u32[]{:S(2)}) collective-permute-start(bf16[80,512]{1,0:T(8,128)(2,1)S(1)} %copy-done.2), channel_id=1, source_target_pairs={{0,256},{256,512},{512,768},{768,0},{1,257},{257,513},{513,769},{7... | collective-permute-start | bytes 245768 | tf_op jit(solution)/shard_map/ppermute | solution.py:23
  78.7 11.9 %collective-permute-start = (bf16[80,512]{1,0:T(8,128)(2,1)S(1)}, bf16[80,512]{1,0:T(8,128)(2,1)S(1)}, u32[]{:S(2)}, u32[]{:S(2)}) collective-permute-start(bf16[80,512]{1,0:T(8,128)(2,1)S(1)} %copy-done.2), channel_id=1, source_target_pairs={{0,768},{256,0},{512,256},{768,512},{1,769},{257,1},{513,257},{769... | collective-permute-start | bytes 245768 | tf_op jit(solution)/shard_map/ppermute | solution.py:23
  90.6 0.0 copy-done.4
  90.6 0.0 copy-done.3
  90.7 1.6 collective-permute-done.1
  92.2 6.1 %collective-permute-start.2 = (bf16[80,256]{1,0:T(8,128)(2,1)S(1)}, bf16[80,256]{1,0:T(8,128)(2,1)S(1)}, u32[]{:S(2)}, u32[]{:S(2)}) collective-permute-start(bf16[80,256]{1,0:T(8,128)(2,1)S(1)} %slice.8), channel_id=1, source_target_pairs={{0,256},{256,512},{512,768},{768,0},{1,257},{257,513},{513,769},{7... | collective-permute-start | bytes 122888 | tf_op jit(solution)/shard_map/ppermute | solution.py:23
  98.4 1.8 collective-permute-done
  100.2 11.8 %collective-permute-start.3 = (bf16[80,256]{1,0:T(8,128)(2,1)S(1)}, bf16[80,256]{1,0:T(8,128)(2,1)S(1)}, u32[]{:S(2)}, u32[]{:S(2)}) collective-permute-start(bf16[80,256]{1,0:T(8,128)(2,1)S(1)} %slice.9), channel_id=1, source_target_pairs={{0,768},{256,0},{512,256},{768,512},{1,769},{257,1},{513,257},{769... | collective-permute-start | bytes 122888 | tf_op jit(solution)/shard_map/ppermute | solution.py:23
  112.1 0.0 collective-permute-done.2
  112.1 2.9 %collective-permute-done.3 = bf16[80,256]{1,0:T(8,128)(2,1)S(1)} collective-permute-done((bf16[80,256]{1,0:T(8,128)(2,1)S(1)}, bf16[80,256]{1,0:T(8,128)(2,1)S(1)}, u32[]{:S(2)}, u32[]{:S(2)}) %collective-permute-start.3) | collective-permute-done | bytes 40992 | tf_op jit(solution)/shard_map/ppermute | solution.py:23
  115.0 0.0 all-to-all-done.3.w_ref
  115.0 0.0 copy-start
  115.0 0.8 broadcast_in_dim.13
  115.8 4.3 %all-to-all-start = ((bf16[4,328,128]{2,1,0:T(8,128)(2,1)}), bf16[4,328,128]{2,1,0:T(8,128)(2,1)S(1)}, u32[]{:S(2)}, u32[]{:S(2)}) async-start(bf16[4,328,128]{2,1,0:T(8,128)(2,1)} %broadcast_in_dim.13), calls=%async_computation | async-start | bytes 671744 | tf_op jit(solution)/shard_map/all_to_all | solution.py:27
  120.2 2.4 %all-gather = bf16[8,80,512]{2,1,0:T(8,128)(2,1)} all-gather(bf16[4,80,512]{2,1,0:T(8,128)(2,1)S(1)} %pad_maximum_fusion), channel_id=2, replica_groups=mesh['zh'=4,'core'=2,'x'=4,'y'=4,'zl'=8] {'core'}, dimensions={0}, use_global_device_ids=true | all-gather | bytes 983040 | tf_op jit(solution)/shard_map/all_gather | solution.py:180
  122.6 0.0 copy-done
  122.6 3.1 %project.1 = bf16[8,88,256]{2,1,0:T(8,128)(2,1)} custom-call(s32[1]{0:T(128)} %bitcast.3.zh_ref, s32[2]{0:T(128)} %span_ref.1, bf16[2,4,80,512]{3,2,1,0:T(8,128)(2,1)} %bitcast.18, bf16[16,8,32,256]{3,2,1,0:T(8,128)(2,1)} %copy-done), custom_call_target="tpu_custom_call" | custom-call | tf_op jit(solution)/shard_map/project/pallas_call | solution.py:193
  125.7 1.6 all-to-all-done.refs_0_
  127.2 0.0 copy-start.1
  127.2 28.3 %all_to_all.37 = bf16[8,88,256]{2,1,0:T(8,128)(2,1)S(1)} all-to-all(bf16[8,88,256]{2,1,0:T(8,128)(2,1)} %project.1), channel_id=1, replica_groups=mesh['zh'=4,'core'=2,'x'=4,'y'=4,'zl'=8] {'zl'}, dimensions={0} | all-to-all | bytes 720896 | tf_op jit(solution)/shard_map/all_to_all | solution.py:27
  155.6 0.1 broadcast_in_dim.33
  155.7 22.1 %all_to_all.38.refs_1_ = bf16[4,8,88,256]{3,2,1,0:T(8,128)(2,1)} all-to-all(bf16[4,8,88,256]{3,2,1,0:T(8,128)(2,1)S(1)} %broadcast_in_dim.33), channel_id=1, replica_groups=mesh['zh'=4,'core'=2,'x'=4,'y'=4,'zl'=8] {'x'}, dimensions={0} | all-to-all | bytes 2883584 | tf_op jit(solution)/shard_map/all_to_all | solution.py:27
  177.8 0.0 copy-done.1
  177.8 8.7 %attend.1 = bf16[4,336,128]{2,1,0:T(8,128)(2,1)} custom-call(bf16[4,328,128]{2,1,0:T(8,128)(2,1)} %copy-done.1, bf16[4,8,88,256]{3,2,1,0:T(8,128)(2,1)} %all_to_all.38.refs_1_), custom_call_target="tpu_custom_call" | custom-call | tf_op jit(solution)/shard_map/attend/pallas_call | solution.py:204
  186.5 12.2 %all_to_all.39.refs_0_ = bf16[4,336,128]{2,1,0:T(8,128)(2,1)} all-to-all(bf16[4,336,128]{2,1,0:T(8,128)(2,1)} %attend.1), channel_id=1, replica_groups=mesh['zh'=4,'core'=2,'x'=4,'y'=4,'zl'=8] {'y'}, dimensions={0} | all-to-all | bytes 688128 | tf_op jit(solution)/shard_map/all_to_all | solution.py:27
  198.7 2.0 %combine.1 = bf16[80,512]{1,0:T(8,128)(2,1)} custom-call(bf16[4,336,128]{2,1,0:T(8,128)(2,1)} %all_to_all.39.refs_0_), custom_call_target="tpu_custom_call" | custom-call | tf_op jit(solution)/shard_map/combine/pallas_call | solution.py:216
  (11 shorter events, 0.2 us)
Async XLA Ops:
  68.9 7.2 %copy-start.2 = (bf16[80,512]{1,0:T(8,128)(2,1)S(1)}, bf16[80,512]{1,0:T(8,128)(2,1)}, u32[]{:S(2)}) copy-start(bf16[80,512]{1,0:T(8,128)(2,1)} %param.4) | copy-start | bytes 245764
  68.9 21.8 %copy-start.4 = (s32[2]{0:T(128)S(1)}, s32[2]{0:T(128)}, u32[]{:S(2)}) copy-start(s32[2]{0:T(128)} %span_ref.1) | copy-start | bytes 28
  68.9 21.8 %copy-start.3 = (bf16[80,4,128]{2,1,0:T(4,128)(2,1)S(1)}, bf16[80,4,128]{2,1,0:T(4,128)(2,1)}, u32[]{:S(2)}) copy-start(bf16[80,4,128]{2,1,0:T(4,128)(2,1)} %param.5) | copy-start | bytes 245764
  68.9 46.1 %all-to-all-start.3 = ((bf16[16,8,32,256]{3,2,1,0:T(8,128)(2,1)}), bf16[16,8,32,256]{3,2,1,0:T(8,128)(2,1)S(1)}, u32[]{:S(2)}, u32[]{:S(2)}) async-start(bf16[16,8,32,256]{3,2,1,0:T(8,128)(2,1)} %broadcast_in_dim.32), calls=%async_computation.3 | async-start | bytes 4194304 | tf_op jit(solution)/shard_map/all_to_all | solution.py:27
  76.0 16.2 %collective-permute-start.1 = (bf16[80,512]{1,0:T(8,128)(2,1)S(1)}, bf16[80,512]{1,0:T(8,128)(2,1)S(1)}, u32[]{:S(2)}, u32[]{:S(2)}) collective-permute-start(bf16[80,512]{1,0:T(8,128)(2,1)S(1)} %copy-done.2), channel_id=1, source_target_pairs={{0,256},{256,512},{512,768},{768,0},{1,257},{257,513},{513,769},{7... | collective-permute-start | bytes 245768 | tf_op jit(solution)/shard_map/ppermute | solution.py:23
  78.7 21.5 %collective-permute-start = (bf16[80,512]{1,0:T(8,128)(2,1)S(1)}, bf16[80,512]{1,0:T(8,128)(2,1)S(1)}, u32[]{:S(2)}, u32[]{:S(2)}) collective-permute-start(bf16[80,512]{1,0:T(8,128)(2,1)S(1)} %copy-done.2), channel_id=1, source_target_pairs={{0,768},{256,0},{512,256},{768,512},{1,769},{257,1},{513,257},{769... | collective-permute-start | bytes 245768 | tf_op jit(solution)/shard_map/ppermute | solution.py:23
  92.2 19.8 %collective-permute-start.2 = (bf16[80,256]{1,0:T(8,128)(2,1)S(1)}, bf16[80,256]{1,0:T(8,128)(2,1)S(1)}, u32[]{:S(2)}, u32[]{:S(2)}) collective-permute-start(bf16[80,256]{1,0:T(8,128)(2,1)S(1)} %slice.8), channel_id=1, source_target_pairs={{0,256},{256,512},{512,768},{768,0},{1,257},{257,513},{513,769},{7... | collective-permute-start | bytes 122888 | tf_op jit(solution)/shard_map/ppermute | solution.py:23
  100.2 14.7 %collective-permute-start.3 = (bf16[80,256]{1,0:T(8,128)(2,1)S(1)}, bf16[80,256]{1,0:T(8,128)(2,1)S(1)}, u32[]{:S(2)}, u32[]{:S(2)}) collective-permute-start(bf16[80,256]{1,0:T(8,128)(2,1)S(1)} %slice.9), channel_id=1, source_target_pairs={{0,768},{256,0},{512,256},{768,512},{1,769},{257,1},{513,257},{769... | collective-permute-start | bytes 122888 | tf_op jit(solution)/shard_map/ppermute | solution.py:23
  115.0 7.6 %copy-start = (bf16[16,8,32,256]{3,2,1,0:T(8,128)(2,1)}, bf16[16,8,32,256]{3,2,1,0:T(8,128)(2,1)S(1)}, u32[]{:S(2)}) copy-start(bf16[16,8,32,256]{3,2,1,0:T(8,128)(2,1)S(1)} %all-to-all-done.3.w_ref) | copy-start | bytes 6291460
  115.8 11.4 %all-to-all-start = ((bf16[4,328,128]{2,1,0:T(8,128)(2,1)}), bf16[4,328,128]{2,1,0:T(8,128)(2,1)S(1)}, u32[]{:S(2)}, u32[]{:S(2)}) async-start(bf16[4,328,128]{2,1,0:T(8,128)(2,1)} %broadcast_in_dim.13), calls=%async_computation | async-start | bytes 671744 | tf_op jit(solution)/shard_map/all_to_all | solution.py:27
  127.2 50.5 %copy-start.1 = (bf16[4,328,128]{2,1,0:T(8,128)(2,1)}, bf16[4,328,128]{2,1,0:T(8,128)(2,1)S(1)}, u32[]{:S(2)}) copy-start(bf16[4,328,128]{2,1,0:T(8,128)(2,1)S(1)} %all-to-all-done.refs_0_) | copy-start | bytes 1007620

commit v2 on v1

--- a/solution.py
+++ b/solution.py
@@ -55,7 +55,10 @@
         out_ref[peer, tokens:, :] = spans
 
 
-def attend_kernel(q_ref, kv_ref, out_ref, stat_ref, pos_ref, *, scale):
+def attend_kernel(y_ref, q0_ref, q1_ref, q2_ref, q3_ref, kv_ref, out_ref, stat_ref, pos_ref, q_ref, *, scale):
+    for place, source_ref in enumerate((q0_ref, q1_ref, q2_ref, q3_ref)):
+        q_ref[place] = source_ref[...]
+    own = y_ref[0]
     blocks, _, width = q_ref.shape
     chunks, peers = kv_ref.shape[:2]
     tokens = kv_ref.shape[2] - SPAN_ROWS
@@ -81,6 +84,7 @@
     stat_ref[...] = jnp.zeros(stat_ref.shape, jnp.float32)
 
     def step(block, carry):
+        owner = lax.rem(own + blocks - block, blocks)
         spans = q_ref[block, rows : rows + SPAN_ROWS, :].astype(jnp.float32) * half
         query_pos = jnp.where(row < half, spans[0:1, 0:1], spans[0:1, 1:2] - half) + row
         query_pos = jnp.concatenate([query_pos] * (rows // tokens), axis=0)
@@ -106,9 +110,9 @@
             )
         seen = total > 0.0
         safe = jnp.where(seen, total, 1.0)
-        out_ref[block, :rows, :] = (mixed / safe).astype(jnp.bfloat16)
+        out_ref[owner, :rows, :] = (mixed / safe).astype(jnp.bfloat16)
         size = jnp.where(seen, top * factor + jnp.log2(safe), HIDDEN)
-        stat_ref[:rows, :] = jnp.where(column == block, size, stat_ref[:rows, :])
+        stat_ref[:rows, :] = jnp.where(column == owner, size, stat_ref[:rows, :])
         return carry
 
     lax.fori_loop(0, blocks, step, 0)
@@ -156,7 +160,7 @@
         out_ref[:, head * width : (head + 1) * width] = kept.astype(out_ref.dtype)
 
 
-VMEM = pl.BlockSpec(memory_space=pltpu.VMEM)
+VMEM = pl.BlockSpec()
 SMEM = pl.BlockSpec(memory_space=pltpu.SMEM)
 
 
@@ -169,6 +173,7 @@
     plane = lax.axis_size(PLANE)
     side = lax.axis_size("y")
     zh = lax.axis_index("zh").astype(jnp.int32).reshape(1)
+    own_y = lax.axis_index("y").astype(jnp.int32).reshape(1)
 
     left = shifted(activations, "zh", 1)
     right = shifted(activations, "zh", -1)
@@ -188,7 +193,10 @@
 
     spans = jnp.pad(span_of.astype(jnp.bfloat16)[None], ((0, SPAN_ROWS - 1), (0, width - 2)))
     q = queries.transpose(1, 0, 2).reshape(rows, width)
-    q = exchanged(copies(jnp.concatenate([q, spans]), side), "y")
+    q = jnp.concatenate([q, spans])
+    moved = []
+    for by in range(1, side):
+        moved.append(shifted(q, "y", by))
 
     kv = pl.pallas_call(
         project_kernel,
@@ -196,6 +204,7 @@
         in_specs=[SMEM, SMEM, VMEM, VMEM],
         out_specs=VMEM,
         name="project",
+        compiler_params=pltpu.CompilerParams(vmem_limit_bytes=12 * 1024 * 1024),
     )(zh, span_of, acts, w)
     kv = exchanged(kv, "zl")
     kv = exchanged(copies(kv, side), "x")
@@ -204,14 +213,16 @@
     mixed = pl.pallas_call(
         lambda *refs: attend_kernel(*refs, scale=1.0 / math.sqrt(width)),
         out_shape=jax.ShapeDtypeStruct((side, rows + STAT_ROWS, width), jnp.bfloat16),
-        in_specs=[VMEM, VMEM],
+        in_specs=[SMEM] + [VMEM] * 5,
         out_specs=VMEM,
         scratch_shapes=[
             pltpu.VMEM((padded, 128), jnp.float32),
             pltpu.VMEM((8, line * tokens), jnp.float32),
+            pltpu.VMEM((side, rows + SPAN_ROWS, width), jnp.bfloat16),
         ],
         name="attend",
-    )(q, kv)
+        compiler_params=pltpu.CompilerParams(vmem_limit_bytes=20 * 1024 * 1024),
+    )(own_y, q, *moved, kv)
     mixed = exchanged(mixed, "y")
     return pl.pallas_call(
         lambda *refs: combine_kernel(*refs, rows=rows),
@@ -220,6 +231,7 @@
         out_specs=VMEM,
         scratch_shapes=[pltpu.VMEM((rows, width), jnp.float32)],
         name="combine",
+        compiler_params=pltpu.CompilerParams(vmem_limit_bytes=8 * 1024 * 1024),
     )(mixed)
 
 

time: 202 us -> 191 us (0.946)
  blocking collectives: 131 us -> 109 us
  starting transfers between devices: 44 us -> 55.4 us
  waiting for transfers between devices: 7.88 us -> 13.1 us
  Pallas kernels: 13.8 us -> 8.68 us
    all_to_all x5 -> x4, blocking collectives: 129 us -> 107 us  [exchanged(): return lax.all_to_all(blocks, axes, 0, 0, tiled=True)]
    ppermute x4 -> x7, starting transfers between devices: 32.5 us -> 43.8 us  [shifted(): lax.ppermute(value, axis, [(i, (i + by) % size) for i in range(size)])]
    ppermute x4 -> x7, waiting for transfers between devices: 6.31 us -> 9.34 us  [shifted(): lax.ppermute(value, axis, [(i, (i + by) % size) for i in range(size)])]
    all_to_all x2, waiting for transfers between devices: 1.57 us -> 3.81 us  [exchanged(): return lax.all_to_all(blocks, axes, 0, 0, tiled=True)]
    pallas_call x1, Pallas kernels: 8.7 us -> 6.62 us  [body(): pl.pallas_call(lambda *refs: attend_kernel(*refs, scale=1.0 / math.sqrt(w...]
    pallas_call x1, Pallas kernels: 3.05 us -> 1.03 us  [body(): pl.pallas_call(project_kernel, out_shape=jax.ShapeDtypeStruct((line, toke...]
  transfers between devices with their start and end apart: 6 -> 9, of which waited for: 4 -> 5; matrix products, arithmetic and copies ran while one was open for 0% -> 0% of each run, Pallas kernels for 2% -> 0%
where the time goes in v2:
time: 191 us
  blocking collectives  109 us (57%)
  starting transfers between devices  55.4 us (29%)
  waiting for transfers between devices  13.1 us (7%)
  Pallas kernels  8.68 us (5%)
  local copies, waits for them, and re-layouts  3.66 us (2%)
    all_to_all x4, blocking collectives, exchanged(): return lax.all_to_all(blocks, axes, 0, 0, tiled=True)  107 us
    ppermute x7, starting transfers between devices, shifted(): lax.ppermute(value, axis, [(i, (i + by) % size) for i in range(size)])  43.8 us
    all_to_all x2, starting transfers between devices, exchanged(): return lax.all_to_all(blocks, axes, 0, 0, tiled=True)  11.6 us
    ppermute x7, waiting for transfers between devices, shifted(): lax.ppermute(value, axis, [(i, (i + by) % size) for i in range(size)])  9.34 us
    pallas_call x1, Pallas kernels, body(): pl.pallas_call(lambda *refs: attend_kernel(*refs, scale=1.0 / math.sqrt(w...  6.62 us
  transfers between devices with their start and end apart: 9, of which 5 were waited for; matrix products, arithmetic and copies ran while one was open for 0% of the time, Pallas kernels for 0%

profile of v2, /device:TPU:32, one launch (start us, length us, event | category | flops | bytes accessed | tf_op | source)
XLA Modules:
  0.0 190.5 jit_solution(7622199575802181136)
XLA Ops:
  0.0 0.7 reshape.20
  0.8 49.5 %all_to_all.30 = bf16[8,4,256]{2,1,0:T(4,128)(2,1)S(1)} all-to-all(bf16[8,4,256]{2,1,0:T(4,128)(2,1)S(1)} %bitcast.25), channel_id=1, replica_groups=mesh['zh'=4,'core'=2,'x'=4,'y'=4,'zl'=8] {'zh','core'}, dimensions={0} | all-to-all | bytes 32768 | tf_op jit(solution)/shard_map/all_to_all | solution.py:27
  50.3 17.0 %all_to_all.31 = bf16[8,8,4,256]{3,2,1,0:T(4,128)(2,1)S(1)} all-to-all(bf16[8,8,4,256]{3,2,1,0:T(4,128)(2,1)S(1)} %broadcast_in_dim.11), channel_id=1, replica_groups=mesh['zh'=4,'core'=2,'x'=4,'y'=4,'zl'=8] {'zl'}, dimensions={0} | all-to-all | bytes 262144 | tf_op jit(solution)/shard_map/all_to_all | solution.py:27
  67.3 1.6 broadcast_in_dim.25
  68.9 0.0 copy-start.1
  68.9 0.0 copy-start
  68.9 7.2 %all-to-all-start.2 = ((bf16[16,8,32,256]{3,2,1,0:T(8,128)(2,1)}), bf16[16,8,32,256]{3,2,1,0:T(8,128)(2,1)S(1)}, u32[]{:S(2)}, u32[]{:S(2)}) async-start(bf16[16,8,32,256]{3,2,1,0:T(8,128)(2,1)} %broadcast_in_dim.25), calls=%async_computation.2 | async-start | bytes 4194304 | tf_op jit(solution)/shard_map/all_to_all | solution.py:27
  76.0 0.0 copy-done.1
  76.0 2.7 %collective-permute-start.4 = (bf16[80,512]{1,0:T(8,128)(2,1)S(1)}, bf16[80,512]{1,0:T(8,128)(2,1)S(1)}, u32[]{:S(2)}, u32[]{:S(2)}) collective-permute-start(bf16[80,512]{1,0:T(8,128)(2,1)S(1)} %copy-done.1), channel_id=1, source_target_pairs={{0,256},{256,512},{512,768},{768,0},{1,257},{257,513},{513,769},{7... | collective-permute-start | bytes 245768 | tf_op jit(solution)/shard_map/ppermute | solution.py:23
  78.7 11.9 %collective-permute-start.3 = (bf16[80,512]{1,0:T(8,128)(2,1)S(1)}, bf16[80,512]{1,0:T(8,128)(2,1)S(1)}, u32[]{:S(2)}, u32[]{:S(2)}) collective-permute-start(bf16[80,512]{1,0:T(8,128)(2,1)S(1)} %copy-done.1), channel_id=1, source_target_pairs={{0,768},{256,0},{512,256},{768,512},{1,769},{257,1},{513,257},{769... | collective-permute-start | bytes 245768 | tf_op jit(solution)/shard_map/ppermute | solution.py:23
  90.6 1.6 collective-permute-done.4
  92.2 6.1 %collective-permute-start.5 = (bf16[80,256]{1,0:T(8,128)(2,1)S(1)}, bf16[80,256]{1,0:T(8,128)(2,1)S(1)}, u32[]{:S(2)}, u32[]{:S(2)}) collective-permute-start(bf16[80,256]{1,0:T(8,128)(2,1)S(1)} %slice.8), channel_id=1, source_target_pairs={{0,256},{256,512},{512,768},{768,0},{1,257},{257,513},{513,769},{7... | collective-permute-start | bytes 122888 | tf_op jit(solution)/shard_map/ppermute | solution.py:23
  98.4 1.8 collective-permute-done.3
  100.2 11.8 %collective-permute-start.6 = (bf16[80,256]{1,0:T(8,128)(2,1)S(1)}, bf16[80,256]{1,0:T(8,128)(2,1)S(1)}, u32[]{:S(2)}, u32[]{:S(2)}) collective-permute-start(bf16[80,256]{1,0:T(8,128)(2,1)S(1)} %slice.9), channel_id=1, source_target_pairs={{0,768},{256,0},{512,256},{768,512},{1,769},{257,1},{513,257},{769... | collective-permute-start | bytes 122888 | tf_op jit(solution)/shard_map/ppermute | solution.py:23
  112.0 0.0 collective-permute-done.5
  112.1 2.9 %collective-permute-done.6 = bf16[80,256]{1,0:T(8,128)(2,1)S(1)} collective-permute-done((bf16[80,256]{1,0:T(8,128)(2,1)S(1)}, bf16[80,256]{1,0:T(8,128)(2,1)S(1)}, u32[]{:S(2)}, u32[]{:S(2)}) %collective-permute-start.6) | collective-permute-done | bytes 40992 | tf_op jit(solution)/shard_map/ppermute | solution.py:23
  115.0 2.3 %all-gather = bf16[8,80,512]{2,1,0:T(8,128)(2,1)S(1)} all-gather(bf16[4,80,512]{2,1,0:T(8,128)(2,1)S(1)} %pad_maximum_fusion), channel_id=2, replica_groups=mesh['zh'=4,'core'=2,'x'=4,'y'=4,'zl'=8] {'core'}, dimensions={0}, use_global_device_ids=true | all-gather | bytes 983040 | tf_op jit(solution)/shard_map/all_gather | solution.py:185
  117.3 0.0 all-to-all-done.2.w_ref
  117.3 0.0 copy-done
  117.3 1.0 project.1
  118.3 29.6 %all_to_all.32 = bf16[8,88,256]{2,1,0:T(8,128)(2,1)S(1)} all-to-all(bf16[8,88,256]{2,1,0:T(8,128)(2,1)S(1)} %project.1), channel_id=1, replica_groups=mesh['zh'=4,'core'=2,'x'=4,'y'=4,'zl'=8] {'zl'}, dimensions={0} | all-to-all | bytes 720896 | tf_op jit(solution)/shard_map/all_to_all | solution.py:27
  147.9 0.0 copy-start.2
  147.9 1.2 broadcast_in_dim.26
  149.1 4.4 %all-to-all-start.4 = ((bf16[4,8,88,256]{3,2,1,0:T(8,128)(2,1)}), bf16[4,8,88,256]{3,2,1,0:T(8,128)(2,1)S(1)}, u32[]{:S(2)}, u32[]{:S(2)}) async-start(bf16[4,8,88,256]{3,2,1,0:T(8,128)(2,1)} %broadcast_in_dim.26), calls=%async_computation.4 | async-start | bytes 2883584 | tf_op jit(solution)/shard_map/all_to_all | solution.py:27
  153.5 0.0 copy-done.2
  153.6 3.4 %collective-permute-start = (bf16[328,128]{1,0:T(8,128)(2,1)S(1)}, bf16[328,128]{1,0:T(8,128)(2,1)S(1)}, u32[]{:S(2)}, u32[]{:S(2)}) collective-permute-start(bf16[328,128]{1,0:T(8,128)(2,1)S(1)} %fusion.1.refs_1_), channel_id=1, source_target_pairs={{0,8},{8,16},{16,24},{24,0},{1,9},{9,17},{17,25},{25,1},{2,10},{10... | collective-permute-start | bytes 251912 | tf_op jit(solution)/shard_map/ppermute | solution.py:23
  157.0 4.6 %collective-permute-start.1 = (bf16[328,128]{1,0:T(8,128)(2,1)S(1)}, bf16[328,128]{1,0:T(8,128)(2,1)S(1)}, u32[]{:S(2)}, u32[]{:S(2)}) collective-permute-start(bf16[328,128]{1,0:T(8,128)(2,1)S(1)} %fusion.1.refs_1_), channel_id=1, source_target_pairs={{0,16},{8,24},{16,0},{24,8},{1,17},{9,25},{17,1},{25,9},{2,18},{10... | collective-permute-start | bytes 251912 | tf_op jit(solution)/shard_map/ppermute | solution.py:23
  161.5 3.4 %collective-permute-start.2 = (bf16[328,128]{1,0:T(8,128)(2,1)S(1)}, bf16[328,128]{1,0:T(8,128)(2,1)S(1)}, u32[]{:S(2)}, u32[]{:S(2)}) collective-permute-start(bf16[328,128]{1,0:T(8,128)(2,1)S(1)} %fusion.1.refs_1_), channel_id=1, source_target_pairs={{0,24},{8,0},{16,8},{24,16},{1,25},{9,1},{17,9},{25,17},{2,26},{10... | collective-permute-start | bytes 251912 | tf_op jit(solution)/shard_map/ppermute | solution.py:23
  164.9 0.0 collective-permute-done.refs_2_
  164.9 0.0 collective-permute-done.1.refs_3_
  164.9 3.0 %collective-permute-done.2.refs_4_ = bf16[328,128]{1,0:T(8,128)(2,1)S(1)} collective-permute-done((bf16[328,128]{1,0:T(8,128)(2,1)S(1)}, bf16[328,128]{1,0:T(8,128)(2,1)S(1)}, u32[]{:S(2)}, u32[]{:S(2)}) %collective-permute-start.2) | collective-permute-done | bytes 84000 | tf_op jit(solution)/shard_map/ppermute | solution.py:23
  167.9 3.8 %all-to-all-done.4.refs_5_ = bf16[4,8,88,256]{3,2,1,0:T(8,128)(2,1)S(1)} async-done(((bf16[4,8,88,256]{3,2,1,0:T(8,128)(2,1)}), bf16[4,8,88,256]{3,2,1,0:T(8,128)(2,1)S(1)}, u32[]{:S(2)}, u32[]{:S(2)}) %all-to-all-start.4) | async-done | bytes 1441824 | tf_op jit(solution)/shard_map/all_to_all | solution.py:27
  171.7 6.6 %attend.1 = bf16[4,336,128]{2,1,0:T(8,128)(2,1)S(1)} custom-call(s32[1]{0:T(128)} %bitcast.refs_0_, bf16[328,128]{1,0:T(8,128)(2,1)S(1)} %fusion.1.refs_1_, bf16[328,128]{1,0:T(8,128)(2,1)S(1)} %collective-permute-done.refs_2_, bf16[328,128]{1,0:T(8,128)(2,1)S(1)} %collective-permute-done.1.refs_3_, bf16[328,128]{1,0:T(8,128)(2,1)S(1)} %collective-permute-done.2.refs_4_, ...), custom_call_target="tpu_custom_call" | custom-call | tf_op jit(solution)/shard_map/attend/pallas_call | solution.py:213
  178.3 11.1 %all_to_all.33.refs_0_ = bf16[4,336,128]{2,1,0:T(8,128)(2,1)S(1)} all-to-all(bf16[4,336,128]{2,1,0:T(8,128)(2,1)S(1)} %attend.1), channel_id=1, replica_groups=mesh['zh'=4,'core'=2,'x'=4,'y'=4,'zl'=8] {'y'}, dimensions={0} | all-to-all | bytes 688128 | tf_op jit(solution)/shard_map/all_to_all | solution.py:27
  189.5 1.0 combine.1
  (11 shorter events, 0.2 us)
Async XLA Ops:
  68.9 7.2 %copy-start.1 = (bf16[80,512]{1,0:T(8,128)(2,1)S(1)}, bf16[80,512]{1,0:T(8,128)(2,1)}, u32[]{:S(2)}) copy-start(bf16[80,512]{1,0:T(8,128)(2,1)} %param.4) | copy-start | bytes 245764
  68.9 48.4 %copy-start = (s32[2]{0:T(128)S(1)}, s32[2]{0:T(128)}, u32[]{:S(2)}) copy-start(s32[2]{0:T(128)} %span_ref.1) | copy-start | bytes 28
  68.9 48.4 %all-to-all-start.2 = ((bf16[16,8,32,256]{3,2,1,0:T(8,128)(2,1)}), bf16[16,8,32,256]{3,2,1,0:T(8,128)(2,1)S(1)}, u32[]{:S(2)}, u32[]{:S(2)}) async-start(bf16[16,8,32,256]{3,2,1,0:T(8,128)(2,1)} %broadcast_in_dim.25), calls=%async_computation.2 | async-start | bytes 4194304 | tf_op jit(solution)/shard_map/all_to_all | solution.py:27
  76.0 16.2 %collective-permute-start.4 = (bf16[80,512]{1,0:T(8,128)(2,1)S(1)}, bf16[80,512]{1,0:T(8,128)(2,1)S(1)}, u32[]{:S(2)}, u32[]{:S(2)}) collective-permute-start(bf16[80,512]{1,0:T(8,128)(2,1)S(1)} %copy-done.1), channel_id=1, source_target_pairs={{0,256},{256,512},{512,768},{768,0},{1,257},{257,513},{513,769},{7... | collective-permute-start | bytes 245768 | tf_op jit(solution)/shard_map/ppermute | solution.py:23
  78.7 21.5 %collective-permute-start.3 = (bf16[80,512]{1,0:T(8,128)(2,1)S(1)}, bf16[80,512]{1,0:T(8,128)(2,1)S(1)}, u32[]{:S(2)}, u32[]{:S(2)}) collective-permute-start(bf16[80,512]{1,0:T(8,128)(2,1)S(1)} %copy-done.1), channel_id=1, source_target_pairs={{0,768},{256,0},{512,256},{768,512},{1,769},{257,1},{513,257},{769... | collective-permute-start | bytes 245768 | tf_op jit(solution)/shard_map/ppermute | solution.py:23
  92.2 19.8 %collective-permute-start.5 = (bf16[80,256]{1,0:T(8,128)(2,1)S(1)}, bf16[80,256]{1,0:T(8,128)(2,1)S(1)}, u32[]{:S(2)}, u32[]{:S(2)}) collective-permute-start(bf16[80,256]{1,0:T(8,128)(2,1)S(1)} %slice.8), channel_id=1, source_target_pairs={{0,256},{256,512},{512,768},{768,0},{1,257},{257,513},{513,769},{7... | collective-permute-start | bytes 122888 | tf_op jit(solution)/shard_map/ppermute | solution.py:23
  100.2 14.7 %collective-permute-start.6 = (bf16[80,256]{1,0:T(8,128)(2,1)S(1)}, bf16[80,256]{1,0:T(8,128)(2,1)S(1)}, u32[]{:S(2)}, u32[]{:S(2)}) collective-permute-start(bf16[80,256]{1,0:T(8,128)(2,1)S(1)} %slice.9), channel_id=1, source_target_pairs={{0,768},{256,0},{512,256},{768,512},{1,769},{257,1},{513,257},{769... | collective-permute-start | bytes 122888 | tf_op jit(solution)/shard_map/ppermute | solution.py:23
  147.9 5.6 %copy-start.2 = (bf16[80,4,128]{2,1,0:T(4,128)(2,1)S(1)}, bf16[80,4,128]{2,1,0:T(4,128)(2,1)}, u32[]{:S(2)}) copy-start(bf16[80,4,128]{2,1,0:T(4,128)(2,1)} %param.5) | copy-start | bytes 245764
  149.1 22.6 %all-to-all-start.4 = ((bf16[4,8,88,256]{3,2,1,0:T(8,128)(2,1)}), bf16[4,8,88,256]{3,2,1,0:T(8,128)(2,1)S(1)}, u32[]{:S(2)}, u32[]{:S(2)}) async-start(bf16[4,8,88,256]{3,2,1,0:T(8,128)(2,1)} %broadcast_in_dim.26), calls=%async_computation.4 | async-start | bytes 2883584 | tf_op jit(solution)/shard_map/all_to_all | solution.py:27
  153.6 11.4 %collective-permute-start = (bf16[328,128]{1,0:T(8,128)(2,1)S(1)}, bf16[328,128]{1,0:T(8,128)(2,1)S(1)}, u32[]{:S(2)}, u32[]{:S(2)}) collective-permute-start(bf16[328,128]{1,0:T(8,128)(2,1)S(1)} %fusion.1.refs_1_), channel_id=1, source_target_pairs={{0,8},{8,16},{16,24},{24,0},{1,9},{9,17},{17,25},{25,1},{2,10},{10... | collective-permute-start | bytes 251912 | tf_op jit(solution)/shard_map/ppermute | solution.py:23
  157.0 8.0 %collective-permute-start.1 = (bf16[328,128]{1,0:T(8,128)(2,1)S(1)}, bf16[328,128]{1,0:T(8,128)(2,1)S(1)}, u32[]{:S(2)}, u32[]{:S(2)}) collective-permute-start(bf16[328,128]{1,0:T(8,128)(2,1)S(1)} %fusion.1.refs_1_), channel_id=1, source_target_pairs={{0,16},{8,24},{16,0},{24,8},{1,17},{9,25},{17,1},{25,9},{2,18},{10... | collective-permute-start | bytes 251912 | tf_op jit(solution)/shard_map/ppermute | solution.py:23
  161.5 6.4 %collective-permute-start.2 = (bf16[328,128]{1,0:T(8,128)(2,1)S(1)}, bf16[328,128]{1,0:T(8,128)(2,1)S(1)}, u32[]{:S(2)}, u32[]{:S(2)}) collective-permute-start(bf16[328,128]{1,0:T(8,128)(2,1)S(1)} %fusion.1.refs_1_), channel_id=1, source_target_pairs={{0,24},{8,0},{16,8},{24,16},{1,25},{9,1},{17,9},{25,17},{2,26},{10... | collective-permute-start | bytes 251912 | tf_op jit(solution)/shard_map/ppermute | solution.py:23

commit v3 on v2

--- a/solution.py
+++ b/solution.py
@@ -9,9 +9,10 @@
 from jax.sharding import PartitionSpec as P
 
 
-ROWS = ("x", "y", "zl")
+ROWS = ("x", "y", "zo", "zi")
 HEADS = ("zh", "core")
 PLANE = ("x", "y")
+LINE = ("zo", "zi")
 HIDDEN = -1e30
 FLOOR = -1e29
 STAT_ROWS = 16
@@ -49,16 +50,14 @@
             part = jnp.dot(act, w.reshape(-1, w.shape[-1]), preferred_element_type=jnp.float32)
             total = part if total is None else total + part
     rounded = total.astype(out_ref.dtype)
-    spans = span_rows(span_ref[0], span_ref[1], (SPAN_ROWS, total.shape[1]))
-    for peer in range(out_ref.shape[0]):
-        out_ref[peer, :tokens, :] = rounded
-        out_ref[peer, tokens:, :] = spans
-
-
-def attend_kernel(y_ref, q0_ref, q1_ref, q2_ref, q3_ref, kv_ref, out_ref, stat_ref, pos_ref, q_ref, *, scale):
+    out_ref[:tokens, :] = rounded
+    out_ref[tokens:, :] = span_rows(span_ref[0], span_ref[1], (SPAN_ROWS, total.shape[1]))
+
+
+def attend_kernel(own_ref, q0_ref, q1_ref, q2_ref, q3_ref, kv_ref, out_ref, stat_ref, pos_ref, q_ref, *, scale):
     for place, source_ref in enumerate((q0_ref, q1_ref, q2_ref, q3_ref)):
         q_ref[place] = source_ref[...]
-    own = y_ref[0]
+    own = own_ref[0]
     blocks, _, width = q_ref.shape
     chunks, peers = kv_ref.shape[:2]
     tokens = kv_ref.shape[2] - SPAN_ROWS
@@ -165,29 +164,26 @@
 
 
 def body(activations, queries, w_kv, span_of):
-    tokens, features = activations.shape
+    tokens, _ = activations.shape
     group, width = queries.shape[1:]
     rows = tokens * group
     ranks = lax.axis_size(HEADS)
-    line = lax.axis_size("zl")
+    line = lax.axis_size(LINE)
     plane = lax.axis_size(PLANE)
-    side = lax.axis_size("y")
+    side = lax.axis_size("zi")
     zh = lax.axis_index("zh").astype(jnp.int32).reshape(1)
-    own_y = lax.axis_index("y").astype(jnp.int32).reshape(1)
+    own = lax.axis_index("zi").astype(jnp.int32).reshape(1)
 
     left = shifted(activations, "zh", 1)
     right = shifted(activations, "zh", -1)
-    cut = features // 2
-    far_a = shifted(left[:, :cut], "zh", 1)
-    far_b = shifted(right[:, cut:], "zh", -1)
-    far = jnp.concatenate([far_a, far_b], axis=1)
+    far = shifted(activations, "zh", 2)
     near = jnp.stack([activations, right, far, left])
     acts = lax.all_gather(near, "core")
 
     piece = w_kv.shape[0]
     w = w_kv.reshape(piece, ranks, 2 * width).transpose(1, 0, 2)
     w = exchanged(w, HEADS)
-    w = exchanged(copies(w, line), "zl")
+    w = exchanged(copies(w, line), LINE)
     w = w.transpose(1, 0, 2, 3).reshape(ranks, line * piece, 2 * width)
     w = exchanged(copies(w, plane), PLANE)
 
@@ -196,18 +192,19 @@
     q = jnp.concatenate([q, spans])
     moved = []
     for by in range(1, side):
-        moved.append(shifted(q, "y", by))
+        moved.append(shifted(q, "zi", by))
 
     kv = pl.pallas_call(
         project_kernel,
-        out_shape=jax.ShapeDtypeStruct((line, tokens + SPAN_ROWS, 2 * width), jnp.bfloat16),
+        out_shape=jax.ShapeDtypeStruct((tokens + SPAN_ROWS, 2 * width), jnp.bfloat16),
         in_specs=[SMEM, SMEM, VMEM, VMEM],
         out_specs=VMEM,
         name="project",
         compiler_params=pltpu.CompilerParams(vmem_limit_bytes=12 * 1024 * 1024),
     )(zh, span_of, acts, w)
-    kv = exchanged(kv, "zl")
-    kv = exchanged(copies(kv, side), "x")
+    kv = jnp.stack([kv, shifted(kv, "zo", 1)])
+    kv = exchanged(copies(kv, plane), PLANE)
+    kv = kv.reshape(side, plane * 2 // side, tokens + SPAN_ROWS, 2 * width)
 
     padded = (rows + 127) // 128 * 128
     mixed = pl.pallas_call(
@@ -217,13 +214,13 @@
         out_specs=VMEM,
         scratch_shapes=[
             pltpu.VMEM((padded, 128), jnp.float32),
-            pltpu.VMEM((8, line * tokens), jnp.float32),
+            pltpu.VMEM((8, plane * 2 // side * tokens), jnp.float32),
             pltpu.VMEM((side, rows + SPAN_ROWS, width), jnp.bfloat16),
         ],
         name="attend",
         compiler_params=pltpu.CompilerParams(vmem_limit_bytes=20 * 1024 * 1024),
-    )(own_y, q, *moved, kv)
-    mixed = exchanged(mixed, "y")
+    )(own, q, *moved, kv)
+    mixed = exchanged(mixed, "zi")
     return pl.pallas_call(
         lambda *refs: combine_kernel(*refs, rows=rows),
         out_shape=jax.ShapeDtypeStruct((tokens, group * width), jnp.bfloat16),
@@ -236,6 +233,6 @@
 
 
 def solution(mesh):
-    finer = Mesh(mesh.devices.reshape(4, 2, 4, 4, 8), ("zh", "core", "x", "y", "zl"))
+    finer = Mesh(mesh.devices.reshape(4, 2, 4, 4, 2, 4), ("zh", "core", "x", "y", "zo", "zi"))
     in_specs = (P(ROWS, HEADS), P(ROWS, HEADS, None), P(HEADS + ROWS, None, None, None), P(ROWS))
     return jax.shard_map(body, mesh=finer, in_specs=in_specs, out_specs=P(ROWS, HEADS), check_vma=False)

time: 191 us -> 186 us (0.974)
  the two profiles are of different devices: /device:TPU:32 before, /device:TPU:8 now
where the time goes in v3:
time: 186 us; the launch traced here: 185 us
  blocking collectives  84.9 us (46%)
  starting transfers between devices  46.5 us (25%)
  waiting for transfers between devices  41.5 us (22%)
  Pallas kernels  8.69 us (5%)
  local copies, waits for them, and re-layouts  3.65 us (2%)
    all_to_all x3, blocking collectives, exchanged(): return lax.all_to_all(blocks, axes, 0, 0, tiled=True)  82.7 us
    ppermute x7, waiting for transfers between devices, shifted(): lax.ppermute(value, axis, [(i, (i + by) % size) for i in range(size)])  38.1 us
    ppermute x7, starting transfers between devices, shifted(): lax.ppermute(value, axis, [(i, (i + by) % size) for i in range(size)])  31.8 us
    all_to_all x2, starting transfers between devices, exchanged(): return lax.all_to_all(blocks, axes, 0, 0, tiled=True)  14.7 us
    pallas_call x1, Pallas kernels, body(): pl.pallas_call(lambda *refs: attend_kernel(*refs, scale=1.0 / math.sqrt(w...  6.63 us
  transfers between devices with their start and end apart: 9, of which 7 were waited for; matrix products, arithmetic and copies ran while one was open for 0% of the time, Pallas kernels for 0%

profile of v3, /device:TPU:8, one launch (start us, length us, event | category | flops | bytes accessed | tf_op | source)
XLA Modules:
  0.0 185.5 jit_solution(7597695360192524645)
XLA Ops:
  0.0 0.7 reshape.24
  0.8 50.4 %all_to_all.25 = bf16[8,4,256]{2,1,0:T(4,128)(2,1)S(1)} all-to-all(bf16[8,4,256]{2,1,0:T(4,128)(2,1)S(1)} %bitcast.30), channel_id=1, replica_groups=mesh['zh'=4,'core'=2,'x'=4,'y'=4,'zo'=2,'zi'=4] {'zh','core'}, dimensions={0} | all-to-all | bytes 32768 | tf_op jit(solution)/shard_map/all_to_all | solution.py:28
  51.2 16.7 %all_to_all.26 = bf16[8,8,4,256]{3,2,1,0:T(4,128)(2,1)S(1)} all-to-all(bf16[8,8,4,256]{3,2,1,0:T(4,128)(2,1)S(1)} %broadcast_in_dim.11), channel_id=1, replica_groups=mesh['zh'=4,'core'=2,'x'=4,'y'=4,'zo'=2,'zi'=4] {'zo','zi'}, dimensions={0} | all-to-all | bytes 262144 | tf_op jit(solution)/shard_map/all_to_all | solution.py:28
  67.9 1.6 broadcast_in_dim.25
  69.5 0.0 copy-start.1
  69.5 0.0 copy-start
  69.5 7.5 %all-to-all-start.2 = ((bf16[16,8,32,256]{3,2,1,0:T(8,128)(2,1)}), bf16[16,8,32,256]{3,2,1,0:T(8,128)(2,1)S(1)}, u32[]{:S(2)}, u32[]{:S(2)}) async-start(bf16[16,8,32,256]{3,2,1,0:T(8,128)(2,1)} %broadcast_in_dim.25), calls=%async_computation.2 | async-start | bytes 4194304 | tf_op jit(solution)/shard_map/all_to_all | solution.py:28
  77.1 0.0 copy-done.1
  77.1 2.7 %collective-permute-start.3 = (bf16[80,512]{1,0:T(8,128)(2,1)S(1)}, bf16[80,512]{1,0:T(8,128)(2,1)S(1)}, u32[]{:S(2)}, u32[]{:S(2)}) collective-permute-start(bf16[80,512]{1,0:T(8,128)(2,1)S(1)} %copy-done.1), channel_id=1, source_target_pairs={{0,768},{256,0},{512,256},{768,512},{1,769},{257,1},{513,257},{769... | collective-permute-start | bytes 245768 | tf_op jit(solution)/shard_map/ppermute | solution.py:24
  79.7 12.1 %collective-permute-start.4 = (bf16[80,512]{1,0:T(8,128)(2,1)S(1)}, bf16[80,512]{1,0:T(8,128)(2,1)S(1)}, u32[]{:S(2)}, u32[]{:S(2)}) collective-permute-start(bf16[80,512]{1,0:T(8,128)(2,1)S(1)} %copy-done.1), channel_id=1, source_target_pairs={{0,512},{256,768},{512,0},{768,256},{1,513},{257,769},{513,1},{769... | collective-permute-start | bytes 245768 | tf_op jit(solution)/shard_map/ppermute | solution.py:24
  91.8 2.2 %collective-permute-start.5 = (bf16[80,512]{1,0:T(8,128)(2,1)S(1)}, bf16[80,512]{1,0:T(8,128)(2,1)S(1)}, u32[]{:S(2)}, u32[]{:S(2)}) collective-permute-start(bf16[80,512]{1,0:T(8,128)(2,1)S(1)} %copy-done.1), channel_id=1, source_target_pairs={{0,256},{256,512},{512,768},{768,0},{1,257},{257,513},{513,769},{7... | collective-permute-start | bytes 245768 | tf_op jit(solution)/shard_map/ppermute | solution.py:24
  94.0 8.0 %collective-permute-done.3 = bf16[80,512]{1,0:T(8,128)(2,1)S(1)} collective-permute-done((bf16[80,512]{1,0:T(8,128)(2,1)S(1)}, bf16[80,512]{1,0:T(8,128)(2,1)S(1)}, u32[]{:S(2)}, u32[]{:S(2)}) %collective-permute-start.3) | collective-permute-done | bytes 81952 | tf_op jit(solution)/shard_map/ppermute | solution.py:24
  102.0 3.6 %collective-permute-done.4 = bf16[80,512]{1,0:T(8,128)(2,1)S(1)} collective-permute-done((bf16[80,512]{1,0:T(8,128)(2,1)S(1)}, bf16[80,512]{1,0:T(8,128)(2,1)S(1)}, u32[]{:S(2)}, u32[]{:S(2)}) %collective-permute-start.4) | collective-permute-done | bytes 81952 | tf_op jit(solution)/shard_map/ppermute | solution.py:24
  105.7 14.9 %collective-permute-done.5 = bf16[80,512]{1,0:T(8,128)(2,1)S(1)} collective-permute-done((bf16[80,512]{1,0:T(8,128)(2,1)S(1)}, bf16[80,512]{1,0:T(8,128)(2,1)S(1)}, u32[]{:S(2)}, u32[]{:S(2)}) %collective-permute-start.5) | collective-permute-done | bytes 81952 | tf_op jit(solution)/shard_map/ppermute | solution.py:24
  120.6 2.3 %all-gather = bf16[8,80,512]{2,1,0:T(8,128)(2,1)S(1)} all-gather(bf16[4,80,512]{2,1,0:T(8,128)(2,1)S(1)} %pad_maximum_fusion), channel_id=2, replica_groups=mesh['zh'=4,'core'=2,'x'=4,'y'=4,'zo'=2,'zi'=4] {'core'}, dimensions={0}, use_global_device_ids=true | all-gather | bytes 983040 | tf_op jit(solution)/shard_map/all_gather | solution.py:181
  122.9 0.0 all-to-all-done.2.w_ref
  122.9 0.0 copy-done
  122.9 1.0 project.1
  123.9 2.7 %collective-permute-start.6 = (bf16[88,256]{1,0:T(8,128)(2,1)S(1)}, bf16[88,256]{1,0:T(8,128)(2,1)S(1)}, u32[]{:S(2)}, u32[]{:S(2)}) collective-permute-start(bf16[88,256]{1,0:T(8,128)(2,1)S(1)} %project.1), channel_id=1, source_target_pairs={{0,4},{4,0},{1,5},{5,1},{2,6},{6,2},{3,7},{7,3},{8,12},{12,8},{9,1... | collective-permute-start | bytes 135176 | tf_op jit(solution)/shard_map/ppermute | solution.py:24
  126.6 7.1 %collective-permute-done.6 = bf16[88,256]{1,0:T(8,128)(2,1)S(1)} collective-permute-done((bf16[88,256]{1,0:T(8,128)(2,1)S(1)}, bf16[88,256]{1,0:T(8,128)(2,1)S(1)}, u32[]{:S(2)}, u32[]{:S(2)}) %collective-permute-start.6) | collective-permute-done | bytes 45088 | tf_op jit(solution)/shard_map/ppermute | solution.py:24
  133.8 0.0 copy-start.2
  133.8 1.2 broadcast_in_dim.26
  135.0 7.2 %all-to-all-start.3 = ((bf16[16,2,88,256]{3,2,1,0:T(8,128)(2,1)}), bf16[16,2,88,256]{3,2,1,0:T(8,128)(2,1)S(1)}, u32[]{:S(2)}, u32[]{:S(2)}) async-start(bf16[16,2,88,256]{3,2,1,0:T(8,128)(2,1)} %broadcast_in_dim.26), calls=%async_computation.3 | async-start | bytes 2883584 | tf_op jit(solution)/shard_map/all_to_all | solution.py:28
  142.2 0.0 copy-done.2
  142.3 5.4 %collective-permute-start = (bf16[328,128]{1,0:T(8,128)(2,1)S(1)}, bf16[328,128]{1,0:T(8,128)(2,1)S(1)}, u32[]{:S(2)}, u32[]{:S(2)}) collective-permute-start(bf16[328,128]{1,0:T(8,128)(2,1)S(1)} %fusion.1.refs_1_), channel_id=1, source_target_pairs={{0,1},{1,2},{2,3},{3,0},{4,5},{5,6},{6,7},{7,4},{8,9},{9,10},{10,1... | collective-permute-start | bytes 251912 | tf_op jit(solution)/shard_map/ppermute | solution.py:24
  147.6 4.8 %collective-permute-start.1 = (bf16[328,128]{1,0:T(8,128)(2,1)S(1)}, bf16[328,128]{1,0:T(8,128)(2,1)S(1)}, u32[]{:S(2)}, u32[]{:S(2)}) collective-permute-start(bf16[328,128]{1,0:T(8,128)(2,1)S(1)} %fusion.1.refs_1_), channel_id=1, source_target_pairs={{0,2},{1,3},{2,0},{3,1},{4,6},{5,7},{6,4},{7,5},{8,10},{9,11},{10,... | collective-permute-start | bytes 251912 | tf_op jit(solution)/shard_map/ppermute | solution.py:24
  152.5 1.9 %collective-permute-start.2 = (bf16[328,128]{1,0:T(8,128)(2,1)S(1)}, bf16[328,128]{1,0:T(8,128)(2,1)S(1)}, u32[]{:S(2)}, u32[]{:S(2)}) collective-permute-start(bf16[328,128]{1,0:T(8,128)(2,1)S(1)} %fusion.1.refs_1_), channel_id=1, source_target_pairs={{0,3},{1,0},{2,1},{3,2},{4,7},{5,4},{6,5},{7,6},{8,11},{9,8},{10,9... | collective-permute-start | bytes 251912 | tf_op jit(solution)/shard_map/ppermute | solution.py:24
  154.4 0.0 collective-permute-done.refs_2_
  154.4 2.2 %collective-permute-done.1.refs_3_ = bf16[328,128]{1,0:T(8,128)(2,1)S(1)} collective-permute-done((bf16[328,128]{1,0:T(8,128)(2,1)S(1)}, bf16[328,128]{1,0:T(8,128)(2,1)S(1)}, u32[]{:S(2)}, u32[]{:S(2)}) %collective-permute-start.1) | collective-permute-done | bytes 84000 | tf_op jit(solution)/shard_map/ppermute | solution.py:24
  156.7 2.2 %collective-permute-done.2.refs_4_ = bf16[328,128]{1,0:T(8,128)(2,1)S(1)} collective-permute-done((bf16[328,128]{1,0:T(8,128)(2,1)S(1)}, bf16[328,128]{1,0:T(8,128)(2,1)S(1)}, u32[]{:S(2)}, u32[]{:S(2)}) %collective-permute-start.2) | collective-permute-done | bytes 84000 | tf_op jit(solution)/shard_map/ppermute | solution.py:24
  158.8 3.4 %all-to-all-done.3 = bf16[16,2,88,256]{3,2,1,0:T(8,128)(2,1)S(1)} async-done(((bf16[16,2,88,256]{3,2,1,0:T(8,128)(2,1)}), bf16[16,2,88,256]{3,2,1,0:T(8,128)(2,1)S(1)}, u32[]{:S(2)}, u32[]{:S(2)}) %all-to-all-start.3) | async-done | bytes 1441824 | tf_op jit(solution)/shard_map/all_to_all | solution.py:28
  162.2 6.6 %attend.1 = bf16[4,336,128]{2,1,0:T(8,128)(2,1)S(1)} custom-call(s32[1]{0:T(128)} %bitcast.refs_0_, bf16[328,128]{1,0:T(8,128)(2,1)S(1)} %fusion.1.refs_1_, bf16[328,128]{1,0:T(8,128)(2,1)S(1)} %collective-permute-done.refs_2_, bf16[328,128]{1,0:T(8,128)(2,1)S(1)} %collective-permute-done.1.refs_3_, bf16[328,128]{1,0:T(8,128)(2,1)S(1)} %collective-permute-done.2.refs_4_, ...), custom_call_target="tpu_custom_call" | custom-call | tf_op jit(solution)/shard_map/attend/pallas_call | solution.py:210
  168.9 15.6 %all_to_all.27.refs_0_ = bf16[4,336,128]{2,1,0:T(8,128)(2,1)S(1)} all-to-all(bf16[4,336,128]{2,1,0:T(8,128)(2,1)S(1)} %attend.1), channel_id=1, replica_groups=mesh['zh'=4,'core'=2,'x'=4,'y'=4,'zo'=2,'zi'=4] {'zi'}, dimensions={0} | all-to-all | bytes 688128 | tf_op jit(solution)/shard_map/all_to_all | solution.py:28
  184.4 1.0 combine.1
  (9 shorter events, 0.2 us)
Async XLA Ops:
  69.5 7.5 %copy-start.1 = (bf16[80,512]{1,0:T(8,128)(2,1)S(1)}, bf16[80,512]{1,0:T(8,128)(2,1)}, u32[]{:S(2)}) copy-start(bf16[80,512]{1,0:T(8,128)(2,1)} %param.4) | copy-start | bytes 245764
  69.5 53.4 %copy-start = (s32[2]{0:T(128)S(1)}, s32[2]{0:T(128)}, u32[]{:S(2)}) copy-start(s32[2]{0:T(128)} %span_ref.1) | copy-start | bytes 28
  69.5 53.3 %all-to-all-start.2 = ((bf16[16,8,32,256]{3,2,1,0:T(8,128)(2,1)}), bf16[16,8,32,256]{3,2,1,0:T(8,128)(2,1)S(1)}, u32[]{:S(2)}, u32[]{:S(2)}) async-start(bf16[16,8,32,256]{3,2,1,0:T(8,128)(2,1)} %broadcast_in_dim.25), calls=%async_computation.2 | async-start | bytes 4194304 | tf_op jit(solution)/shard_map/all_to_all | solution.py:28
  77.1 25.0 %collective-permute-start.3 = (bf16[80,512]{1,0:T(8,128)(2,1)S(1)}, bf16[80,512]{1,0:T(8,128)(2,1)S(1)}, u32[]{:S(2)}, u32[]{:S(2)}) collective-permute-start(bf16[80,512]{1,0:T(8,128)(2,1)S(1)} %copy-done.1), channel_id=1, source_target_pairs={{0,768},{256,0},{512,256},{768,512},{1,769},{257,1},{513,257},{769... | collective-permute-start | bytes 245768 | tf_op jit(solution)/shard_map/ppermute | solution.py:24
  79.7 25.9 %collective-permute-start.4 = (bf16[80,512]{1,0:T(8,128)(2,1)S(1)}, bf16[80,512]{1,0:T(8,128)(2,1)S(1)}, u32[]{:S(2)}, u32[]{:S(2)}) collective-permute-start(bf16[80,512]{1,0:T(8,128)(2,1)S(1)} %copy-done.1), channel_id=1, source_target_pairs={{0,512},{256,768},{512,0},{768,256},{1,513},{257,769},{513,1},{769... | collective-permute-start | bytes 245768 | tf_op jit(solution)/shard_map/ppermute | solution.py:24
  91.8 28.7 %collective-permute-start.5 = (bf16[80,512]{1,0:T(8,128)(2,1)S(1)}, bf16[80,512]{1,0:T(8,128)(2,1)S(1)}, u32[]{:S(2)}, u32[]{:S(2)}) collective-permute-start(bf16[80,512]{1,0:T(8,128)(2,1)S(1)} %copy-done.1), channel_id=1, source_target_pairs={{0,256},{256,512},{512,768},{768,0},{1,257},{257,513},{513,769},{7... | collective-permute-start | bytes 245768 | tf_op jit(solution)/shard_map/ppermute | solution.py:24
  123.9 9.8 %collective-permute-start.6 = (bf16[88,256]{1,0:T(8,128)(2,1)S(1)}, bf16[88,256]{1,0:T(8,128)(2,1)S(1)}, u32[]{:S(2)}, u32[]{:S(2)}) collective-permute-start(bf16[88,256]{1,0:T(8,128)(2,1)S(1)} %project.1), channel_id=1, source_target_pairs={{0,4},{4,0},{1,5},{5,1},{2,6},{6,2},{3,7},{7,3},{8,12},{12,8},{9,1... | collective-permute-start | bytes 135176 | tf_op jit(solution)/shard_map/ppermute | solution.py:24
  133.8 8.5 %copy-start.2 = (bf16[80,4,128]{2,1,0:T(4,128)(2,1)S(1)}, bf16[80,4,128]{2,1,0:T(4,128)(2,1)}, u32[]{:S(2)}) copy-start(bf16[80,4,128]{2,1,0:T(4,128)(2,1)} %param.5) | copy-start | bytes 245764
  135.0 27.2 %all-to-all-start.3 = ((bf16[16,2,88,256]{3,2,1,0:T(8,128)(2,1)}), bf16[16,2,88,256]{3,2,1,0:T(8,128)(2,1)S(1)}, u32[]{:S(2)}, u32[]{:S(2)}) async-start(bf16[16,2,88,256]{3,2,1,0:T(8,128)(2,1)} %broadcast_in_dim.26), calls=%async_computation.3 | async-start | bytes 2883584 | tf_op jit(solution)/shard_map/all_to_all | solution.py:28
  142.3 12.1 %collective-permute-start = (bf16[328,128]{1,0:T(8,128)(2,1)S(1)}, bf16[328,128]{1,0:T(8,128)(2,1)S(1)}, u32[]{:S(2)}, u32[]{:S(2)}) collective-permute-start(bf16[328,128]{1,0:T(8,128)(2,1)S(1)} %fusion.1.refs_1_), channel_id=1, source_target_pairs={{0,1},{1,2},{2,3},{3,0},{4,5},{5,6},{6,7},{7,4},{8,9},{9,10},{10,1... | collective-permute-start | bytes 251912 | tf_op jit(solution)/shard_map/ppermute | solution.py:24
  147.6 9.0 %collective-permute-start.1 = (bf16[328,128]{1,0:T(8,128)(2,1)S(1)}, bf16[328,128]{1,0:T(8,128)(2,1)S(1)}, u32[]{:S(2)}, u32[]{:S(2)}) collective-permute-start(bf16[328,128]{1,0:T(8,128)(2,1)S(1)} %fusion.1.refs_1_), channel_id=1, source_target_pairs={{0,2},{1,3},{2,0},{3,1},{4,6},{5,7},{6,4},{7,5},{8,10},{9,11},{10,... | collective-permute-start | bytes 251912 | tf_op jit(solution)/shard_map/ppermute | solution.py:24
  152.5 6.4 %collective-permute-start.2 = (bf16[328,128]{1,0:T(8,128)(2,1)S(1)}, bf16[328,128]{1,0:T(8,128)(2,1)S(1)}, u32[]{:S(2)}, u32[]{:S(2)}) collective-permute-start(bf16[328,128]{1,0:T(8,128)(2,1)S(1)} %fusion.1.refs_1_), channel_id=1, source_target_pairs={{0,3},{1,0},{2,1},{3,2},{4,7},{5,4},{6,5},{7,6},{8,11},{9,8},{10,9... | collective-permute-start | bytes 251912 | tf_op jit(solution)/shard_map/ppermute | solution.py:24

commit v4 on v3

--- a/solution.py
+++ b/solution.py
@@ -38,14 +38,15 @@
     return row.astype(jnp.float32).astype(jnp.bfloat16)
 
 
-def project_kernel(zh_ref, span_ref, act_ref, w_ref, out_ref):
+def project_kernel(zh_ref, span_ref, chip_ref, others_ref, w_ref, out_ref):
     zh = zh_ref[0]
-    places, tokens = act_ref.shape[1:3]
+    tokens = chip_ref.shape[1]
+    places = w_ref.shape[1] // 2
     total = None
-    for place in range(places):
-        source = lax.rem(zh + place, places)
-        for core in range(2):
-            act = act_ref[core, place]
+    for core in range(2):
+        near = [chip_ref[core], others_ref[1, core], others_ref[core, 2], others_ref[0, core]]
+        for place, act in enumerate(near):
+            source = lax.rem(zh + place, places)
             w = w_ref[:, source * 2 + core]
             part = jnp.dot(act, w.reshape(-1, w.shape[-1]), preferred_element_type=jnp.float32)
             total = part if total is None else total + part
@@ -174,11 +175,12 @@
     zh = lax.axis_index("zh").astype(jnp.int32).reshape(1)
     own = lax.axis_index("zi").astype(jnp.int32).reshape(1)
 
-    left = shifted(activations, "zh", 1)
-    right = shifted(activations, "zh", -1)
+    slabs = lax.axis_size("zh")
+    turn = [(2 * i + c, 2 * ((i + 1 - 2 * c) % slabs) + c) for i in range(slabs) for c in range(2)]
+    chip = lax.all_gather(activations, "core")
+    near = lax.ppermute(chip, HEADS, turn)
     far = shifted(activations, "zh", 2)
-    near = jnp.stack([activations, right, far, left])
-    acts = lax.all_gather(near, "core")
+    others = lax.all_gather(jnp.concatenate([near, far[None]]), "core")
 
     piece = w_kv.shape[0]
     w = w_kv.reshape(piece, ranks, 2 * width).transpose(1, 0, 2)
@@ -197,11 +199,11 @@
     kv = pl.pallas_call(
         project_kernel,
         out_shape=jax.ShapeDtypeStruct((tokens + SPAN_ROWS, 2 * width), jnp.bfloat16),
-        in_specs=[SMEM, SMEM, VMEM, VMEM],
+        in_specs=[SMEM, SMEM, VMEM, VMEM, VMEM],
         out_specs=VMEM,
         name="project",
         compiler_params=pltpu.CompilerParams(vmem_limit_bytes=12 * 1024 * 1024),
-    )(zh, span_of, acts, w)
+    )(zh, span_of, chip, others, w)
     kv = jnp.stack([kv, shifted(kv, "zo", 1)])
     kv = exchanged(copies(kv, plane), PLANE)
     kv = kv.reshape(side, plane * 2 // side, tokens + SPAN_ROWS, 2 * width)

time: 186 us -> 181 us (0.973)
  waiting for transfers between devices: 41.5 us -> 31.9 us
  blocking collectives: 84.9 us -> 94.5 us
  starting transfers between devices: 46.5 us -> 41 us
    all_gather x1 -> x2, blocking collectives: 2.28 us -> 16.7 us  [the longest x1 14.8 us: body(): others = lax.all_gather(jnp.concatenate([near, far[None]]), 'core')]
    ppermute x7 -> x5, waiting for transfers between devices: 38.1 us -> 24.2 us  [shifted(): lax.ppermute(value, axis, [(i, (i + by) % size) for i in range(size)])]
    ppermute x7 -> x5, starting transfers between devices: 31.8 us -> 23.6 us  [shifted(): lax.ppermute(value, axis, [(i, (i + by) % size) for i in range(size)])]
    all_to_all x3, blocking collectives: 82.7 us -> 77.8 us  [exchanged(): return lax.all_to_all(blocks, axes, 0, 0, tiled=True)]
    all_to_all x2, waiting for transfers between devices: 3.41 us -> 7.7 us  [exchanged(): return lax.all_to_all(blocks, axes, 0, 0, tiled=True)]
    ppermute x0 -> x1, starting transfers between devices: none -> 2.67 us  [body(): near = lax.ppermute(chip, HEADS, turn)]
  transfers between devices with their start and end apart: 9 -> 8, of which waited for: 7 -> 5; matrix products, arithmetic and copies ran while one was open for 0% -> 0% of each run, Pallas kernels for 0% -> 0%
where the time goes in v4:
time: 181 us; the launch traced here: 180 us
  blocking collectives  94.5 us (52%)
  starting transfers between devices  41 us (23%)
  waiting for transfers between devices  31.9 us (18%)
  Pallas kernels  8.66 us (5%)
  local copies, waits for them, and re-layouts  3.66 us (2%)
    all_to_all x3, blocking collectives, exchanged(): return lax.all_to_all(blocks, axes, 0, 0, tiled=True)  77.8 us
    ppermute x5, waiting for transfers between devices, shifted(): lax.ppermute(value, axis, [(i, (i + by) % size) for i in range(size)])  24.2 us
    ppermute x5, starting transfers between devices, shifted(): lax.ppermute(value, axis, [(i, (i + by) % size) for i in range(size)])  23.6 us
    all_gather x1, blocking collectives, body(): others = lax.all_gather(jnp.concatenate([near, far[None]]), 'core')  14.8 us
    all_to_all x2, starting transfers between devices, exchanged(): return lax.all_to_all(blocks, axes, 0, 0, tiled=True)  14.7 us
    all_to_all x2, waiting for transfers between devices, exchanged(): return lax.all_to_all(blocks, axes, 0, 0, tiled=True)  7.7 us
    pallas_call x1, Pallas kernels, body(): pl.pallas_call(lambda *refs: attend_kernel(*refs, scale=1.0 / math.sqrt(w...  6.6 us
  transfers between devices with their start and end apart: 8, of which 5 were waited for; matrix products, arithmetic and copies ran while one was open for 0% of the time, Pallas kernels for 0%

profile of v4, /device:TPU:8, one launch (start us, length us, event | category | flops | bytes accessed | tf_op | source)
XLA Modules:
  0.0 180.0 jit_solution(8415646016219548199)
XLA Ops:
  0.0 0.7 reshape.25
  0.8 50.4 %all_to_all.25 = bf16[8,4,256]{2,1,0:T(4,128)(2,1)S(1)} all-to-all(bf16[8,4,256]{2,1,0:T(4,128)(2,1)S(1)} %bitcast.27), channel_id=1, replica_groups=mesh['zh'=4,'core'=2,'x'=4,'y'=4,'zo'=2,'zi'=4] {'zh','core'}, dimensions={0} | all-to-all | bytes 32768 | tf_op jit(solution)/shard_map/all_to_all | solution.py:28
  51.2 16.7 %all_to_all.26 = bf16[8,8,4,256]{3,2,1,0:T(4,128)(2,1)S(1)} all-to-all(bf16[8,8,4,256]{3,2,1,0:T(4,128)(2,1)S(1)} %broadcast_in_dim.27), channel_id=1, replica_groups=mesh['zh'=4,'core'=2,'x'=4,'y'=4,'zo'=2,'zi'=4] {'zo','zi'}, dimensions={0} | all-to-all | bytes 262144 | tf_op jit(solution)/shard_map/all_to_all | solution.py:28
  67.9 1.6 broadcast_in_dim.29
  69.5 0.0 copy-start.2
  69.5 0.0 copy-start
  69.5 7.5 %all-to-all-start.2 = ((bf16[16,8,32,256]{3,2,1,0:T(8,128)(2,1)}), bf16[16,8,32,256]{3,2,1,0:T(8,128)(2,1)S(1)}, u32[]{:S(2)}, u32[]{:S(2)}) async-start(bf16[16,8,32,256]{3,2,1,0:T(8,128)(2,1)} %broadcast_in_dim.29), calls=%async_computation.2 | async-start | bytes 4194304 | tf_op jit(solution)/shard_map/all_to_all | solution.py:28
  77.1 0.0 copy-done.2
  77.1 1.9 %all-gather = bf16[160,512]{1,0:T(8,128)(2,1)S(1)} all-gather(bf16[80,512]{1,0:T(8,128)(2,1)S(1)} %copy-done.2), channel_id=2, replica_groups=mesh['zh'=4,'core'=2,'x'=4,'y'=4,'zo'=2,'zi'=4] {'core'}, dimensions={0}, use_global_device_ids=true | all-gather | bytes 245760 | tf_op jit(solution)/shard_map/all_gather | solution.py:180
  79.0 2.7 %collective-permute-start.3 = (bf16[2,80,512]{2,1,0:T(8,128)(2,1)S(1)}, bf16[2,80,512]{2,1,0:T(8,128)(2,1)S(1)}, u32[]{:S(2)}, u32[]{:S(2)}) collective-permute-start(bf16[2,80,512]{2,1,0:T(8,128)(2,1)S(1)} %bitcast.20), channel_id=1, source_target_pairs={{0,256},{128,896},{256,512},{384,128},{512,768},{640,384},{768,0},... | collective-permute-start | bytes 491528 | tf_op jit(solution)/shard_map/ppermute | solution.py:181
  81.7 12.1 %collective-permute-start.4 = (bf16[80,512]{1,0:T(8,128)(2,1)S(1)}, bf16[80,512]{1,0:T(8,128)(2,1)S(1)}, u32[]{:S(2)}, u32[]{:S(2)}) collective-permute-start(bf16[80,512]{1,0:T(8,128)(2,1)S(1)} %copy-done.2), channel_id=1, source_target_pairs={{0,512},{256,768},{512,0},{768,256},{1,513},{257,769},{513,1},{769... | collective-permute-start | bytes 245768 | tf_op jit(solution)/shard_map/ppermute | solution.py:24
  93.8 13.4 %collective-permute-done.4 = bf16[80,512]{1,0:T(8,128)(2,1)S(1)} collective-permute-done((bf16[80,512]{1,0:T(8,128)(2,1)S(1)}, bf16[80,512]{1,0:T(8,128)(2,1)S(1)}, u32[]{:S(2)}, u32[]{:S(2)}) %collective-permute-start.4) | collective-permute-done | bytes 81952 | tf_op jit(solution)/shard_map/ppermute | solution.py:24
  107.1 0.0 collective-permute-done.3
  107.2 14.8 %all-gather.1 = bf16[6,80,512]{2,1,0:T(8,128)(2,1)S(1)} all-gather(bf16[3,80,512]{2,1,0:T(8,128)(2,1)S(1)} %pad_maximum_fusion), channel_id=3, replica_groups=mesh['zh'=4,'core'=2,'x'=4,'y'=4,'zo'=2,'zi'=4] {'core'}, dimensions={0}, use_global_device_ids=true | all-gather | bytes 737280 | tf_op jit(solution)/shard_map/all_gather | solution.py:183
  121.9 0.0 all-to-all-done.2.w_ref
  121.9 0.0 copy-done
  121.9 1.0 project.1
  123.0 1.9 %collective-permute-start.5 = (bf16[88,256]{1,0:T(8,128)(2,1)S(1)}, bf16[88,256]{1,0:T(8,128)(2,1)S(1)}, u32[]{:S(2)}, u32[]{:S(2)}) collective-permute-start(bf16[88,256]{1,0:T(8,128)(2,1)S(1)} %project.1), channel_id=1, source_target_pairs={{0,4},{4,0},{1,5},{5,1},{2,6},{6,2},{3,7},{7,3},{8,12},{12,8},{9,1... | collective-permute-start | bytes 135176 | tf_op jit(solution)/shard_map/ppermute | solution.py:24
  124.9 7.9 %collective-permute-done.5 = bf16[88,256]{1,0:T(8,128)(2,1)S(1)} collective-permute-done((bf16[88,256]{1,0:T(8,128)(2,1)S(1)}, bf16[88,256]{1,0:T(8,128)(2,1)S(1)}, u32[]{:S(2)}, u32[]{:S(2)}) %collective-permute-start.5) | collective-permute-done | bytes 45088 | tf_op jit(solution)/shard_map/ppermute | solution.py:24
  132.8 0.0 copy-start.1
  132.8 1.2 broadcast_in_dim.30
  134.0 7.2 %all-to-all-start.3 = ((bf16[16,2,88,256]{3,2,1,0:T(8,128)(2,1)}), bf16[16,2,88,256]{3,2,1,0:T(8,128)(2,1)S(1)}, u32[]{:S(2)}, u32[]{:S(2)}) async-start(bf16[16,2,88,256]{3,2,1,0:T(8,128)(2,1)} %broadcast_in_dim.30), calls=%async_computation.3 | async-start | bytes 2883584 | tf_op jit(solution)/shard_map/all_to_all | solution.py:28
  141.3 0.0 copy-done.1
  141.3 1.9 %collective-permute-start = (bf16[328,128]{1,0:T(8,128)(2,1)S(1)}, bf16[328,128]{1,0:T(8,128)(2,1)S(1)}, u32[]{:S(2)}, u32[]{:S(2)}) collective-permute-start(bf16[328,128]{1,0:T(8,128)(2,1)S(1)} %fusion.1.refs_1_), channel_id=1, source_target_pairs={{0,1},{1,2},{2,3},{3,0},{4,5},{5,6},{6,7},{7,4},{8,9},{9,10},{10,1... | collective-permute-start | bytes 251912 | tf_op jit(solution)/shard_map/ppermute | solution.py:24
  143.2 1.9 %collective-permute-start.1 = (bf16[328,128]{1,0:T(8,128)(2,1)S(1)}, bf16[328,128]{1,0:T(8,128)(2,1)S(1)}, u32[]{:S(2)}, u32[]{:S(2)}) collective-permute-start(bf16[328,128]{1,0:T(8,128)(2,1)S(1)} %fusion.1.refs_1_), channel_id=1, source_target_pairs={{0,2},{1,3},{2,0},{3,1},{4,6},{5,7},{6,4},{7,5},{8,10},{9,11},{10,... | collective-permute-start | bytes 251912 | tf_op jit(solution)/shard_map/ppermute | solution.py:24
  145.2 5.7 %collective-permute-start.2 = (bf16[328,128]{1,0:T(8,128)(2,1)S(1)}, bf16[328,128]{1,0:T(8,128)(2,1)S(1)}, u32[]{:S(2)}, u32[]{:S(2)}) collective-permute-start(bf16[328,128]{1,0:T(8,128)(2,1)S(1)} %fusion.1.refs_1_), channel_id=1, source_target_pairs={{0,3},{1,0},{2,1},{3,2},{4,7},{5,4},{6,5},{7,6},{8,11},{9,8},{10,9... | collective-permute-start | bytes 251912 | tf_op jit(solution)/shard_map/ppermute | solution.py:24
  150.9 0.0 collective-permute-done.refs_2_
  150.9 0.4 collective-permute-done.1.refs_3_
  151.3 2.6 %collective-permute-done.2.refs_4_ = bf16[328,128]{1,0:T(8,128)(2,1)S(1)} collective-permute-done((bf16[328,128]{1,0:T(8,128)(2,1)S(1)}, bf16[328,128]{1,0:T(8,128)(2,1)S(1)}, u32[]{:S(2)}, u32[]{:S(2)}) %collective-permute-start.2) | collective-permute-done | bytes 84000 | tf_op jit(solution)/shard_map/ppermute | solution.py:24
  153.9 7.7 %all-to-all-done.3 = bf16[16,2,88,256]{3,2,1,0:T(8,128)(2,1)S(1)} async-done(((bf16[16,2,88,256]{3,2,1,0:T(8,128)(2,1)}), bf16[16,2,88,256]{3,2,1,0:T(8,128)(2,1)S(1)}, u32[]{:S(2)}, u32[]{:S(2)}) %all-to-all-start.3) | async-done | bytes 1441824 | tf_op jit(solution)/shard_map/all_to_all | solution.py:28
  161.6 6.6 %attend.1 = bf16[4,336,128]{2,1,0:T(8,128)(2,1)S(1)} custom-call(s32[1]{0:T(128)} %bitcast.refs_0_, bf16[328,128]{1,0:T(8,128)(2,1)S(1)} %fusion.1.refs_1_, bf16[328,128]{1,0:T(8,128)(2,1)S(1)} %collective-permute-done.refs_2_, bf16[328,128]{1,0:T(8,128)(2,1)S(1)} %collective-permute-done.1.refs_3_, bf16[328,128]{1,0:T(8,128)(2,1)S(1)} %collective-permute-done.2.refs_4_, ...), custom_call_target="tpu_custom_call" | custom-call | tf_op jit(solution)/shard_map/attend/pallas_call | solution.py:212
  168.2 10.7 %all_to_all.27.refs_0_ = bf16[4,336,128]{2,1,0:T(8,128)(2,1)S(1)} all-to-all(bf16[4,336,128]{2,1,0:T(8,128)(2,1)S(1)} %attend.1), channel_id=1, replica_groups=mesh['zh'=4,'core'=2,'x'=4,'y'=4,'zo'=2,'zi'=4] {'zi'}, dimensions={0} | all-to-all | bytes 688128 | tf_op jit(solution)/shard_map/all_to_all | solution.py:28
  178.9 1.0 combine.1
  (9 shorter events, 0.1 us)
Async XLA Ops:
  69.5 7.5 %copy-start.2 = (bf16[80,512]{1,0:T(8,128)(2,1)S(1)}, bf16[80,512]{1,0:T(8,128)(2,1)}, u32[]{:S(2)}) copy-start(bf16[80,512]{1,0:T(8,128)(2,1)} %param.4) | copy-start | bytes 245764
  69.5 52.4 %copy-start = (s32[2]{0:T(128)S(1)}, s32[2]{0:T(128)}, u32[]{:S(2)}) copy-start(s32[2]{0:T(128)} %span_ref.1) | copy-start | bytes 28
  69.5 52.4 %all-to-all-start.2 = ((bf16[16,8,32,256]{3,2,1,0:T(8,128)(2,1)}), bf16[16,8,32,256]{3,2,1,0:T(8,128)(2,1)S(1)}, u32[]{:S(2)}, u32[]{:S(2)}) async-start(bf16[16,8,32,256]{3,2,1,0:T(8,128)(2,1)} %broadcast_in_dim.29), calls=%async_computation.2 | async-start | bytes 4194304 | tf_op jit(solution)/shard_map/all_to_all | solution.py:28
  79.0 28.1 %collective-permute-start.3 = (bf16[2,80,512]{2,1,0:T(8,128)(2,1)S(1)}, bf16[2,80,512]{2,1,0:T(8,128)(2,1)S(1)}, u32[]{:S(2)}, u32[]{:S(2)}) collective-permute-start(bf16[2,80,512]{2,1,0:T(8,128)(2,1)S(1)} %bitcast.20), channel_id=1, source_target_pairs={{0,256},{128,896},{256,512},{384,128},{512,768},{640,384},{768,0},... | collective-permute-start | bytes 491528 | tf_op jit(solution)/shard_map/ppermute | solution.py:181
  81.7 25.5 %collective-permute-start.4 = (bf16[80,512]{1,0:T(8,128)(2,1)S(1)}, bf16[80,512]{1,0:T(8,128)(2,1)S(1)}, u32[]{:S(2)}, u32[]{:S(2)}) collective-permute-start(bf16[80,512]{1,0:T(8,128)(2,1)S(1)} %copy-done.2), channel_id=1, source_target_pairs={{0,512},{256,768},{512,0},{768,256},{1,513},{257,769},{513,1},{769... | collective-permute-start | bytes 245768 | tf_op jit(solution)/shard_map/ppermute | solution.py:24
  123.0 9.8 %collective-permute-start.5 = (bf16[88,256]{1,0:T(8,128)(2,1)S(1)}, bf16[88,256]{1,0:T(8,128)(2,1)S(1)}, u32[]{:S(2)}, u32[]{:S(2)}) collective-permute-start(bf16[88,256]{1,0:T(8,128)(2,1)S(1)} %project.1), channel_id=1, source_target_pairs={{0,4},{4,0},{1,5},{5,1},{2,6},{6,2},{3,7},{7,3},{8,12},{12,8},{9,1... | collective-permute-start | bytes 135176 | tf_op jit(solution)/shard_map/ppermute | solution.py:24
  132.8 8.5 %copy-start.1 = (bf16[80,4,128]{2,1,0:T(4,128)(2,1)S(1)}, bf16[80,4,128]{2,1,0:T(4,128)(2,1)}, u32[]{:S(2)}) copy-start(bf16[80,4,128]{2,1,0:T(4,128)(2,1)} %param.5) | copy-start | bytes 245764
  134.0 27.5 %all-to-all-start.3 = ((bf16[16,2,88,256]{3,2,1,0:T(8,128)(2,1)}), bf16[16,2,88,256]{3,2,1,0:T(8,128)(2,1)S(1)}, u32[]{:S(2)}, u32[]{:S(2)}) async-start(bf16[16,2,88,256]{3,2,1,0:T(8,128)(2,1)} %broadcast_in_dim.30), calls=%async_computation.3 | async-start | bytes 2883584 | tf_op jit(solution)/shard_map/all_to_all | solution.py:28
  141.3 9.6 %collective-permute-start = (bf16[328,128]{1,0:T(8,128)(2,1)S(1)}, bf16[328,128]{1,0:T(8,128)(2,1)S(1)}, u32[]{:S(2)}, u32[]{:S(2)}) collective-permute-start(bf16[328,128]{1,0:T(8,128)(2,1)S(1)} %fusion.1.refs_1_), channel_id=1, source_target_pairs={{0,1},{1,2},{2,3},{3,0},{4,5},{5,6},{6,7},{7,4},{8,9},{9,10},{10,1... | collective-permute-start | bytes 251912 | tf_op jit(solution)/shard_map/ppermute | solution.py:24
  143.2 8.0 %collective-permute-start.1 = (bf16[328,128]{1,0:T(8,128)(2,1)S(1)}, bf16[328,128]{1,0:T(8,128)(2,1)S(1)}, u32[]{:S(2)}, u32[]{:S(2)}) collective-permute-start(bf16[328,128]{1,0:T(8,128)(2,1)S(1)} %fusion.1.refs_1_), channel_id=1, source_target_pairs={{0,2},{1,3},{2,0},{3,1},{4,6},{5,7},{6,4},{7,5},{8,10},{9,11},{10,... | collective-permute-start | bytes 251912 | tf_op jit(solution)/shard_map/ppermute | solution.py:24
  145.2 8.7 %collective-permute-start.2 = (bf16[328,128]{1,0:T(8,128)(2,1)S(1)}, bf16[328,128]{1,0:T(8,128)(2,1)S(1)}, u32[]{:S(2)}, u32[]{:S(2)}) collective-permute-start(bf16[328,128]{1,0:T(8,128)(2,1)S(1)} %fusion.1.refs_1_), channel_id=1, source_target_pairs={{0,3},{1,0},{2,1},{3,2},{4,7},{5,4},{6,5},{7,6},{8,11},{9,8},{10,9... | collective-permute-start | bytes 251912 | tf_op jit(solution)/shard_map/ppermute | solution.py:24

commit v5 on v4

--- a/solution.py
+++ b/solution.py
@@ -55,21 +55,49 @@
     out_ref[tokens:, :] = span_rows(span_ref[0], span_ref[1], (SPAN_ROWS, total.shape[1]))
 
 
-def attend_kernel(own_ref, q0_ref, q1_ref, q2_ref, q3_ref, kv_ref, out_ref, stat_ref, pos_ref, q_ref, *, scale):
-    for place, source_ref in enumerate((q0_ref, q1_ref, q2_ref, q3_ref)):
-        q_ref[place] = source_ref[...]
-    own = own_ref[0]
-    blocks, _, width = q_ref.shape
+def column_of(table, lane, place):
+    return jnp.sum(jnp.where(lane == place, table, 0.0), axis=1, keepdims=True)
+
+
+def attend_block(query, query_pos, kv_ref, pos_ref, top, total, mixed, factor):
+    chunks, peers = kv_ref.shape[:2]
+    width = query.shape[1]
+    tokens = kv_ref.shape[2] - SPAN_ROWS
+    count = peers * tokens
+    scores = []
+    first = top
+    for chunk in range(chunks):
+        keys = kv_ref[chunk, :, :tokens, :width].reshape(count, width)
+        score = lax.dot_general(
+            query, keys, (((1,), (1,)), ((), ())), preferred_element_type=jnp.float32
+        )
+        score = jnp.where(pos_ref[chunk : chunk + 1, :] <= query_pos, score, HIDDEN)
+        top = jnp.maximum(top, jnp.max(score, axis=1, keepdims=True))
+        scores.append(score)
+    if total is None:
+        total = jnp.zeros(top.shape, jnp.float32)
+        mixed = jnp.zeros(query.shape, jnp.float32)
+    else:
+        kept = jnp.exp2((first - top) * factor)
+        total = total * kept
+        mixed = mixed * kept
+    for chunk in range(chunks):
+        values = kv_ref[chunk, :, :tokens, width:].reshape(count, width)
+        weight = jnp.exp2((scores[chunk] - top) * factor)
+        total = total + jnp.sum(weight, axis=1, keepdims=True)
+        mixed = mixed + jnp.dot(
+            weight.astype(jnp.bfloat16), values, preferred_element_type=jnp.float32
+        )
+    return top, total, mixed
+
+
+def fill_positions(kv_ref, pos_ref):
     chunks, peers = kv_ref.shape[:2]
     tokens = kv_ref.shape[2] - SPAN_ROWS
-    rows = q_ref.shape[1] - SPAN_ROWS
     half = tokens // 2
     count = peers * tokens
-    factor = scale * math.log2(math.e)
-
     lane = lax.broadcasted_iota(jnp.int32, (peers, count), 1)
-    start = lax.broadcasted_iota(jnp.int32, (peers, count), 0) * tokens
-    inside = lane - start
+    inside = lane - lax.broadcasted_iota(jnp.int32, (peers, count), 0) * tokens
     early = (inside >= 0) & (inside < half)
     late = (inside >= half) & (inside < tokens)
     for chunk in range(chunks):
@@ -79,40 +107,67 @@
         place = place + jnp.where(early | late, inside.astype(jnp.float32), 0.0)
         pos_ref[chunk : chunk + 1, :] = jnp.sum(place, axis=0, keepdims=True)
 
+
+def query_positions(q_ref, block, rows, tokens):
+    half = tokens // 2
     row = lax.broadcasted_iota(jnp.int32, (tokens, 1), 0).astype(jnp.float32)
-    column = lax.broadcasted_iota(jnp.int32, (rows, 128), 1)
+    spans = q_ref[block, rows : rows + SPAN_ROWS, :].astype(jnp.float32) * half
+    query_pos = jnp.where(row < half, spans[0:1, 0:1], spans[0:1, 1:2] - half) + row
+    return jnp.concatenate([query_pos] * (rows // tokens), axis=0)
+
+
+def begin_kernel(q0_ref, q1_ref, q2_ref, q3_ref, kv_ref, mixed_ref, state_ref, pos_ref, q_ref, *, scale):
+    for place, source_ref in enumerate((q0_ref, q1_ref, q2_ref, q3_ref)):
+        q_ref[place] = source_ref[...]
+    blocks = q_ref.shape[0]
+    rows = q_ref.shape[1] - SPAN_ROWS
+    factor = scale * math.log2(math.e)
+    fill_positions(kv_ref, pos_ref)
+    lane = lax.broadcasted_iota(jnp.int32, (rows, 128), 1)
+    state_ref[...] = jnp.zeros(state_ref.shape, jnp.float32)
+
+    def step(block, carry):
+        query_pos = query_positions(q_ref, block, rows, kv_ref.shape[2] - SPAN_ROWS)
+        top = jnp.full((rows, 1), FLOOR, jnp.float32)
+        query = q_ref[block, :rows, :]
+        top, total, mixed = attend_block(query, query_pos, kv_ref, pos_ref, top, None, None, factor)
+        mixed_ref[block] = mixed
+        state = jnp.where(lane == block, top, state_ref[...])
+        state_ref[...] = jnp.where(lane == block + 8, total, state)
+        return carry
+
+    lax.fori_loop(0, blocks, step, 0)
+
+
+def finish_kernel(
+    own_ref, q0_ref, q1_ref, q2_ref, q3_ref, kv_ref, mixed_ref, state_ref,
+    out_ref, stat_ref, pos_ref, q_ref, *, scale
+):
+    for place, source_ref in enumerate((q0_ref, q1_ref, q2_ref, q3_ref)):
+        q_ref[place] = source_ref[...]
+    own = own_ref[0]
+    blocks = q_ref.shape[0]
+    rows = q_ref.shape[1] - SPAN_ROWS
+    factor = scale * math.log2(math.e)
+    fill_positions(kv_ref, pos_ref)
+    lane = lax.broadcasted_iota(jnp.int32, (rows, 128), 1)
     stat_ref[...] = jnp.zeros(stat_ref.shape, jnp.float32)
 
     def step(block, carry):
         owner = lax.rem(own + blocks - block, blocks)
-        spans = q_ref[block, rows : rows + SPAN_ROWS, :].astype(jnp.float32) * half
-        query_pos = jnp.where(row < half, spans[0:1, 0:1], spans[0:1, 1:2] - half) + row
-        query_pos = jnp.concatenate([query_pos] * (rows // tokens), axis=0)
+        query_pos = query_positions(q_ref, block, rows, kv_ref.shape[2] - SPAN_ROWS)
+        state = state_ref[...]
+        top = column_of(state, lane, block)
+        total = column_of(state, lane, block + 8)
         query = q_ref[block, :rows, :]
-        scores = []
-        top = jnp.full((rows, 1), FLOOR, jnp.float32)
-        for chunk in range(chunks):
-            keys = kv_ref[chunk, :, :tokens, :width].reshape(count, width)
-            score = lax.dot_general(
-                query, keys, (((1,), (1,)), ((), ())), preferred_element_type=jnp.float32
-            )
-            score = jnp.where(pos_ref[chunk : chunk + 1, :] <= query_pos, score, HIDDEN)
-            top = jnp.maximum(top, jnp.max(score, axis=1, keepdims=True))
-            scores.append(score)
-        total = jnp.zeros((rows, 1), jnp.float32)
-        mixed = jnp.zeros((rows, width), jnp.float32)
-        for chunk in range(chunks):
-            values = kv_ref[chunk, :, :tokens, width:].reshape(count, width)
-            weight = jnp.exp2((scores[chunk] - top) * factor)
-            total = total + jnp.sum(weight, axis=1, keepdims=True)
-            mixed = mixed + jnp.dot(
-                weight.astype(jnp.bfloat16), values, preferred_element_type=jnp.float32
-            )
+        top, total, mixed = attend_block(
+            query, query_pos, kv_ref, pos_ref, top, total, mixed_ref[block], factor
+        )
         seen = total > 0.0
         safe = jnp.where(seen, total, 1.0)
         out_ref[owner, :rows, :] = (mixed / safe).astype(jnp.bfloat16)
         size = jnp.where(seen, top * factor + jnp.log2(safe), HIDDEN)
-        stat_ref[:rows, :] = jnp.where(column == owner, size, stat_ref[:rows, :])
+        stat_ref[:rows, :] = jnp.where(lane == owner, size, stat_ref[:rows, :])
         return carry
 
     lax.fori_loop(0, blocks, step, 0)
@@ -204,24 +259,37 @@
         name="project",
         compiler_params=pltpu.CompilerParams(vmem_limit_bytes=12 * 1024 * 1024),
     )(zh, span_of, chip, others, w)
-    kv = jnp.stack([kv, shifted(kv, "zo", 1)])
-    kv = exchanged(copies(kv, plane), PLANE)
-    kv = kv.reshape(side, plane * 2 // side, tokens + SPAN_ROWS, 2 * width)
+    sets = (2, plane // 2, tokens + SPAN_ROWS, 2 * width)
+    other = shifted(kv, "zo", 1)
+    first = exchanged(copies(kv, plane), PLANE).reshape(sets)
+    spread = copies(other, plane)
+    second = exchanged(spread, PLANE).reshape(sets)
 
     padded = (rows + 127) // 128 * 128
+    scale = 1.0 / math.sqrt(width)
+    positions = pltpu.VMEM((8, plane // 2 * tokens), jnp.float32)
+    held = pltpu.VMEM((side, rows + SPAN_ROWS, width), jnp.bfloat16)
+    mixed, state = pl.pallas_call(
+        lambda *refs: begin_kernel(*refs, scale=scale),
+        out_shape=(
+            jax.ShapeDtypeStruct((side, rows, width), jnp.float32),
+            jax.ShapeDtypeStruct((rows, 128), jnp.float32),
+        ),
+        in_specs=[VMEM] * 5,
+        out_specs=(VMEM, VMEM),
+        scratch_shapes=[positions, held],
+        name="begin",
+        compiler_params=pltpu.CompilerParams(vmem_limit_bytes=16 * 1024 * 1024),
+    )(q, *moved, first)
     mixed = pl.pallas_call(
-        lambda *refs: attend_kernel(*refs, scale=1.0 / math.sqrt(width)),
+        lambda *refs: finish_kernel(*refs, scale=scale),
         out_shape=jax.ShapeDtypeStruct((side, rows + STAT_ROWS, width), jnp.bfloat16),
-        in_specs=[SMEM] + [VMEM] * 5,
+        in_specs=[SMEM] + [VMEM] * 7,
         out_specs=VMEM,
-        scratch_shapes=[
-            pltpu.VMEM((padded, 128), jnp.float32),
-            pltpu.VMEM((8, plane * 2 // side * tokens), jnp.float32),
-            pltpu.VMEM((side, rows + SPAN_ROWS, width), jnp.bfloat16),
-        ],
-        name="attend",
-        compiler_params=pltpu.CompilerParams(vmem_limit_bytes=20 * 1024 * 1024),
-    )(own, q, *moved, kv)
+        scratch_shapes=[pltpu.VMEM((padded, 128), jnp.float32), positions, held],
+        name="finish",
+        compiler_params=pltpu.CompilerParams(vmem_limit_bytes=16 * 1024 * 1024),
+    )(own, q, *moved, second, mixed, state)
     mixed = exchanged(mixed, "zi")
     return pl.pallas_call(
         lambda *refs: combine_kernel(*refs, rows=rows),

time: 181 us -> 184 us (1.017)
  the two profiles are of different devices: /device:TPU:8 before, /device:TPU:2 now
where the time goes in v5:
time: 184 us; the launch traced here: 183 us
  blocking collectives  95.4 us (52%)
  starting transfers between devices  45.3 us (25%)
  waiting for transfers between devices  28.1 us (15%)
  Pallas kernels  10.1 us (5%)
  local copies, waits for them, and re-layouts  4.28 us (2%)
    all_to_all x3, blocking collectives, exchanged(): return lax.all_to_all(blocks, axes, 0, 0, tiled=True)  78.7 us
    ppermute x5, waiting for transfers between devices, shifted(): lax.ppermute(value, axis, [(i, (i + by) % size) for i in range(size)])  26 us
    ppermute x5, starting transfers between devices, shifted(): lax.ppermute(value, axis, [(i, (i + by) % size) for i in range(size)])  21.8 us
    all_to_all x3, starting transfers between devices, exchanged(): return lax.all_to_all(blocks, axes, 0, 0, tiled=True)  20.8 us
    all_gather x1, blocking collectives, body(): others = lax.all_gather(jnp.concatenate([near, far[None]]), 'core')  14.8 us
    pallas_call x1, Pallas kernels, body(): pl.pallas_call(lambda *refs: finish_kernel(*refs, scale=scale), out_shape...  4.17 us
    pallas_call x1, Pallas kernels, body(): pl.pallas_call(lambda *refs: begin_kernel(*refs, scale=scale), out_shape=...  3.85 us
  transfers between devices with their start and end apart: 9, of which 5 were waited for; matrix products, arithmetic and copies ran while one was open for 0% of the time, Pallas kernels for 2%

profile of v5, /device:TPU:2, one launch (start us, length us, event | category | flops | bytes accessed | tf_op | source)
XLA Modules:
  0.0 183.3 jit_solution(6923229723606946431)
XLA Ops:
  0.0 0.7 reshape.30
  0.8 50.4 %all_to_all.30 = bf16[8,4,256]{2,1,0:T(4,128)(2,1)S(1)} all-to-all(bf16[8,4,256]{2,1,0:T(4,128)(2,1)S(1)} %bitcast.26), channel_id=1, replica_groups=mesh['zh'=4,'core'=2,'x'=4,'y'=4,'zo'=2,'zi'=4] {'zh','core'}, dimensions={0} | all-to-all | bytes 32768 | tf_op jit(solution)/shard_map/all_to_all | solution.py:28
  51.2 16.7 %all_to_all.31 = bf16[8,8,4,256]{3,2,1,0:T(4,128)(2,1)S(1)} all-to-all(bf16[8,8,4,256]{3,2,1,0:T(4,128)(2,1)S(1)} %broadcast_in_dim.16), channel_id=1, replica_groups=mesh['zh'=4,'core'=2,'x'=4,'y'=4,'zo'=2,'zi'=4] {'zo','zi'}, dimensions={0} | all-to-all | bytes 262144 | tf_op jit(solution)/shard_map/all_to_all | solution.py:28
  67.9 1.6 broadcast_in_dim.35
  69.5 0.0 copy-start.2
  69.5 0.0 copy-start
  69.5 7.6 %all-to-all-start.2 = ((bf16[16,8,32,256]{3,2,1,0:T(8,128)(2,1)}), bf16[16,8,32,256]{3,2,1,0:T(8,128)(2,1)S(1)}, u32[]{:S(2)}, u32[]{:S(2)}) async-start(bf16[16,8,32,256]{3,2,1,0:T(8,128)(2,1)} %broadcast_in_dim.35), calls=%async_computation.2 | async-start | bytes 4194304 | tf_op jit(solution)/shard_map/all_to_all | solution.py:28
  77.1 0.0 copy-done.2
  77.2 1.9 %all-gather = bf16[160,512]{1,0:T(8,128)(2,1)S(1)} all-gather(bf16[80,512]{1,0:T(8,128)(2,1)S(1)} %copy-done.2), channel_id=2, replica_groups=mesh['zh'=4,'core'=2,'x'=4,'y'=4,'zo'=2,'zi'=4] {'core'}, dimensions={0}, use_global_device_ids=true | all-gather | bytes 245760 | tf_op jit(solution)/shard_map/all_gather | solution.py:235
  79.1 2.7 %collective-permute-start.3 = (bf16[2,80,512]{2,1,0:T(8,128)(2,1)S(1)}, bf16[2,80,512]{2,1,0:T(8,128)(2,1)S(1)}, u32[]{:S(2)}, u32[]{:S(2)}) collective-permute-start(bf16[2,80,512]{2,1,0:T(8,128)(2,1)S(1)} %bitcast.20), channel_id=1, source_target_pairs={{0,256},{128,896},{256,512},{384,128},{512,768},{640,384},{768,0},... | collective-permute-start | bytes 491528 | tf_op jit(solution)/shard_map/ppermute | solution.py:236
  81.8 12.1 %collective-permute-start.4 = (bf16[80,512]{1,0:T(8,128)(2,1)S(1)}, bf16[80,512]{1,0:T(8,128)(2,1)S(1)}, u32[]{:S(2)}, u32[]{:S(2)}) collective-permute-start(bf16[80,512]{1,0:T(8,128)(2,1)S(1)} %copy-done.2), channel_id=1, source_target_pairs={{0,512},{256,768},{512,0},{768,256},{1,513},{257,769},{513,1},{769... | collective-permute-start | bytes 245768 | tf_op jit(solution)/shard_map/ppermute | solution.py:24
  93.9 13.4 %collective-permute-done.4 = bf16[80,512]{1,0:T(8,128)(2,1)S(1)} collective-permute-done((bf16[80,512]{1,0:T(8,128)(2,1)S(1)}, bf16[80,512]{1,0:T(8,128)(2,1)S(1)}, u32[]{:S(2)}, u32[]{:S(2)}) %collective-permute-start.4) | collective-permute-done | bytes 81952 | tf_op jit(solution)/shard_map/ppermute | solution.py:24
  107.2 0.0 collective-permute-done.3
  107.2 14.8 %all-gather.1 = bf16[6,80,512]{2,1,0:T(8,128)(2,1)S(1)} all-gather(bf16[3,80,512]{2,1,0:T(8,128)(2,1)S(1)} %pad_maximum_fusion), channel_id=3, replica_groups=mesh['zh'=4,'core'=2,'x'=4,'y'=4,'zo'=2,'zi'=4] {'core'}, dimensions={0}, use_global_device_ids=true | all-gather | bytes 737280 | tf_op jit(solution)/shard_map/all_gather | solution.py:238
  122.0 0.0 all-to-all-done.2.w_ref
  122.0 0.0 copy-done
  122.0 1.0 project.1
  123.0 0.0 copy-start.1
  123.1 0.9 broadcast_in_dim.37
  124.0 7.2 %all-to-all-start.4 = ((bf16[16,88,256]{2,1,0:T(8,128)(2,1)}), bf16[16,88,256]{2,1,0:T(8,128)(2,1)S(1)}, u32[]{:S(2)}, u32[]{:S(2)}) async-start(bf16[16,88,256]{2,1,0:T(8,128)(2,1)} %broadcast_in_dim.37), calls=%async_computation.4 | async-start | bytes 1441792 | tf_op jit(solution)/shard_map/all_to_all | solution.py:28
  131.2 1.9 %collective-permute-start.5 = (bf16[88,256]{1,0:T(8,128)(2,1)S(1)}, bf16[88,256]{1,0:T(8,128)(2,1)S(1)}, u32[]{:S(2)}, u32[]{:S(2)}) collective-permute-start(bf16[88,256]{1,0:T(8,128)(2,1)S(1)} %project.1), channel_id=1, source_target_pairs={{0,4},{4,0},{1,5},{5,1},{2,6},{6,2},{3,7},{7,3},{8,12},{12,8},{9,1... | collective-permute-start | bytes 135176 | tf_op jit(solution)/shard_map/ppermute | solution.py:24
  133.1 7.9 %collective-permute-done.5 = bf16[88,256]{1,0:T(8,128)(2,1)S(1)} collective-permute-done((bf16[88,256]{1,0:T(8,128)(2,1)S(1)}, bf16[88,256]{1,0:T(8,128)(2,1)S(1)}, u32[]{:S(2)}, u32[]{:S(2)}) %collective-permute-start.5) | collective-permute-done | bytes 45088 | tf_op jit(solution)/shard_map/ppermute | solution.py:24
  141.0 2.0 %all-to-all-done.4 = bf16[16,88,256]{2,1,0:T(8,128)(2,1)S(1)} async-done(((bf16[16,88,256]{2,1,0:T(8,128)(2,1)}), bf16[16,88,256]{2,1,0:T(8,128)(2,1)S(1)}, u32[]{:S(2)}, u32[]{:S(2)}) %all-to-all-start.4) | async-done | bytes 720928 | tf_op jit(solution)/shard_map/all_to_all | solution.py:28
  143.1 0.9 broadcast_in_dim.36
  144.0 6.0 %all-to-all-start.3 = ((bf16[16,88,256]{2,1,0:T(8,128)(2,1)}), bf16[16,88,256]{2,1,0:T(8,128)(2,1)S(1)}, u32[]{:S(2)}, u32[]{:S(2)}) async-start(bf16[16,88,256]{2,1,0:T(8,128)(2,1)} %broadcast_in_dim.36), calls=%async_computation.3 | async-start | bytes 1441792 | tf_op jit(solution)/shard_map/all_to_all | solution.py:28
  150.0 0.0 copy-done.1
  150.1 1.9 %collective-permute-start.2 = (bf16[328,128]{1,0:T(8,128)(2,1)S(1)}, bf16[328,128]{1,0:T(8,128)(2,1)S(1)}, u32[]{:S(2)}, u32[]{:S(2)}) collective-permute-start(bf16[328,128]{1,0:T(8,128)(2,1)S(1)} %fusion.1.refs_0_.refs_1_), channel_id=1, source_target_pairs={{0,3},{1,0},{2,1},{3,2},{4,7},{5,4},{6,5},{7,6},{8,11},{9,8},{10,9... | collective-permute-start | bytes 251912 | tf_op jit(solution)/shard_map/ppermute | solution.py:24
  152.0 1.9 %collective-permute-start.1 = (bf16[328,128]{1,0:T(8,128)(2,1)S(1)}, bf16[328,128]{1,0:T(8,128)(2,1)S(1)}, u32[]{:S(2)}, u32[]{:S(2)}) collective-permute-start(bf16[328,128]{1,0:T(8,128)(2,1)S(1)} %fusion.1.refs_0_.refs_1_), channel_id=1, source_target_pairs={{0,2},{1,3},{2,0},{3,1},{4,6},{5,7},{6,4},{7,5},{8,10},{9,11},{10,... | collective-permute-start | bytes 251912 | tf_op jit(solution)/shard_map/ppermute | solution.py:24
  153.9 3.9 %collective-permute-start = (bf16[328,128]{1,0:T(8,128)(2,1)S(1)}, bf16[328,128]{1,0:T(8,128)(2,1)S(1)}, u32[]{:S(2)}, u32[]{:S(2)}) collective-permute-start(bf16[328,128]{1,0:T(8,128)(2,1)S(1)} %fusion.1.refs_0_.refs_1_), channel_id=1, source_target_pairs={{0,1},{1,2},{2,3},{3,0},{4,5},{5,6},{6,7},{7,4},{8,9},{9,10},{10,1... | collective-permute-start | bytes 251912 | tf_op jit(solution)/shard_map/ppermute | solution.py:24
  157.8 0.0 collective-permute-done.2.refs_3_.refs_4_
  157.9 3.2 %collective-permute-done.1.refs_2_.refs_3_ = bf16[328,128]{1,0:T(8,128)(2,1)S(1)} collective-permute-done((bf16[328,128]{1,0:T(8,128)(2,1)S(1)}, bf16[328,128]{1,0:T(8,128)(2,1)S(1)}, u32[]{:S(2)}, u32[]{:S(2)}) %collective-permute-start.1) | collective-permute-done | bytes 84000 | tf_op jit(solution)/shard_map/ppermute | solution.py:24
  161.0 1.6 collective-permute-done.refs_1_.refs_2_
  162.6 3.9 %begin.1 = (f32[4,320,128]{2,1,0:T(8,128)S(1)}, f32[320,128]{1,0:T(8,128)S(1)}) custom-call(bf16[328,128]{1,0:T(8,128)(2,1)S(1)} %fusion.1.refs_0_.refs_1_, bf16[328,128]{1,0:T(8,128)(2,1)S(1)} %collective-permute-done.refs_1_.refs_2_, bf16[328,128]{1,0:T(8,128)(2,1)S(1)} %collective-permute-done.1.refs_2_.refs_3_, ...), custom_call_target="tpu_custom_call" | custom-call | tf_op jit(solution)/shard_map/begin/pallas_call | solution.py:272
  166.5 0.0 all-to-all-done.3
  166.5 4.2 %finish.1 = bf16[4,336,128]{2,1,0:T(8,128)(2,1)S(1)} custom-call(s32[1]{0:T(128)} %bitcast.refs_0_, bf16[328,128]{1,0:T(8,128)(2,1)S(1)} %fusion.1.refs_0_.refs_1_, bf16[328,128]{1,0:T(8,128)(2,1)S(1)} %collective-permute-done.refs_1_.refs_2_, bf16[328,128]{1,0:T(8,128)(2,1)S(1)} %collective-permute-done.1.refs_2_.refs_3_, ...), custom_call_target="tpu_custom_call" | custom-call | tf_op jit(solution)/shard_map/finish/pallas_call | solution.py:284
  170.7 11.6 %all_to_all.32.refs_0_ = bf16[4,336,128]{2,1,0:T(8,128)(2,1)S(1)} all-to-all(bf16[4,336,128]{2,1,0:T(8,128)(2,1)S(1)} %finish.1), channel_id=1, replica_groups=mesh['zh'=4,'core'=2,'x'=4,'y'=4,'zo'=2,'zi'=4] {'zi'}, dimensions={0} | all-to-all | bytes 688128 | tf_op jit(solution)/shard_map/all_to_all | solution.py:28
  182.2 1.0 combine.1
  (8 shorter events, 0.1 us)
Async XLA Ops:
  69.5 7.6 %copy-start.2 = (bf16[80,512]{1,0:T(8,128)(2,1)S(1)}, bf16[80,512]{1,0:T(8,128)(2,1)}, u32[]{:S(2)}) copy-start(bf16[80,512]{1,0:T(8,128)(2,1)} %param.4) | copy-start | bytes 245764
  69.5 52.5 %copy-start = (s32[2]{0:T(128)S(1)}, s32[2]{0:T(128)}, u32[]{:S(2)}) copy-start(s32[2]{0:T(128)} %span_ref.1) | copy-start | bytes 28
  69.5 52.5 %all-to-all-start.2 = ((bf16[16,8,32,256]{3,2,1,0:T(8,128)(2,1)}), bf16[16,8,32,256]{3,2,1,0:T(8,128)(2,1)S(1)}, u32[]{:S(2)}, u32[]{:S(2)}) async-start(bf16[16,8,32,256]{3,2,1,0:T(8,128)(2,1)} %broadcast_in_dim.35), calls=%async_computation.2 | async-start | bytes 4194304 | tf_op jit(solution)/shard_map/all_to_all | solution.py:28
  79.1 28.1 %collective-permute-start.3 = (bf16[2,80,512]{2,1,0:T(8,128)(2,1)S(1)}, bf16[2,80,512]{2,1,0:T(8,128)(2,1)S(1)}, u32[]{:S(2)}, u32[]{:S(2)}) collective-permute-start(bf16[2,80,512]{2,1,0:T(8,128)(2,1)S(1)} %bitcast.20), channel_id=1, source_target_pairs={{0,256},{128,896},{256,512},{384,128},{512,768},{640,384},{768,0},... | collective-permute-start | bytes 491528 | tf_op jit(solution)/shard_map/ppermute | solution.py:236
  81.8 25.5 %collective-permute-start.4 = (bf16[80,512]{1,0:T(8,128)(2,1)S(1)}, bf16[80,512]{1,0:T(8,128)(2,1)S(1)}, u32[]{:S(2)}, u32[]{:S(2)}) collective-permute-start(bf16[80,512]{1,0:T(8,128)(2,1)S(1)} %copy-done.2), channel_id=1, source_target_pairs={{0,512},{256,768},{512,0},{768,256},{1,513},{257,769},{513,1},{769... | collective-permute-start | bytes 245768 | tf_op jit(solution)/shard_map/ppermute | solution.py:24
  123.0 27.0 %copy-start.1 = (bf16[80,4,128]{2,1,0:T(4,128)(2,1)S(1)}, bf16[80,4,128]{2,1,0:T(4,128)(2,1)}, u32[]{:S(2)}) copy-start(bf16[80,4,128]{2,1,0:T(4,128)(2,1)} %param.5) | copy-start | bytes 245764
  124.0 19.1 %all-to-all-start.4 = ((bf16[16,88,256]{2,1,0:T(8,128)(2,1)}), bf16[16,88,256]{2,1,0:T(8,128)(2,1)S(1)}, u32[]{:S(2)}, u32[]{:S(2)}) async-start(bf16[16,88,256]{2,1,0:T(8,128)(2,1)} %broadcast_in_dim.37), calls=%async_computation.4 | async-start | bytes 1441792 | tf_op jit(solution)/shard_map/all_to_all | solution.py:28
  131.2 9.8 %collective-permute-start.5 = (bf16[88,256]{1,0:T(8,128)(2,1)S(1)}, bf16[88,256]{1,0:T(8,128)(2,1)S(1)}, u32[]{:S(2)}, u32[]{:S(2)}) collective-permute-start(bf16[88,256]{1,0:T(8,128)(2,1)S(1)} %project.1), channel_id=1, source_target_pairs={{0,4},{4,0},{1,5},{5,1},{2,6},{6,2},{3,7},{7,3},{8,12},{12,8},{9,1... | collective-permute-start | bytes 135176 | tf_op jit(solution)/shard_map/ppermute | solution.py:24
  144.0 22.5 %all-to-all-start.3 = ((bf16[16,88,256]{2,1,0:T(8,128)(2,1)}), bf16[16,88,256]{2,1,0:T(8,128)(2,1)S(1)}, u32[]{:S(2)}, u32[]{:S(2)}) async-start(bf16[16,88,256]{2,1,0:T(8,128)(2,1)} %broadcast_in_dim.36), calls=%async_computation.3 | async-start | bytes 1441792 | tf_op jit(solution)/shard_map/all_to_all | solution.py:28
  150.1 7.8 %collective-permute-start.2 = (bf16[328,128]{1,0:T(8,128)(2,1)S(1)}, bf16[328,128]{1,0:T(8,128)(2,1)S(1)}, u32[]{:S(2)}, u32[]{:S(2)}) collective-permute-start(bf16[328,128]{1,0:T(8,128)(2,1)S(1)} %fusion.1.refs_0_.refs_1_), channel_id=1, source_target_pairs={{0,3},{1,0},{2,1},{3,2},{4,7},{5,4},{6,5},{7,6},{8,11},{9,8},{10,9... | collective-permute-start | bytes 251912 | tf_op jit(solution)/shard_map/ppermute | solution.py:24
  152.0 9.1 %collective-permute-start.1 = (bf16[328,128]{1,0:T(8,128)(2,1)S(1)}, bf16[328,128]{1,0:T(8,128)(2,1)S(1)}, u32[]{:S(2)}, u32[]{:S(2)}) collective-permute-start(bf16[328,128]{1,0:T(8,128)(2,1)S(1)} %fusion.1.refs_0_.refs_1_), channel_id=1, source_target_pairs={{0,2},{1,3},{2,0},{3,1},{4,6},{5,7},{6,4},{7,5},{8,10},{9,11},{10,... | collective-permute-start | bytes 251912 | tf_op jit(solution)/shard_map/ppermute | solution.py:24
  153.9 8.7 %collective-permute-start = (bf16[328,128]{1,0:T(8,128)(2,1)S(1)}, bf16[328,128]{1,0:T(8,128)(2,1)S(1)}, u32[]{:S(2)}, u32[]{:S(2)}) collective-permute-start(bf16[328,128]{1,0:T(8,128)(2,1)S(1)} %fusion.1.refs_0_.refs_1_), channel_id=1, source_target_pairs={{0,1},{1,2},{2,3},{3,0},{4,5},{5,6},{6,7},{7,4},{8,9},{9,10},{10,1... | collective-permute-start | bytes 251912 | tf_op jit(solution)/shard_map/ppermute | solution.py:24

commit v6 on v5

--- a/solution.py
+++ b/solution.py
@@ -38,21 +38,24 @@
     return row.astype(jnp.float32).astype(jnp.bfloat16)
 
 
-def project_kernel(zh_ref, span_ref, chip_ref, others_ref, w_ref, out_ref):
+def project_kernel(zh_ref, odd_ref, span_ref, mine_ref, pair_ref, w_ref, out_ref):
     zh = zh_ref[0]
-    tokens = chip_ref.shape[1]
+    odd = odd_ref[0]
+    tokens = mine_ref.shape[2]
     places = w_ref.shape[1] // 2
     total = None
     for core in range(2):
-        near = [chip_ref[core], others_ref[1, core], others_ref[core, 2], others_ref[0, core]]
-        for place, act in enumerate(near):
+        for place, (holder, block) in enumerate(((core, 0), (1, 1 + core), (core, 3), (0, 1 + core))):
             source = lax.rem(zh + place, places)
             w = w_ref[:, source * 2 + core]
+            act = jnp.concatenate([mine_ref[holder, block], pair_ref[holder, block]], axis=0)
             part = jnp.dot(act, w.reshape(-1, w.shape[-1]), preferred_element_type=jnp.float32)
             total = part if total is None else total + part
     rounded = total.astype(out_ref.dtype)
-    out_ref[:tokens, :] = rounded
-    out_ref[tokens:, :] = span_rows(span_ref[0], span_ref[1], (SPAN_ROWS, total.shape[1]))
+    spans = span_rows(span_ref[0], span_ref[1], (SPAN_ROWS, total.shape[1]))
+    for slot, rows in ((odd, rounded[:tokens]), (1 - odd, rounded[tokens:])):
+        out_ref[slot, :tokens, :] = rows
+        out_ref[slot, tokens:, :] = spans
 
 
 def column_of(table, lane, place):
@@ -60,14 +63,14 @@
 
 
 def attend_block(query, query_pos, kv_ref, pos_ref, top, total, mixed, factor):
-    chunks, peers = kv_ref.shape[:2]
+    chunks = kv_ref.shape[0]
     width = query.shape[1]
-    tokens = kv_ref.shape[2] - SPAN_ROWS
-    count = peers * tokens
+    tokens = kv_ref.shape[4] - SPAN_ROWS
+    count = kv_ref.shape[2] * 2 * tokens
     scores = []
     first = top
     for chunk in range(chunks):
-        keys = kv_ref[chunk, :, :tokens, :width].reshape(count, width)
+        keys = kv_ref[chunk, 0, :, :, :tokens, :].reshape(count, width)
         score = lax.dot_general(
             query, keys, (((1,), (1,)), ((), ())), preferred_element_type=jnp.float32
         )
@@ -82,7 +85,7 @@
         total = total * kept
         mixed = mixed * kept
     for chunk in range(chunks):
-        values = kv_ref[chunk, :, :tokens, width:].reshape(count, width)
+        values = kv_ref[chunk, 1, :, :, :tokens, :].reshape(count, width)
         weight = jnp.exp2((scores[chunk] - top) * factor)
         total = total + jnp.sum(weight, axis=1, keepdims=True)
         mixed = mixed + jnp.dot(
@@ -92,20 +95,24 @@
 
 
 def fill_positions(kv_ref, pos_ref):
-    chunks, peers = kv_ref.shape[:2]
-    tokens = kv_ref.shape[2] - SPAN_ROWS
+    chunks, _, lines = kv_ref.shape[:3]
+    tokens = kv_ref.shape[4] - SPAN_ROWS
     half = tokens // 2
-    count = peers * tokens
-    lane = lax.broadcasted_iota(jnp.int32, (peers, count), 1)
-    inside = lane - lax.broadcasted_iota(jnp.int32, (peers, count), 0) * tokens
-    early = (inside >= 0) & (inside < half)
-    late = (inside >= half) & (inside < tokens)
+    count = lines * 2 * tokens
+    lane = lax.broadcasted_iota(jnp.int32, (lines, count), 1)
+    line = lax.broadcasted_iota(jnp.int32, (lines, count), 0)
     for chunk in range(chunks):
-        held = kv_ref[chunk, :, tokens:, :128].astype(jnp.float32)
-        spans = jnp.max(held, axis=1) * half
-        place = jnp.where(early, spans[:, 0:1], jnp.where(late, spans[:, 1:2] - half, 0.0))
-        place = place + jnp.where(early | late, inside.astype(jnp.float32), 0.0)
-        pos_ref[chunk : chunk + 1, :] = jnp.sum(place, axis=0, keepdims=True)
+        total = jnp.zeros((1, count), jnp.float32)
+        for slot in range(2):
+            inside = lane - (line * 2 + slot) * tokens
+            early = (inside >= 0) & (inside < half)
+            late = (inside >= half) & (inside < tokens)
+            held = kv_ref[chunk, slot, :, slot, tokens:, :].astype(jnp.float32)
+            spans = jnp.max(held, axis=1) * half
+            place = jnp.where(early, spans[:, 0:1], jnp.where(late, spans[:, 1:2] - half, 0.0))
+            place = place + jnp.where(early | late, inside.astype(jnp.float32), 0.0)
+            total = total + jnp.sum(place, axis=0, keepdims=True)
+        pos_ref[chunk : chunk + 1, :] = total
 
 
 def query_positions(q_ref, block, rows, tokens):
@@ -127,7 +134,7 @@
     state_ref[...] = jnp.zeros(state_ref.shape, jnp.float32)
 
     def step(block, carry):
-        query_pos = query_positions(q_ref, block, rows, kv_ref.shape[2] - SPAN_ROWS)
+        query_pos = query_positions(q_ref, block, rows, kv_ref.shape[4] - SPAN_ROWS)
         top = jnp.full((rows, 1), FLOOR, jnp.float32)
         query = q_ref[block, :rows, :]
         top, total, mixed = attend_block(query, query_pos, kv_ref, pos_ref, top, None, None, factor)
@@ -155,7 +162,7 @@
 
     def step(block, carry):
         owner = lax.rem(own + blocks - block, blocks)
-        query_pos = query_positions(q_ref, block, rows, kv_ref.shape[2] - SPAN_ROWS)
+        query_pos = query_positions(q_ref, block, rows, kv_ref.shape[4] - SPAN_ROWS)
         state = state_ref[...]
         top = column_of(state, lane, block)
         total = column_of(state, lane, block + 8)
@@ -228,6 +235,7 @@
     plane = lax.axis_size(PLANE)
     side = lax.axis_size("zi")
     zh = lax.axis_index("zh").astype(jnp.int32).reshape(1)
+    odd = (lax.axis_index("x") % 2).astype(jnp.int32).reshape(1)
     own = lax.axis_index("zi").astype(jnp.int32).reshape(1)
 
     slabs = lax.axis_size("zh")
@@ -235,14 +243,19 @@
     chip = lax.all_gather(activations, "core")
     near = lax.ppermute(chip, HEADS, turn)
     far = shifted(activations, "zh", 2)
-    others = lax.all_gather(jnp.concatenate([near, far[None]]), "core")
+    own_blocks = jnp.concatenate([activations[None], near, far[None]])
+    pair_blocks = lax.ppermute(own_blocks, "x", [(i, i ^ 1) for i in range(lax.axis_size("x"))])
+    mine = lax.all_gather(own_blocks, "core")
+    pair = lax.all_gather(pair_blocks, "core")
 
     piece = w_kv.shape[0]
     w = w_kv.reshape(piece, ranks, 2 * width).transpose(1, 0, 2)
     w = exchanged(w, HEADS)
     w = exchanged(copies(w, line), LINE)
     w = w.transpose(1, 0, 2, 3).reshape(ranks, line * piece, 2 * width)
-    w = exchanged(copies(w, plane), PLANE)
+    parts = jnp.stack([w[..., :width], w[..., width:]])[None, :, None]
+    parts = jnp.broadcast_to(parts, (lax.axis_size("x") // 2, 2, lax.axis_size("y"), *parts.shape[3:]))
+    w = exchanged(parts.reshape(plane, *parts.shape[3:]), PLANE)
 
     spans = jnp.pad(span_of.astype(jnp.bfloat16)[None], ((0, SPAN_ROWS - 1), (0, width - 2)))
     q = queries.transpose(1, 0, 2).reshape(rows, width)
@@ -253,13 +266,13 @@
 
     kv = pl.pallas_call(
         project_kernel,
-        out_shape=jax.ShapeDtypeStruct((tokens + SPAN_ROWS, 2 * width), jnp.bfloat16),
-        in_specs=[SMEM, SMEM, VMEM, VMEM, VMEM],
+        out_shape=jax.ShapeDtypeStruct((2, tokens + SPAN_ROWS, width), jnp.bfloat16),
+        in_specs=[SMEM, SMEM, SMEM, VMEM, VMEM, VMEM],
         out_specs=VMEM,
         name="project",
         compiler_params=pltpu.CompilerParams(vmem_limit_bytes=12 * 1024 * 1024),
-    )(zh, span_of, chip, others, w)
-    sets = (2, plane // 2, tokens + SPAN_ROWS, 2 * width)
+    )(zh, odd, span_of, mine, pair, w)
+    sets = (lax.axis_size("x") // 2, 2, lax.axis_size("y"), 2, tokens + SPAN_ROWS, width)
     other = shifted(kv, "zo", 1)
     first = exchanged(copies(kv, plane), PLANE).reshape(sets)
     spread = copies(other, plane)

time: 184 us -> 194 us (1.054)
  blocking collectives: 95.4 us -> 102 us
  starting transfers between devices: 45.3 us -> 50.6 us
  waiting for transfers between devices: 28.1 us -> 25 us
    all_gather x1 -> x2, blocking collectives: 14.8 us -> 20.7 us  [the longest x1 14.8 us: body(): mine = lax.all_gather(own_blocks, 'core')]
    ppermute x5, starting transfers between devices: 21.8 us -> 24.9 us  [shifted(): lax.ppermute(value, axis, [(i, (i + by) % size) for i in range(size)])]
    ppermute x5, waiting for transfers between devices: 26 us -> 23.7 us  [shifted(): lax.ppermute(value, axis, [(i, (i + by) % size) for i in range(size)])]
    ppermute x0 -> x1, starting transfers between devices: none -> 2.01 us  [body(): lax.ppermute(own_blocks, 'x', [(i, i ^ 1) for i in range(lax.axis_size('x...]
  transfers between devices with their start and end apart: 9 -> 10, of which waited for: 5 -> 5; matrix products, arithmetic and copies ran while one was open for 0% -> 0% of each run, Pallas kernels for 2% -> 2%
where the time goes in v6:
time: 194 us; the launch traced here: 193 us
  blocking collectives  102 us (53%)
  starting transfers between devices  50.6 us (26%)
  waiting for transfers between devices  25 us (13%)
  Pallas kernels  10.1 us (5%)
  local copies, waits for them, and re-layouts  4.64 us (2%)
    all_to_all x3, blocking collectives, exchanged(): return lax.all_to_all(blocks, axes, 0, 0, tiled=True)  79.8 us
    ppermute x5, starting transfers between devices, shifted(): lax.ppermute(value, axis, [(i, (i + by) % size) for i in range(size)])  24.9 us
    ppermute x5, waiting for transfers between devices, shifted(): lax.ppermute(value, axis, [(i, (i + by) % size) for i in range(size)])  23.7 us
    all_to_all x3, starting transfers between devices, exchanged(): return lax.all_to_all(blocks, axes, 0, 0, tiled=True)  21 us
    all_gather x1, blocking collectives, body(): mine = lax.all_gather(own_blocks, 'core')  14.8 us
    all_gather x1, blocking collectives, body(): pair = lax.all_gather(pair_blocks, 'core')  5.86 us
    pallas_call x1, Pallas kernels, body(): pl.pallas_call(lambda *refs: finish_kernel(*refs, scale=scale), out_shape...  4.15 us
  transfers between devices with their start and end apart: 10, of which 5 were waited for; matrix products, arithmetic and copies ran while one was open for 0% of the time, Pallas kernels for 2%

profile of v6, /device:TPU:2, one launch (start us, length us, event | category | flops | bytes accessed | tf_op | source)
XLA Modules:
  0.0 192.8 jit_solution(11874256001950963258)
XLA Ops:
  0.0 0.7 reshape.43
  0.8 50.4 %all_to_all.30 = bf16[8,4,256]{2,1,0:T(4,128)(2,1)S(1)} all-to-all(bf16[8,4,256]{2,1,0:T(4,128)(2,1)S(1)} %bitcast.35), channel_id=1, replica_groups=mesh['zh'=4,'core'=2,'x'=4,'y'=4,'zo'=2,'zi'=4] {'zh','core'}, dimensions={0} | all-to-all | bytes 32768 | tf_op jit(solution)/shard_map/all_to_all | solution.py:28
  51.2 16.7 %all_to_all.31 = bf16[8,8,4,256]{3,2,1,0:T(4,128)(2,1)S(1)} all-to-all(bf16[8,8,4,256]{3,2,1,0:T(4,128)(2,1)S(1)} %broadcast_in_dim.17), channel_id=1, replica_groups=mesh['zh'=4,'core'=2,'x'=4,'y'=4,'zo'=2,'zi'=4] {'zo','zi'}, dimensions={0} | all-to-all | bytes 262144 | tf_op jit(solution)/shard_map/all_to_all | solution.py:28
  68.0 1.2 broadcast_in_dim.18
  69.2 0.0 copy-start.1
  69.2 7.6 %all-to-all-start.2 = ((bf16[16,8,32,128]{3,2,1,0:T(8,128)(2,1)}), bf16[16,8,32,128]{3,2,1,0:T(8,128)(2,1)S(1)}, u32[]{:S(2)}, u32[]{:S(2)}) async-start(bf16[16,8,32,128]{3,2,1,0:T(8,128)(2,1)} %bitcast.17), calls=%async_computation.2 | async-start | bytes 2097152 | tf_op jit(solution)/shard_map/all_to_all | solution.py:28
  76.8 0.0 copy-done.1
  76.8 1.9 all-gather
  78.7 2.7 %collective-permute-start.3 = (bf16[2,80,512]{2,1,0:T(8,128)(2,1)S(1)}, bf16[2,80,512]{2,1,0:T(8,128)(2,1)S(1)}, u32[]{:S(2)}, u32[]{:S(2)}) collective-permute-start(bf16[2,80,512]{2,1,0:T(8,128)(2,1)S(1)} %bitcast.32), channel_id=1, source_target_pairs={{0,256},{128,896},{256,512},{384,128},{512,768},{640,384},{768,0},... | collective-permute-start | bytes 491528 | tf_op jit(solution)/shard_map/ppermute | solution.py:244
  81.4 12.1 %collective-permute-start.4 = (bf16[80,512]{1,0:T(8,128)(2,1)S(1)}, bf16[80,512]{1,0:T(8,128)(2,1)S(1)}, u32[]{:S(2)}, u32[]{:S(2)}) collective-permute-start(bf16[80,512]{1,0:T(8,128)(2,1)S(1)} %copy-done.1), channel_id=1, source_target_pairs={{0,512},{256,768},{512,0},{768,256},{1,513},{257,769},{513,1},{769... | collective-permute-start | bytes 245768 | tf_op jit(solution)/shard_map/ppermute | solution.py:24
  93.5 13.4 %collective-permute-done.4 = bf16[80,512]{1,0:T(8,128)(2,1)S(1)} collective-permute-done((bf16[80,512]{1,0:T(8,128)(2,1)S(1)}, bf16[80,512]{1,0:T(8,128)(2,1)S(1)}, u32[]{:S(2)}, u32[]{:S(2)}) %collective-permute-start.4) | collective-permute-done | bytes 81952 | tf_op jit(solution)/shard_map/ppermute | solution.py:24
  106.8 0.0 collective-permute-done.3
  106.9 2.0 %collective-permute-start.5 = (bf16[4,80,512]{2,1,0:T(8,128)(2,1)S(1)}, bf16[4,80,512]{2,1,0:T(8,128)(2,1)S(1)}, u32[]{:S(2)}, u32[]{:S(2)}) collective-permute-start(bf16[4,80,512]{2,1,0:T(8,128)(2,1)S(1)} %pad_maximum_fusion), channel_id=1, source_target_pairs={{0,32},{32,0},{64,96},{96,64},{1,33},{33,1},{65,97},{97,65},{2,34}... | collective-permute-start | bytes 983048 | tf_op jit(solution)/shard_map/ppermute | solution.py:247
  108.9 14.8 %all-gather.1 = bf16[8,80,512]{2,1,0:T(8,128)(2,1)S(1)} all-gather(bf16[4,80,512]{2,1,0:T(8,128)(2,1)S(1)} %pad_maximum_fusion), channel_id=3, replica_groups=mesh['zh'=4,'core'=2,'x'=4,'y'=4,'zo'=2,'zi'=4] {'core'}, dimensions={0}, use_global_device_ids=true | all-gather | bytes 983040 | tf_op jit(solution)/shard_map/all_gather | solution.py:248
  123.7 0.0 collective-permute-done.5
  123.7 5.9 %all-gather.2 = bf16[8,80,512]{2,1,0:T(8,128)(2,1)S(1)} all-gather(bf16[4,80,512]{2,1,0:T(8,128)(2,1)S(1)} %collective-permute-done.5), channel_id=4, replica_groups=mesh['zh'=4,'core'=2,'x'=4,'y'=4,'zo'=2,'zi'=4] {'core'}, dimensions={0}, use_global_device_ids=true | all-gather | bytes 983040 | tf_op jit(solution)/shard_map/all_gather | solution.py:249
  129.6 0.0 all-to-all-done.2.w_ref
  129.6 0.0 copy-start
  129.6 0.7 copy-done
  130.2 1.0 project.1
  131.3 1.0 broadcast_in_dim.39
  132.2 7.2 %all-to-all-start.4 = ((bf16[16,2,88,128]{3,2,1,0:T(8,128)(2,1)}), bf16[16,2,88,128]{3,2,1,0:T(8,128)(2,1)S(1)}, u32[]{:S(2)}, u32[]{:S(2)}) async-start(bf16[16,2,88,128]{3,2,1,0:T(8,128)(2,1)} %broadcast_in_dim.39), calls=%async_computation.4 | async-start | bytes 1441792 | tf_op jit(solution)/shard_map/all_to_all | solution.py:28
  139.5 3.3 %collective-permute-start.6 = (bf16[2,88,128]{2,1,0:T(8,128)(2,1)S(1)}, bf16[2,88,128]{2,1,0:T(8,128)(2,1)S(1)}, u32[]{:S(2)}, u32[]{:S(2)}) collective-permute-start(bf16[2,88,128]{2,1,0:T(8,128)(2,1)S(1)} %project.1), channel_id=1, source_target_pairs={{0,4},{4,0},{1,5},{5,1},{2,6},{6,2},{3,7},{7,3},{8,12},{12,8},{9,1... | collective-permute-start | bytes 135176 | tf_op jit(solution)/shard_map/ppermute | solution.py:24
  142.7 7.3 %collective-permute-done.6 = bf16[2,88,128]{2,1,0:T(8,128)(2,1)S(1)} collective-permute-done((bf16[2,88,128]{2,1,0:T(8,128)(2,1)S(1)}, bf16[2,88,128]{2,1,0:T(8,128)(2,1)S(1)}, u32[]{:S(2)}, u32[]{:S(2)}) %collective-permute-start.6) | collective-permute-done | bytes 45088 | tf_op jit(solution)/shard_map/ppermute | solution.py:24
  150.1 1.3 all-to-all-done.4
  151.4 1.0 broadcast_in_dim.38
  152.3 0.0 copy-start.2
  152.3 6.1 %all-to-all-start.3 = ((bf16[16,2,88,128]{3,2,1,0:T(8,128)(2,1)}), bf16[16,2,88,128]{3,2,1,0:T(8,128)(2,1)S(1)}, u32[]{:S(2)}, u32[]{:S(2)}) async-start(bf16[16,2,88,128]{3,2,1,0:T(8,128)(2,1)} %broadcast_in_dim.38), calls=%async_computation.3 | async-start | bytes 1441792 | tf_op jit(solution)/shard_map/all_to_all | solution.py:28
  158.5 0.0 copy-done.2
  158.5 2.6 %collective-permute-start = (bf16[328,128]{1,0:T(8,128)(2,1)S(1)}, bf16[328,128]{1,0:T(8,128)(2,1)S(1)}, u32[]{:S(2)}, u32[]{:S(2)}) collective-permute-start(bf16[328,128]{1,0:T(8,128)(2,1)S(1)} %fusion.1.refs_0_.refs_1_), channel_id=1, source_target_pairs={{0,1},{1,2},{2,3},{3,0},{4,5},{5,6},{6,7},{7,4},{8,9},{9,10},{10,1... | collective-permute-start | bytes 251912 | tf_op jit(solution)/shard_map/ppermute | solution.py:24
  161.1 1.9 collective-permute-start.1
  163.0 5.1 %collective-permute-start.2 = (bf16[328,128]{1,0:T(8,128)(2,1)S(1)}, bf16[328,128]{1,0:T(8,128)(2,1)S(1)}, u32[]{:S(2)}, u32[]{:S(2)}) collective-permute-start(bf16[328,128]{1,0:T(8,128)(2,1)S(1)} %fusion.1.refs_0_.refs_1_), channel_id=1, source_target_pairs={{0,3},{1,0},{2,1},{3,2},{4,7},{5,4},{6,5},{7,6},{8,11},{9,8},{10,9... | collective-permute-start | bytes 251912 | tf_op jit(solution)/shard_map/ppermute | solution.py:24
  168.1 0.0 collective-permute-done.refs_1_.refs_2_
  168.1 1.1 collective-permute-done.1.refs_2_.refs_3_
  169.2 1.9 collective-permute-done.2.refs_3_.refs_4_
  171.1 3.8 %begin.1 = (f32[4,320,128]{2,1,0:T(8,128)S(1)}, f32[320,128]{1,0:T(8,128)S(1)}) custom-call(bf16[328,128]{1,0:T(8,128)(2,1)S(1)} %fusion.1.refs_0_.refs_1_, bf16[328,128]{1,0:T(8,128)(2,1)S(1)} %collective-permute-done.refs_1_.refs_2_, bf16[328,128]{1,0:T(8,128)(2,1)S(1)} %collective-permute-done.1.refs_2_.refs_3_, ...), custom_call_target="tpu_custom_call" | custom-call | tf_op jit(solution)/shard_map/begin/pallas_call | solution.py:285
  174.9 0.0 all-to-all-done.3
  174.9 4.2 %finish.1 = bf16[4,336,128]{2,1,0:T(8,128)(2,1)S(1)} custom-call(s32[1]{0:T(128)} %bitcast.refs_0_, bf16[328,128]{1,0:T(8,128)(2,1)S(1)} %fusion.1.refs_0_.refs_1_, bf16[328,128]{1,0:T(8,128)(2,1)S(1)} %collective-permute-done.refs_1_.refs_2_, bf16[328,128]{1,0:T(8,128)(2,1)S(1)} %collective-permute-done.1.refs_2_.refs_3_, ...), custom_call_target="tpu_custom_call" | custom-call | tf_op jit(solution)/shard_map/finish/pallas_call | solution.py:297
  179.1 12.7 %all_to_all.32.refs_0_ = bf16[4,336,128]{2,1,0:T(8,128)(2,1)S(1)} all-to-all(bf16[4,336,128]{2,1,0:T(8,128)(2,1)S(1)} %finish.1), channel_id=1, replica_groups=mesh['zh'=4,'core'=2,'x'=4,'y'=4,'zo'=2,'zi'=4] {'zi'}, dimensions={0} | all-to-all | bytes 688128 | tf_op jit(solution)/shard_map/all_to_all | solution.py:28
  191.8 1.0 combine.1
  (10 shorter events, 0.2 us)
Async XLA Ops:
  69.2 7.6 %copy-start.1 = (bf16[80,512]{1,0:T(8,128)(2,1)S(1)}, bf16[80,512]{1,0:T(8,128)(2,1)}, u32[]{:S(2)}) copy-start(bf16[80,512]{1,0:T(8,128)(2,1)} %param.4) | copy-start | bytes 245764
  69.2 60.4 %all-to-all-start.2 = ((bf16[16,8,32,128]{3,2,1,0:T(8,128)(2,1)}), bf16[16,8,32,128]{3,2,1,0:T(8,128)(2,1)S(1)}, u32[]{:S(2)}, u32[]{:S(2)}) async-start(bf16[16,8,32,128]{3,2,1,0:T(8,128)(2,1)} %bitcast.17), calls=%async_computation.2 | async-start | bytes 2097152 | tf_op jit(solution)/shard_map/all_to_all | solution.py:28
  78.7 28.1 %collective-permute-start.3 = (bf16[2,80,512]{2,1,0:T(8,128)(2,1)S(1)}, bf16[2,80,512]{2,1,0:T(8,128)(2,1)S(1)}, u32[]{:S(2)}, u32[]{:S(2)}) collective-permute-start(bf16[2,80,512]{2,1,0:T(8,128)(2,1)S(1)} %bitcast.32), channel_id=1, source_target_pairs={{0,256},{128,896},{256,512},{384,128},{512,768},{640,384},{768,0},... | collective-permute-start | bytes 491528 | tf_op jit(solution)/shard_map/ppermute | solution.py:244
  81.4 25.5 %collective-permute-start.4 = (bf16[80,512]{1,0:T(8,128)(2,1)S(1)}, bf16[80,512]{1,0:T(8,128)(2,1)S(1)}, u32[]{:S(2)}, u32[]{:S(2)}) collective-permute-start(bf16[80,512]{1,0:T(8,128)(2,1)S(1)} %copy-done.1), channel_id=1, source_target_pairs={{0,512},{256,768},{512,0},{768,256},{1,513},{257,769},{513,1},{769... | collective-permute-start | bytes 245768 | tf_op jit(solution)/shard_map/ppermute | solution.py:24
  106.9 16.8 %collective-permute-start.5 = (bf16[4,80,512]{2,1,0:T(8,128)(2,1)S(1)}, bf16[4,80,512]{2,1,0:T(8,128)(2,1)S(1)}, u32[]{:S(2)}, u32[]{:S(2)}) collective-permute-start(bf16[4,80,512]{2,1,0:T(8,128)(2,1)S(1)} %pad_maximum_fusion), channel_id=1, source_target_pairs={{0,32},{32,0},{64,96},{96,64},{1,33},{33,1},{65,97},{97,65},{2,34}... | collective-permute-start | bytes 983048 | tf_op jit(solution)/shard_map/ppermute | solution.py:247
  129.6 0.7 copy-start
  132.2 19.1 %all-to-all-start.4 = ((bf16[16,2,88,128]{3,2,1,0:T(8,128)(2,1)}), bf16[16,2,88,128]{3,2,1,0:T(8,128)(2,1)S(1)}, u32[]{:S(2)}, u32[]{:S(2)}) async-start(bf16[16,2,88,128]{3,2,1,0:T(8,128)(2,1)} %broadcast_in_dim.39), calls=%async_computation.4 | async-start | bytes 1441792 | tf_op jit(solution)/shard_map/all_to_all | solution.py:28
  139.5 10.6 %collective-permute-start.6 = (bf16[2,88,128]{2,1,0:T(8,128)(2,1)S(1)}, bf16[2,88,128]{2,1,0:T(8,128)(2,1)S(1)}, u32[]{:S(2)}, u32[]{:S(2)}) collective-permute-start(bf16[2,88,128]{2,1,0:T(8,128)(2,1)S(1)} %project.1), channel_id=1, source_target_pairs={{0,4},{4,0},{1,5},{5,1},{2,6},{6,2},{3,7},{7,3},{8,12},{12,8},{9,1... | collective-permute-start | bytes 135176 | tf_op jit(solution)/shard_map/ppermute | solution.py:24
  152.3 6.1 %copy-start.2 = (bf16[80,4,128]{2,1,0:T(4,128)(2,1)S(1)}, bf16[80,4,128]{2,1,0:T(4,128)(2,1)}, u32[]{:S(2)}) copy-start(bf16[80,4,128]{2,1,0:T(4,128)(2,1)} %param.5) | copy-start | bytes 245764
  152.3 22.6 %all-to-all-start.3 = ((bf16[16,2,88,128]{3,2,1,0:T(8,128)(2,1)}), bf16[16,2,88,128]{3,2,1,0:T(8,128)(2,1)S(1)}, u32[]{:S(2)}, u32[]{:S(2)}) async-start(bf16[16,2,88,128]{3,2,1,0:T(8,128)(2,1)} %broadcast_in_dim.38), calls=%async_computation.3 | async-start | bytes 1441792 | tf_op jit(solution)/shard_map/all_to_all | solution.py:28
  158.5 9.6 %collective-permute-start = (bf16[328,128]{1,0:T(8,128)(2,1)S(1)}, bf16[328,128]{1,0:T(8,128)(2,1)S(1)}, u32[]{:S(2)}, u32[]{:S(2)}) collective-permute-start(bf16[328,128]{1,0:T(8,128)(2,1)S(1)} %fusion.1.refs_0_.refs_1_), channel_id=1, source_target_pairs={{0,1},{1,2},{2,3},{3,0},{4,5},{5,6},{6,7},{7,4},{8,9},{9,10},{10,1... | collective-permute-start | bytes 251912 | tf_op jit(solution)/shard_map/ppermute | solution.py:24
  161.1 8.1 %collective-permute-start.1 = (bf16[328,128]{1,0:T(8,128)(2,1)S(1)}, bf16[328,128]{1,0:T(8,128)(2,1)S(1)}, u32[]{:S(2)}, u32[]{:S(2)}) collective-permute-start(bf16[328,128]{1,0:T(8,128)(2,1)S(1)} %fusion.1.refs_0_.refs_1_), channel_id=1, source_target_pairs={{0,2},{1,3},{2,0},{3,1},{4,6},{5,7},{6,4},{7,5},{8,10},{9,11},{10,... | collective-permute-start | bytes 251912 | tf_op jit(solution)/shard_map/ppermute | solution.py:24
  163.0 8.1 %collective-permute-start.2 = (bf16[328,128]{1,0:T(8,128)(2,1)S(1)}, bf16[328,128]{1,0:T(8,128)(2,1)S(1)}, u32[]{:S(2)}, u32[]{:S(2)}) collective-permute-start(bf16[328,128]{1,0:T(8,128)(2,1)S(1)} %fusion.1.refs_0_.refs_1_), channel_id=1, source_target_pairs={{0,3},{1,0},{2,1},{3,2},{4,7},{5,4},{6,5},{7,6},{8,11},{9,8},{10,9... | collective-permute-start | bytes 251912 | tf_op jit(solution)/shard_map/ppermute | solution.py:24

commit v7 on v6

--- a/solution.py
+++ b/solution.py
@@ -243,10 +243,12 @@
     chip = lax.all_gather(activations, "core")
     near = lax.ppermute(chip, HEADS, turn)
     far = shifted(activations, "zh", 2)
-    own_blocks = jnp.concatenate([activations[None], near, far[None]])
-    pair_blocks = lax.ppermute(own_blocks, "x", [(i, i ^ 1) for i in range(lax.axis_size("x"))])
-    mine = lax.all_gather(own_blocks, "core")
-    pair = lax.all_gather(pair_blocks, "core")
+    swap = [(i, i ^ 1) for i in range(lax.axis_size("x"))]
+    first_blocks = jnp.concatenate([activations[None], near])
+    pair_near = lax.ppermute(first_blocks, "x", swap)
+    pair_far = lax.ppermute(far, "x", swap)
+    mine = lax.all_gather(jnp.concatenate([first_blocks, far[None]]), "core")
+    pair = lax.all_gather(jnp.concatenate([pair_near, pair_far[None]]), "core")
 
     piece = w_kv.shape[0]
     w = w_kv.reshape(piece, ranks, 2 * width).transpose(1, 0, 2)

time: 194 us -> 194 us (level)
  starting transfers between devices: 50.6 us -> 57.4 us
  blocking collectives: 102 us -> 97.8 us
  waiting for transfers between devices: 25 us -> 22.9 us
    all_gather x2, blocking collectives: 20.7 us -> 15.9 us  [the longest x1 10.9 us: body(): mine = lax.all_gather(jnp.concatenate([first_blocks, far[None]]), 'core')]
    ppermute x1 -> x2, starting transfers between devices: 2.01 us -> 5.83 us  [the longest x1 3.83 us: body(): pair_near = lax.ppermute(first_blocks, 'x', swap)]
    ppermute x5, starting transfers between devices: 24.9 us -> 27.4 us  [shifted(): lax.ppermute(value, axis, [(i, (i + by) % size) for i in range(size)])]
  transfers between devices with their start and end apart: 10 -> 11, of which waited for: 5 -> 5; matrix products, arithmetic and copies ran while one was open for 0% -> 0% of each run, Pallas kernels for 2% -> 2%
where the time goes in v7:
time: 194 us; the launch traced here: 193 us
  blocking collectives  97.8 us (50%)
  starting transfers between devices  57.4 us (30%)
  waiting for transfers between devices  22.9 us (12%)
  Pallas kernels  10.1 us (5%)
  local copies, waits for them, and re-layouts  4.66 us (2%)
    all_to_all x3, blocking collectives, exchanged(): return lax.all_to_all(blocks, axes, 0, 0, tiled=True)  80 us
    ppermute x5, starting transfers between devices, shifted(): lax.ppermute(value, axis, [(i, (i + by) % size) for i in range(size)])  27.4 us
    ppermute x5, waiting for transfers between devices, shifted(): lax.ppermute(value, axis, [(i, (i + by) % size) for i in range(size)])  22.2 us
    all_to_all x3, starting transfers between devices, exchanged(): return lax.all_to_all(blocks, axes, 0, 0, tiled=True)  21.5 us
    all_gather x1, blocking collectives, body(): mine = lax.all_gather(jnp.concatenate([first_blocks, far[None]]), 'core')  10.9 us
    all_gather x1, blocking collectives, body(): pair = lax.all_gather(jnp.concatenate([pair_near, pair_far[None]]), 'core')  4.96 us
    pallas_call x1, Pallas kernels, body(): pl.pallas_call(lambda *refs: finish_kernel(*refs, scale=scale), out_shape...  4.15 us
  transfers between devices with their start and end apart: 11, of which 5 were waited for; matrix products, arithmetic and copies ran while one was open for 0% of the time, Pallas kernels for 2%

profile of v7, /device:TPU:2, one launch (start us, length us, event | category | flops | bytes accessed | tf_op | source)
XLA Modules:
  0.0 193.1 jit_solution(514711185666032713)
XLA Ops:
  0.0 0.7 reshape.43
  0.8 50.4 %all_to_all.30 = bf16[8,4,256]{2,1,0:T(4,128)(2,1)S(1)} all-to-all(bf16[8,4,256]{2,1,0:T(4,128)(2,1)S(1)} %bitcast.38), channel_id=1, replica_groups=mesh['zh'=4,'core'=2,'x'=4,'y'=4,'zo'=2,'zi'=4] {'zh','core'}, dimensions={0} | all-to-all | bytes 32768 | tf_op jit(solution)/shard_map/all_to_all | solution.py:28
  51.2 16.7 %all_to_all.31 = bf16[8,8,4,256]{3,2,1,0:T(4,128)(2,1)S(1)} all-to-all(bf16[8,8,4,256]{3,2,1,0:T(4,128)(2,1)S(1)} %broadcast_in_dim.40), channel_id=1, replica_groups=mesh['zh'=4,'core'=2,'x'=4,'y'=4,'zo'=2,'zi'=4] {'zo','zi'}, dimensions={0} | all-to-all | bytes 262144 | tf_op jit(solution)/shard_map/all_to_all | solution.py:28
  68.0 1.2 broadcast_in_dim.41
  69.2 0.0 copy-start.1
  69.2 7.6 %all-to-all-start.2 = ((bf16[16,8,32,128]{3,2,1,0:T(8,128)(2,1)}), bf16[16,8,32,128]{3,2,1,0:T(8,128)(2,1)S(1)}, u32[]{:S(2)}, u32[]{:S(2)}) async-start(bf16[16,8,32,128]{3,2,1,0:T(8,128)(2,1)} %bitcast.18), calls=%async_computation.2 | async-start | bytes 2097152 | tf_op jit(solution)/shard_map/all_to_all | solution.py:28
  76.8 0.0 copy-done.1
  76.8 1.9 all-gather
  78.7 2.7 %collective-permute-start.3 = (bf16[2,80,512]{2,1,0:T(8,128)(2,1)S(1)}, bf16[2,80,512]{2,1,0:T(8,128)(2,1)S(1)}, u32[]{:S(2)}, u32[]{:S(2)}) collective-permute-start(bf16[2,80,512]{2,1,0:T(8,128)(2,1)S(1)} %bitcast.34), channel_id=1, source_target_pairs={{0,256},{128,896},{256,512},{384,128},{512,768},{640,384},{768,0},... | collective-permute-start | bytes 491528 | tf_op jit(solution)/shard_map/ppermute | solution.py:244
  81.4 12.1 %collective-permute-start.4 = (bf16[80,512]{1,0:T(8,128)(2,1)S(1)}, bf16[80,512]{1,0:T(8,128)(2,1)S(1)}, u32[]{:S(2)}, u32[]{:S(2)}) collective-permute-start(bf16[80,512]{1,0:T(8,128)(2,1)S(1)} %copy-done.1), channel_id=1, source_target_pairs={{0,512},{256,768},{512,0},{768,256},{1,513},{257,769},{513,1},{769... | collective-permute-start | bytes 245768 | tf_op jit(solution)/shard_map/ppermute | solution.py:24
  93.5 13.4 %collective-permute-done.4 = bf16[80,512]{1,0:T(8,128)(2,1)S(1)} collective-permute-done((bf16[80,512]{1,0:T(8,128)(2,1)S(1)}, bf16[80,512]{1,0:T(8,128)(2,1)S(1)}, u32[]{:S(2)}, u32[]{:S(2)}) %collective-permute-start.4) | collective-permute-done | bytes 81952 | tf_op jit(solution)/shard_map/ppermute | solution.py:24
  106.8 2.0 %collective-permute-start.6 = (bf16[80,512]{1,0:T(8,128)(2,1)S(1)}, bf16[80,512]{1,0:T(8,128)(2,1)S(1)}, u32[]{:S(2)}, u32[]{:S(2)}) collective-permute-start(bf16[80,512]{1,0:T(8,128)(2,1)S(1)} %collective-permute-done.4), channel_id=1, source_target_pairs={{0,32},{32,0},{64,96},{96,64},{1,33},{33,1},{65,97},{97,65},{2,34}... | collective-permute-start | bytes 245768 | tf_op jit(solution)/shard_map/ppermute | solution.py:249
  108.8 0.0 collective-permute-done.3
  108.9 3.8 %collective-permute-start.5 = (bf16[3,80,512]{2,1,0:T(8,128)(2,1)S(1)}, bf16[3,80,512]{2,1,0:T(8,128)(2,1)S(1)}, u32[]{:S(2)}, u32[]{:S(2)}) collective-permute-start(bf16[3,80,512]{2,1,0:T(8,128)(2,1)S(1)} %pad_maximum_fusion.2), channel_id=1, source_target_pairs={{0,32},{32,0},{64,96},{96,64},{1,33},{33,1},{65,97},{97,65},{2,34}... | collective-permute-start | bytes 737288 | tf_op jit(solution)/shard_map/ppermute | solution.py:248
  112.8 10.9 %all-gather.1 = bf16[8,80,512]{2,1,0:T(8,128)(2,1)S(1)} all-gather(bf16[4,80,512]{2,1,0:T(8,128)(2,1)S(1)} %pad_maximum_fusion), channel_id=3, replica_groups=mesh['zh'=4,'core'=2,'x'=4,'y'=4,'zo'=2,'zi'=4] {'core'}, dimensions={0}, use_global_device_ids=true | all-gather | bytes 983040 | tf_op jit(solution)/shard_map/all_gather | solution.py:250
  123.7 0.0 collective-permute-done.6
  123.7 0.0 collective-permute-done.5
  123.8 5.0 %all-gather.2 = bf16[8,80,512]{2,1,0:T(8,128)(2,1)S(1)} all-gather(bf16[4,80,512]{2,1,0:T(8,128)(2,1)S(1)} %pad_maximum_fusion.1), channel_id=4, replica_groups=mesh['zh'=4,'core'=2,'x'=4,'y'=4,'zo'=2,'zi'=4] {'core'}, dimensions={0}, use_global_device_ids=true | all-gather | bytes 983040 | tf_op jit(solution)/shard_map/all_gather | solution.py:251
  128.7 0.0 all-to-all-done.2.w_ref
  128.7 0.0 copy-start
  128.7 0.7 copy-done
  129.4 1.0 project.1
  130.4 1.0 broadcast_in_dim.43
  131.4 7.2 %all-to-all-start.4 = ((bf16[16,2,88,128]{3,2,1,0:T(8,128)(2,1)}), bf16[16,2,88,128]{3,2,1,0:T(8,128)(2,1)S(1)}, u32[]{:S(2)}, u32[]{:S(2)}) async-start(bf16[16,2,88,128]{3,2,1,0:T(8,128)(2,1)} %broadcast_in_dim.43), calls=%async_computation.4 | async-start | bytes 1441792 | tf_op jit(solution)/shard_map/all_to_all | solution.py:28
  138.6 5.2 %collective-permute-start.7 = (bf16[2,88,128]{2,1,0:T(8,128)(2,1)S(1)}, bf16[2,88,128]{2,1,0:T(8,128)(2,1)S(1)}, u32[]{:S(2)}, u32[]{:S(2)}) collective-permute-start(bf16[2,88,128]{2,1,0:T(8,128)(2,1)S(1)} %project.1), channel_id=1, source_target_pairs={{0,4},{4,0},{1,5},{5,1},{2,6},{6,2},{3,7},{7,3},{8,12},{12,8},{9,1... | collective-permute-start | bytes 135176 | tf_op jit(solution)/shard_map/ppermute | solution.py:24
  143.8 6.0 %collective-permute-done.7 = bf16[2,88,128]{2,1,0:T(8,128)(2,1)S(1)} collective-permute-done((bf16[2,88,128]{2,1,0:T(8,128)(2,1)S(1)}, bf16[2,88,128]{2,1,0:T(8,128)(2,1)S(1)}, u32[]{:S(2)}, u32[]{:S(2)}) %collective-permute-start.7) | collective-permute-done | bytes 45088 | tf_op jit(solution)/shard_map/ppermute | solution.py:24
  149.8 0.7 all-to-all-done.4
  150.5 1.0 broadcast_in_dim.42
  151.5 0.0 copy-start.2
  151.5 6.7 %all-to-all-start.3 = ((bf16[16,2,88,128]{3,2,1,0:T(8,128)(2,1)}), bf16[16,2,88,128]{3,2,1,0:T(8,128)(2,1)S(1)}, u32[]{:S(2)}, u32[]{:S(2)}) async-start(bf16[16,2,88,128]{3,2,1,0:T(8,128)(2,1)} %broadcast_in_dim.42), calls=%async_computation.3 | async-start | bytes 1441792 | tf_op jit(solution)/shard_map/all_to_all | solution.py:28
  158.2 0.0 copy-done.2
  158.2 4.0 %collective-permute-start = (bf16[328,128]{1,0:T(8,128)(2,1)S(1)}, bf16[328,128]{1,0:T(8,128)(2,1)S(1)}, u32[]{:S(2)}, u32[]{:S(2)}) collective-permute-start(bf16[328,128]{1,0:T(8,128)(2,1)S(1)} %fusion.1.refs_0_.refs_1_), channel_id=1, source_target_pairs={{0,1},{1,2},{2,3},{3,0},{4,5},{5,6},{6,7},{7,4},{8,9},{9,10},{10,1... | collective-permute-start | bytes 251912 | tf_op jit(solution)/shard_map/ppermute | solution.py:24
  162.2 1.9 collective-permute-start.1
  164.1 4.3 %collective-permute-start.2 = (bf16[328,128]{1,0:T(8,128)(2,1)S(1)}, bf16[328,128]{1,0:T(8,128)(2,1)S(1)}, u32[]{:S(2)}, u32[]{:S(2)}) collective-permute-start(bf16[328,128]{1,0:T(8,128)(2,1)S(1)} %fusion.1.refs_0_.refs_1_), channel_id=1, source_target_pairs={{0,3},{1,0},{2,1},{3,2},{4,7},{5,4},{6,5},{7,6},{8,11},{9,8},{10,9... | collective-permute-start | bytes 251912 | tf_op jit(solution)/shard_map/ppermute | solution.py:24
  168.4 0.0 collective-permute-done.refs_1_.refs_2_
  168.4 2.3 %collective-permute-done.1.refs_2_.refs_3_ = bf16[328,128]{1,0:T(8,128)(2,1)S(1)} collective-permute-done((bf16[328,128]{1,0:T(8,128)(2,1)S(1)}, bf16[328,128]{1,0:T(8,128)(2,1)S(1)}, u32[]{:S(2)}, u32[]{:S(2)}) %collective-permute-start.1) | collective-permute-done | bytes 84000 | tf_op jit(solution)/shard_map/ppermute | solution.py:24
  170.7 0.5 collective-permute-done.2.refs_3_.refs_4_
  171.2 3.8 %begin.1 = (f32[4,320,128]{2,1,0:T(8,128)S(1)}, f32[320,128]{1,0:T(8,128)S(1)}) custom-call(bf16[328,128]{1,0:T(8,128)(2,1)S(1)} %fusion.1.refs_0_.refs_1_, bf16[328,128]{1,0:T(8,128)(2,1)S(1)} %collective-permute-done.refs_1_.refs_2_, bf16[328,128]{1,0:T(8,128)(2,1)S(1)} %collective-permute-done.1.refs_2_.refs_3_, ...), custom_call_target="tpu_custom_call" | custom-call | tf_op jit(solution)/shard_map/begin/pallas_call | solution.py:287
  175.1 0.0 all-to-all-done.3
  175.1 4.2 %finish.1 = bf16[4,336,128]{2,1,0:T(8,128)(2,1)S(1)} custom-call(s32[1]{0:T(128)} %bitcast.refs_0_, bf16[328,128]{1,0:T(8,128)(2,1)S(1)} %fusion.1.refs_0_.refs_1_, bf16[328,128]{1,0:T(8,128)(2,1)S(1)} %collective-permute-done.refs_1_.refs_2_, bf16[328,128]{1,0:T(8,128)(2,1)S(1)} %collective-permute-done.1.refs_2_.refs_3_, ...), custom_call_target="tpu_custom_call" | custom-call | tf_op jit(solution)/shard_map/finish/pallas_call | solution.py:299
  179.2 12.9 %all_to_all.32.refs_0_ = bf16[4,336,128]{2,1,0:T(8,128)(2,1)S(1)} all-to-all(bf16[4,336,128]{2,1,0:T(8,128)(2,1)S(1)} %finish.1), channel_id=1, replica_groups=mesh['zh'=4,'core'=2,'x'=4,'y'=4,'zo'=2,'zi'=4] {'zi'}, dimensions={0} | all-to-all | bytes 688128 | tf_op jit(solution)/shard_map/all_to_all | solution.py:28
  192.1 1.0 combine.1
  (12 shorter events, 0.2 us)
Async XLA Ops:
  69.2 7.6 %copy-start.1 = (bf16[80,512]{1,0:T(8,128)(2,1)S(1)}, bf16[80,512]{1,0:T(8,128)(2,1)}, u32[]{:S(2)}) copy-start(bf16[80,512]{1,0:T(8,128)(2,1)} %param.4) | copy-start | bytes 245764
  69.2 59.6 %all-to-all-start.2 = ((bf16[16,8,32,128]{3,2,1,0:T(8,128)(2,1)}), bf16[16,8,32,128]{3,2,1,0:T(8,128)(2,1)S(1)}, u32[]{:S(2)}, u32[]{:S(2)}) async-start(bf16[16,8,32,128]{3,2,1,0:T(8,128)(2,1)} %bitcast.18), calls=%async_computation.2 | async-start | bytes 2097152 | tf_op jit(solution)/shard_map/all_to_all | solution.py:28
  78.7 30.1 %collective-permute-start.3 = (bf16[2,80,512]{2,1,0:T(8,128)(2,1)S(1)}, bf16[2,80,512]{2,1,0:T(8,128)(2,1)S(1)}, u32[]{:S(2)}, u32[]{:S(2)}) collective-permute-start(bf16[2,80,512]{2,1,0:T(8,128)(2,1)S(1)} %bitcast.34), channel_id=1, source_target_pairs={{0,256},{128,896},{256,512},{384,128},{512,768},{640,384},{768,0},... | collective-permute-start | bytes 491528 | tf_op jit(solution)/shard_map/ppermute | solution.py:244
  81.4 25.5 %collective-permute-start.4 = (bf16[80,512]{1,0:T(8,128)(2,1)S(1)}, bf16[80,512]{1,0:T(8,128)(2,1)S(1)}, u32[]{:S(2)}, u32[]{:S(2)}) collective-permute-start(bf16[80,512]{1,0:T(8,128)(2,1)S(1)} %copy-done.1), channel_id=1, source_target_pairs={{0,512},{256,768},{512,0},{768,256},{1,513},{257,769},{513,1},{769... | collective-permute-start | bytes 245768 | tf_op jit(solution)/shard_map/ppermute | solution.py:24
  106.8 16.9 %collective-permute-start.6 = (bf16[80,512]{1,0:T(8,128)(2,1)S(1)}, bf16[80,512]{1,0:T(8,128)(2,1)S(1)}, u32[]{:S(2)}, u32[]{:S(2)}) collective-permute-start(bf16[80,512]{1,0:T(8,128)(2,1)S(1)} %collective-permute-done.4), channel_id=1, source_target_pairs={{0,32},{32,0},{64,96},{96,64},{1,33},{33,1},{65,97},{97,65},{2,34}... | collective-permute-start | bytes 245768 | tf_op jit(solution)/shard_map/ppermute | solution.py:249
  108.9 14.8 %collective-permute-start.5 = (bf16[3,80,512]{2,1,0:T(8,128)(2,1)S(1)}, bf16[3,80,512]{2,1,0:T(8,128)(2,1)S(1)}, u32[]{:S(2)}, u32[]{:S(2)}) collective-permute-start(bf16[3,80,512]{2,1,0:T(8,128)(2,1)S(1)} %pad_maximum_fusion.2), channel_id=1, source_target_pairs={{0,32},{32,0},{64,96},{96,64},{1,33},{33,1},{65,97},{97,65},{2,34}... | collective-permute-start | bytes 737288 | tf_op jit(solution)/shard_map/ppermute | solution.py:248
  128.7 0.7 copy-start
  131.4 19.1 %all-to-all-start.4 = ((bf16[16,2,88,128]{3,2,1,0:T(8,128)(2,1)}), bf16[16,2,88,128]{3,2,1,0:T(8,128)(2,1)S(1)}, u32[]{:S(2)}, u32[]{:S(2)}) async-start(bf16[16,2,88,128]{3,2,1,0:T(8,128)(2,1)} %broadcast_in_dim.43), calls=%async_computation.4 | async-start | bytes 1441792 | tf_op jit(solution)/shard_map/all_to_all | solution.py:28
  138.6 11.2 %collective-permute-start.7 = (bf16[2,88,128]{2,1,0:T(8,128)(2,1)S(1)}, bf16[2,88,128]{2,1,0:T(8,128)(2,1)S(1)}, u32[]{:S(2)}, u32[]{:S(2)}) collective-permute-start(bf16[2,88,128]{2,1,0:T(8,128)(2,1)S(1)} %project.1), channel_id=1, source_target_pairs={{0,4},{4,0},{1,5},{5,1},{2,6},{6,2},{3,7},{7,3},{8,12},{12,8},{9,1... | collective-permute-start | bytes 135176 | tf_op jit(solution)/shard_map/ppermute | solution.py:24
  151.5 6.7 %copy-start.2 = (bf16[80,4,128]{2,1,0:T(4,128)(2,1)S(1)}, bf16[80,4,128]{2,1,0:T(4,128)(2,1)}, u32[]{:S(2)}) copy-start(bf16[80,4,128]{2,1,0:T(4,128)(2,1)} %param.5) | copy-start | bytes 245764
  151.5 23.6 %all-to-all-start.3 = ((bf16[16,2,88,128]{3,2,1,0:T(8,128)(2,1)}), bf16[16,2,88,128]{3,2,1,0:T(8,128)(2,1)S(1)}, u32[]{:S(2)}, u32[]{:S(2)}) async-start(bf16[16,2,88,128]{3,2,1,0:T(8,128)(2,1)} %broadcast_in_dim.42), calls=%async_computation.3 | async-start | bytes 1441792 | tf_op jit(solution)/shard_map/all_to_all | solution.py:28
  158.2 10.2 %collective-permute-start = (bf16[328,128]{1,0:T(8,128)(2,1)S(1)}, bf16[328,128]{1,0:T(8,128)(2,1)S(1)}, u32[]{:S(2)}, u32[]{:S(2)}) collective-permute-start(bf16[328,128]{1,0:T(8,128)(2,1)S(1)} %fusion.1.refs_0_.refs_1_), channel_id=1, source_target_pairs={{0,1},{1,2},{2,3},{3,0},{4,5},{5,6},{6,7},{7,4},{8,9},{9,10},{10,1... | collective-permute-start | bytes 251912 | tf_op jit(solution)/shard_map/ppermute | solution.py:24
  162.2 8.6 %collective-permute-start.1 = (bf16[328,128]{1,0:T(8,128)(2,1)S(1)}, bf16[328,128]{1,0:T(8,128)(2,1)S(1)}, u32[]{:S(2)}, u32[]{:S(2)}) collective-permute-start(bf16[328,128]{1,0:T(8,128)(2,1)S(1)} %fusion.1.refs_0_.refs_1_), channel_id=1, source_target_pairs={{0,2},{1,3},{2,0},{3,1},{4,6},{5,7},{6,4},{7,5},{8,10},{9,11},{10,... | collective-permute-start | bytes 251912 | tf_op jit(solution)/shard_map/ppermute | solution.py:24
  164.1 7.1 %collective-permute-start.2 = (bf16[328,128]{1,0:T(8,128)(2,1)S(1)}, bf16[328,128]{1,0:T(8,128)(2,1)S(1)}, u32[]{:S(2)}, u32[]{:S(2)}) collective-permute-start(bf16[328,128]{1,0:T(8,128)(2,1)S(1)} %fusion.1.refs_0_.refs_1_), channel_id=1, source_target_pairs={{0,3},{1,0},{2,1},{3,2},{4,7},{5,4},{6,5},{7,6},{8,11},{9,8},{10,9... | collective-permute-start | bytes 251912 | tf_op jit(solution)/shard_map/ppermute | solution.py:24
